TPU v7x, 16 devices: a 4x2x1 block of a 4x4x8 slice. The times are simulated.
16 devices in a mesh: dp: 2 (over y, z), tp: 8 (over x, core).
Axes of the slice: x: 4, y: 2, z: 1, core: 2. Of those that a mesh axis runs over, the one named last changes fastest.
The devices are a block of a 4x4x8 slice.
Arguments:
- y_one: float32 [16, 1024, 1024], P('dp', 'tp'), parts along dimension 0
- y_two: float32 [16, 1024, 1024], P('dp', 'tp'), parts along dimension 0
- dy_one: float32 [16, 1024, 1024], P('dp', 'tp'), parts along dimension 0
- dy_two: float32 [16, 1024, 1024], P('dp', 'tp'), parts along dimension 0
- w_qkv: bfloat16 [1, 1024, 8, 3, 128], P(None, None, 'tp')
- w_out: bfloat16 [1, 8, 128, 1024], P(None, 'tp')
- w_up: bfloat16 [1, 1024, 4096], P(None, None, 'tp')
- w_down: bfloat16 [1, 4096, 1024], P(None, 'tp')
Outputs:
- output 1: float32 [16, 1024, 1024], P('dp', 'tp'), parts along dimension 0
- output 2: float32 [16, 1024, 1024], P('dp', 'tp'), parts along dimension 0
- output 3: float32 [16, 1024, 1024], P('dp', 'tp'), parts along dimension 0
- output 4: float32 [16, 1024, 1024], P('dp', 'tp'), parts along dimension 0
- output 5: float32 [2, 1024, 8, 3, 128], P('dp', None, 'tp'), parts along dimension 0
- output 6: float32 [2, 8, 128, 1024], P('dp', 'tp'), parts along dimension 0
- output 7: float32 [2, 1024, 4096], P('dp', None, 'tp'), parts along dimension 0
- output 8: float32 [2, 4096, 1024], P('dp', 'tp'), parts along dimension 0
There are 2 independent parts. A program takes and returns all parts, laid end to end along the dimension named above; an argument that names none is the same for every part.
All inputs are finite; a program needn't handle non-finite values.
Results may differ from a plain program's by a relative error of at most 0.00836604.
Values are sent between devices in bfloat16 or wider.
A program may use at most 768 MiB of HBM per device.

v0:
```python
import jax
import jax.numpy as jnp
from jax import lax
from jax.sharding import PartitionSpec as P

RMS_EPS = 1e-6


def rms_norm(tensor):
    return tensor * lax.rsqrt(jnp.mean(tensor * tensor, axis=-1, keepdims=True) + RMS_EPS)


def rms_back(tensor, grad_in):
    inv_rms = lax.rsqrt(jnp.mean(tensor * tensor, axis=-1, keepdims=True) + RMS_EPS)
    return inv_rms * grad_in - tensor * (inv_rms * inv_rms * inv_rms) * jnp.mean(grad_in * tensor, axis=-1, keepdims=True)


def gelu_tanh(tensor):
    return jax.nn.gelu(tensor, approximate=True)


def gather_positions(tensor):
    return lax.all_gather(tensor, "tp", axis=1, tiled=True)


def scatter_positions(tensor):
    return lax.psum_scatter(tensor, "tp", scatter_dimension=1, tiled=True)


def local_backward(y_one, y_two, dy_one, dy_two, w_qkv, w_out, w_up, w_down):
    n_layers = w_qkv.shape[0]
    attn_scale = w_qkv.shape[4] ** -0.5
    grads_qkv, grads_out, grads_up, grads_down = [], [], [], []
    for layer_idx in reversed(range(n_layers)):
        wq_layer = w_qkv[layer_idx]
        wo_layer = w_out[layer_idx]
        wu_layer = w_up[layer_idx]
        wd_layer = w_down[layer_idx]
        u_mlp = gather_positions(rms_norm(y_one).astype(jnp.bfloat16))
        pre_act = jnp.einsum("bsh,hf->bsf", u_mlp, wu_layer, preferred_element_type=jnp.float32)
        hidden, gelu_pull = jax.vjp(gelu_tanh, pre_act)
        hidden_b = hidden.astype(jnp.bfloat16)
        g_part = jnp.einsum("bsf,fh->bsh", hidden_b, wd_layer, preferred_element_type=jnp.float32)
        x_two = y_two - scatter_positions(g_part)
        cot_mlp = gather_positions(dy_two.astype(jnp.bfloat16))
        grads_down.append(jnp.einsum("bsf,bsh->fh", hidden_b, cot_mlp, preferred_element_type=jnp.float32))
        d_hidden = jnp.einsum("bsh,fh->bsf", cot_mlp, wd_layer, preferred_element_type=jnp.float32)
        d_pre = gelu_pull(d_hidden)[0].astype(jnp.bfloat16)
        grads_up.append(jnp.einsum("bsh,bsf->hf", u_mlp, d_pre, preferred_element_type=jnp.float32))
        du_mlp = jnp.einsum("bsf,hf->bsh", d_pre, wu_layer, preferred_element_type=jnp.float32)
        dy_one = dy_one + rms_back(y_one, scatter_positions(du_mlp))
        u_att = gather_positions(rms_norm(x_two).astype(jnp.bfloat16))
        qkv_all = jnp.einsum("bsh,hnjd->jbnsd", u_att, wq_layer, preferred_element_type=jnp.float32).astype(jnp.bfloat16)
        q_heads, k_heads, v_heads = qkv_all[0], qkv_all[1], qkv_all[2]
        scores = jnp.einsum("bnqd,bnkd->bnqk", q_heads, k_heads, preferred_element_type=jnp.float32) * attn_scale
        attn_prob = jax.nn.softmax(scores, axis=-1)
        prob_b = attn_prob.astype(jnp.bfloat16)
        context = jnp.einsum("bnqk,bnkd->bnqd", prob_b, v_heads, preferred_element_type=jnp.float32).astype(jnp.bfloat16)
        f_part = jnp.einsum("bnqd,ndh->bqh", context, wo_layer, preferred_element_type=jnp.float32)
        x_one = y_one - scatter_positions(f_part)
        cot_att = gather_positions(dy_one.astype(jnp.bfloat16))
        grads_out.append(jnp.einsum("bnqd,bqh->ndh", context, cot_att, preferred_element_type=jnp.float32))
        d_context = jnp.einsum("bqh,ndh->bnqd", cot_att, wo_layer, preferred_element_type=jnp.float32).astype(jnp.bfloat16)
        d_prob = jnp.einsum("bnqd,bnkd->bnqk", d_context, v_heads, preferred_element_type=jnp.float32)
        d_value = jnp.einsum("bnqk,bnqd->bnkd", prob_b, d_context, preferred_element_type=jnp.float32)
        d_scores = (attn_prob * (d_prob - jnp.sum(d_prob * attn_prob, axis=-1, keepdims=True)) * attn_scale).astype(jnp.bfloat16)
        d_query = jnp.einsum("bnqk,bnkd->bnqd", d_scores, k_heads, preferred_element_type=jnp.float32)
        d_key = jnp.einsum("bnqk,bnqd->bnkd", d_scores, q_heads, preferred_element_type=jnp.float32)
        d_qkv = jnp.stack([d_query.astype(jnp.bfloat16), d_key.astype(jnp.bfloat16), d_value.astype(jnp.bfloat16)])
        grads_qkv.append(jnp.einsum("bsh,jbnsd->hnjd", u_att, d_qkv, preferred_element_type=jnp.float32))
        du_att = jnp.einsum("jbnsd,hnjd->bsh", d_qkv, wq_layer, preferred_element_type=jnp.float32)
        dx_two = dy_two + rms_back(x_two, scatter_positions(du_att))
        y_one, y_two, dy_two = x_one, x_two, dx_two
    return (y_one, y_two, dy_one, dy_two, jnp.stack(grads_qkv[::-1]), jnp.stack(grads_out[::-1]), jnp.stack(grads_up[::-1]), jnp.stack(grads_down[::-1]))


def solution(mesh):
    state_spec = P("dp", "tp", None)
    in_specs = (state_spec, state_spec, state_spec, state_spec, P(None, None, "tp", None, None), P(None, "tp", None, None), P(None, None, "tp"), P(None, "tp", None))
    out_specs = (state_spec, state_spec, state_spec, state_spec, P("dp", None, "tp", None, None), P("dp", "tp", None, None), P("dp", None, "tp"), P("dp", "tp", None))
    return jax.shard_map(local_backward, mesh=mesh, in_specs=in_specs, out_specs=out_specs, check_vma=False)
```

profile of v0, /device:TPU:112, one launch (start us, length us, event | category | flops | bytes accessed | tf_op | source)
XLA Modules:
  0.0 1217.4 jit_solution(11726834230652518920)
XLA Ops:
  7.3 2.7 multiply_reduce_fusion.5
  9.9 0.6 multiply_multiply_fusion.3
  10.6 0.6 copy-done.10
  11.1 3.8 multiply_convert_fusion.3
  15.1 84.0 %all-gather.5.cloned.1.call-done = bf16[8,1024,1024]{2,1,0:T(8,128)(2,1)} async-done(((bf16[8,128,1024]{2,1,0:T(8,128)(2,1)}), bf16[8,1024,1024]{2,1,0:T(8,128)(2,1)}) %all-gather.5.cloned.1.call-update) | async-done | bytes 16777232 | tf_op jit(solution)/shard_map/all_gather | solution.py:23
  99.1 15.7 %fusion.53 = f32[8,1024,512]{2,1,0:T(8,128)} fusion(bf16[8,1024,1024]{2,1,0:T(8,128)(2,1)} %all-gather.5.cloned.1.call-done, bf16[1,1024,512]{2,1,0:T(8,128)(2,1)S(1)} %copy-done.14), kind=kOutput, calls=%fused_computation.61 | convolution fusion | flops 8589934592 | bytes 34603008 | tf_op jit(solution)/shard_map/bsh,hf->bsf/dot_general | solution.py:40
  114.8 19.6 %fusion.49 = f32[8,1024,1024]{2,1,0:T(8,128)} fusion(bf16[1,512,1024]{2,1,0:T(8,128)(2,1)S(1)} %copy-done, f32[8,1024,512]{2,1,0:T(8,128)} %fusion.53), kind=kOutput, calls=%fused_computation.57 | convolution fusion | flops 8627683328 | bytes 51380224 | tf_op jit(solution)/shard_map/bsf,fh->bsh/dot_general | solution.py:43
  134.5 3.8 convert_element_type.69
  138.4 0.1 all-gather.7.cloned.1.call-start
  138.5 163.1 %reduce-scatter.5.cloned.1.call-done = f32[8,128,1024]{2,1,0:T(8,128)} async-done(((f32[8,1024,1024]{2,1,0:T(8,128)}), f32[8,128,1024]{2,1,0:T(8,128)}) %reduce-scatter.5.cloned.1.call-update) | async-done | bytes 4194320 | tf_op jit(solution)/shard_map/reduce_scatter | solution.py:27
  301.6 4.0 multiply_reduce_fusion.4
  305.6 0.6 multiply_multiply_fusion.2
  306.2 1.4 copy-done.2
  307.6 1.6 multiply_convert_fusion.2
  309.3 0.2 reduce-scatter.9.cloned.1.call-start
  309.5 75.0 %all-gather.9.cloned.1.call-done = bf16[8,1024,1024]{2,1,0:T(8,128)(2,1)} async-done(((bf16[8,128,1024]{2,1,0:T(8,128)(2,1)}), bf16[8,1024,1024]{2,1,0:T(8,128)(2,1)}) %all-gather.9.cloned.1.call-update) | async-done | bytes 16777232 | tf_op jit(solution)/shard_map/all_gather | solution.py:23
  384.5 25.1 %fusion.14 = bf16[8,1024,512]{2,1,0:T(8,128)(2,1)} fusion(f32[8,1024,512]{2,1,0:T(8,128)} %fusion.53, bf16[8,1024,1024]{2,1,0:T(8,128)(2,1)} %all-gather.9.cloned.1.call-done, bf16[1,512,1024]{2,1,0:T(8,128)(2,1)S(1)} %copy-done), kind=kOutput, calls=%fused_computation.16 | convolution fusion | flops 8673820672 | bytes 42991616 | tf_op jit(solution)/shard_map/bsh,fh->bsf/dot_general | solution.py:47
  409.6 18.8 %fusion.51 = f32[8,1024,1024]{2,1,0:T(8,128)} fusion(bf16[8,1024,512]{2,1,0:T(8,128)(2,1)} %fusion.14, bf16[1,1024,512]{2,1,0:T(8,128)(2,1)S(1)} %copy-done.14), kind=kOutput, calls=%fused_computation.59 | convolution fusion | flops 8589934592 | bytes 42991616 | tf_op jit(solution)/shard_map/bsf,hf->bsh/dot_general | solution.py:50
  428.5 0.3 reduce-scatter.7.cloned.1.call-start
  428.7 39.5 %all-gather.7.cloned.1.call-done = bf16[8,1024,1024]{2,1,0:T(8,128)(2,1)} async-done(((bf16[8,128,1024]{2,1,0:T(8,128)(2,1)}), bf16[8,1024,1024]{2,1,0:T(8,128)(2,1)}) %all-gather.7.cloned.1.call-update) | async-done | bytes 16777232 | tf_op jit(solution)/shard_map/all_gather | solution.py:23
  468.2 14.2 %convert_bitcast_fusion = bf16[3,8,1,1024,128]{4,3,0,1,2:T(8,128)(2,1)} fusion(bf16[8,1024,1024]{2,1,0:T(8,128)(2,1)} %all-gather.7.cloned.1.call-done, bf16[1,1024,1,3,128]{4,1,3,2,0:T(8,128)(2,1)S(1)} %copy-done.15), kind=kOutput, calls=%fused_computation.30 | convolution fusion | flops 6445596672 | bytes 23855104 | tf_op jit(solution)/shard_map/bsh,hnjd->jbnsd/dot_general | solution.py:53
  482.4 17.6 %fusion.84 = (f32[8,1024]{1,0:T(8,128)S(1)}, f32[8,1024,1024]{1,2,0:T(8,128)}) fusion(bf16[3,8,1,1024,128]{4,3,0,1,2:T(8,128)(2,1)} %convert_bitcast_fusion), kind=kOutput, calls=%fused_computation.82 | convolution fusion | flops 2172650496 | bytes 37781504 | tf_op jit(solution)/shard_map/sub | solution.py:56
  500.0 18.2 %fusion.38 = bf16[8,1024,128]{2,1,0:T(8,128)(2,1)S(1)} fusion(bf16[3,8,1,1024,128]{4,3,0,1,2:T(8,128)(2,1)} %convert_bitcast_fusion, f32[8,1024]{1,0:T(8,128)S(1)} %get-tuple-element.25), kind=kOutput, calls=%fused_computation.49 | convolution fusion | flops 4329579520 | bytes 8421376 | tf_op jit(solution)/shard_map/bnqk,bnkd->bnqd/dot_general | solution.py:58
  518.2 13.0 %fusion.58 = f32[8,1024,1024]{2,1,0:T(8,128)} fusion(bf16[8,1024,128]{2,1,0:T(8,128)(2,1)S(1)} %fusion.38, bf16[1,1,128,1024]{3,2,1,0:T(8,128)(2,1)S(1)} %copy-done.7), kind=kOutput, calls=%fused_computation.66 | convolution fusion | flops 2147483648 | bytes 35913728 | tf_op jit(solution)/shard_map/bnqd,ndh->bqh/dot_general | solution.py:59
  531.4 106.0 %reduce-scatter.9.cloned.1.call-done = f32[8,128,1024]{2,1,0:T(8,128)} async-done(((f32[8,1024,1024]{2,1,0:T(8,128)}), f32[8,128,1024]{2,1,0:T(8,128)}) %reduce-scatter.9.cloned.1.call-update) | async-done | bytes 4194320 | tf_op jit(solution)/shard_map/reduce_scatter | solution.py:27
  637.4 3.9 multiply_reduce_fusion.3
  641.3 164.4 %reduce-scatter.7.cloned.1.call-done = f32[8,128,1024]{2,1,0:T(8,128)} async-done(((f32[8,1024,1024]{2,1,0:T(8,128)}), f32[8,128,1024]{2,1,0:T(8,128)}) %reduce-scatter.7.cloned.1.call-update) | async-done | bytes 4194320 | tf_op jit(solution)/shard_map/reduce_scatter | solution.py:27
  805.7 10.6 fusion.83
  816.4 0.1 reduce-scatter.11.cloned.1.call-start
  816.5 18.6 %fusion.106 = bf16[8,1024,1024]{1,2,0:T(8,128)(2,1)} fusion(f32[8,1024]{1,0:T(8,128)S(1)} %get-tuple-element.25, bf16[3,8,1,1024,128]{4,3,0,1,2:T(8,128)(2,1)} %convert_bitcast_fusion), kind=kOutput, calls=%fused_computation.26.clone.clone.clone.1 | convolution fusion | flops 2181047296 | bytes 21004288 | tf_op jit(solution)/shard_map/sub | solution.py:56
  835.1 62.2 %all-gather.11.cloned.1.call-done = bf16[8,1024,1024]{2,1,0:T(8,128)(2,1)} async-done(((bf16[8,128,1024]{2,1,0:T(8,128)(2,1)}), bf16[8,1024,1024]{2,1,0:T(8,128)(2,1)}) %all-gather.11.cloned.1.call-update) | async-done | bytes 16777232 | tf_op jit(solution)/shard_map/all_gather | solution.py:23
  897.3 8.3 convolution_convert_fusion
  905.6 14.8 %fusion.43 = f32[8,1024,1024]{1,2,0:T(8,128)} fusion(bf16[8,1024,128]{2,1,0:T(8,128)(2,1)S(1)} %convolution_convert_fusion, bf16[3,8,1,1024,128]{4,3,0,1,2:T(8,128)(2,1)} %convert_bitcast_fusion), kind=kOutput, calls=%fused_computation.50 | convolution fusion | flops 2147483648 | bytes 37748736 | tf_op jit(solution)/shard_map/bnqd,bnkd->bnqk/dot_general | solution.py:64
  920.4 44.2 %convert_bitcast_fusion.3 = bf16[1,8,1,1024,128]{4,3,1,2,0:T(8,128)(2,1)} fusion(f32[8,1024,1024]{1,2,0:T(8,128)} %fusion.43, bf16[3,8,1,1024,128]{4,3,0,1,2:T(8,128)(2,1)} %convert_bitcast_fusion, f32[8,1024,1024]{1,2,0:T(8,128)} %get-tuple-element.26, f32[8,1024]{1,0:T(8,128)S(1)} %get-tuple-element.25), kind=kOutput, calls=%fused_computation.46 | convolution fusion | flops 2207261696 | bytes 138477568 | tf_op jit(solution)/shard_map/bnqk,bnkd->bnqd/dot_general | solution.py:67
  964.6 44.1 %convert_bitcast_fusion.2 = bf16[1,8,1,1024,128]{4,3,1,2,0:T(8,128)(2,1)} fusion(f32[8,1024,1024]{1,2,0:T(8,128)} %fusion.43, bf16[3,8,1,1024,128]{4,3,0,1,2:T(8,128)(2,1)} %convert_bitcast_fusion, f32[8,1024,1024]{1,2,0:T(8,128)} %get-tuple-element.26, f32[8,1024]{1,0:T(8,128)S(1)} %get-tuple-element.25), kind=kOutput, calls=%fused_computation.45 | convolution fusion | flops 2207261696 | bytes 138477568 | tf_op jit(solution)/shard_map/bnqk,bnqd->bnkd/dot_general | solution.py:68
  1008.7 8.5 convert_bitcast_fusion.1
  1017.2 1.4 copy-done.21
  1018.6 14.4 %convolution_bitcast_fusion = f32[8,1024,1024]{2,1,0:T(8,128)} fusion(bf16[1,8,1,1024,128]{4,3,1,2,0:T(8,128)(2,1)S(1)} %convert_bitcast_fusion.1, bf16[1,8,1,1024,128]{4,3,1,2,0:T(8,128)(2,1)S(1)} %copy-done.19, bf16[1,8,1,1024,128]{4,3,1,2,0:T(8,128)(2,1)S(1)} %copy-done.17, bf16[1,1024,1,3,128]{4,1,3,2,0:T(8,128)(2,1)S(1)} %copy-done.16), kind=kOutput, calls=%fused_computation.24 | convolution fusion | flops 6448742400 | bytes 40632320 | tf_op jit(solution)/shard_map/jbnsd,hnjd->bsh/dot_general | solution.py:71
  1033.0 15.8 %convolution_bitcast_fusion.2 = f32[1,1024,512]{2,1,0:T(8,128)} fusion(bf16[8,1024,1024]{2,1,0:T(8,128)(2,1)} %all-gather.5.cloned.1.call-done, bf16[8,1024,512]{2,1,0:T(8,128)(2,1)} %fusion.14), kind=kOutput, calls=%fused_computation.52 | convolution fusion | flops 8589934592 | bytes 27262976 | tf_op jit(solution)/shard_map/bsh,bsf->hf/dot_general | solution.py:49
  1048.8 19.2 %convolution_bitcast_fusion.1 = f32[1,512,1024]{2,1,0:T(8,128)} fusion(bf16[8,1024,1024]{2,1,0:T(8,128)(2,1)} %all-gather.9.cloned.1.call-done, f32[8,1024,512]{2,1,0:T(8,128)} %fusion.53), kind=kOutput, calls=%fused_computation.51 | convolution fusion | flops 8627683328 | bytes 35651584 | tf_op jit(solution)/shard_map/bsf,bsh->fh/dot_general | solution.py:46
  1068.0 11.2 fusion.45
  1079.3 4.8 copy.23
  1084.1 8.9 convolution_bitcast_fusion.3
  1093.0 107.1 %reduce-scatter.11.cloned.1.call-done = f32[8,128,1024]{2,1,0:T(8,128)} async-done(((f32[8,1024,1024]{2,1,0:T(8,128)}), f32[8,128,1024]{2,1,0:T(8,128)}) %reduce-scatter.11.cloned.1.call-update) | async-done | bytes 4194320 | tf_op jit(solution)/shard_map/reduce_scatter | solution.py:27
  1200.1 4.0 multiply_reduce_fusion.2
  1204.2 0.6 copy-done.3
  1204.8 1.3 copy-done.4
  1206.0 4.1 subtract_add_fusion
  (55 shorter events, 0.8 us)
Async XLA Ops:
  7.2 107.6 %copy-start = (bf16[1,512,1024]{2,1,0:T(8,128)(2,1)S(1)}, bf16[1,512,1024]{2,1,0:T(8,128)(2,1)}, u32[]{:S(2)}) copy-start(bf16[1,512,1024]{2,1,0:T(8,128)(2,1)} %param.15) | copy-start | bytes 3145732
  7.2 91.9 %copy-start.14 = (bf16[1,1024,512]{2,1,0:T(8,128)(2,1)S(1)}, bf16[1,1024,512]{2,1,0:T(8,128)(2,1)}, u32[]{:S(2)}) copy-start(bf16[1,1024,512]{2,1,0:T(8,128)(2,1)} %param.14) | copy-start | bytes 3145732
  7.2 91.9 %all-gather.5.cloned.1.call-start = ((), (), s32[]{:S(2)}) async-start(), calls=%async_computation.4 | async-start | bytes 18874368 | tf_op jit(solution)/shard_map/all_gather | solution.py:23
  10.5 0.6 copy-start.10
  15.0 286.6 %reduce-scatter.5.cloned.1.call-start = ((), (), s32[]{:S(2)}) async-start(), calls=%async_computation.5 | async-start | bytes 37748736 | tf_op jit(solution)/shard_map/reduce_scatter | solution.py:27
  134.5 250.1 %all-gather.9.cloned.1.call-start = ((), (), s32[]{:S(2)}) async-start(), calls=%async_computation.8 | async-start | bytes 18874368 | tf_op jit(solution)/shard_map/all_gather | solution.py:23
  138.4 329.8 %all-gather.7.cloned.1.call-start = ((), (), s32[]{:S(2)}) async-start(), calls=%async_computation.6 | async-start | bytes 18874368 | tf_op jit(solution)/shard_map/all_gather | solution.py:23
  305.6 2.0 copy-start.2
  306.2 1.4 copy-start.8
  309.3 328.1 %reduce-scatter.9.cloned.1.call-start = ((), (), s32[]{:S(2)}) async-start(), calls=%async_computation.9 | async-start | bytes 37748736 | tf_op jit(solution)/shard_map/reduce_scatter | solution.py:27
  428.4 39.8 %copy-start.15 = (bf16[1,1024,1,3,128]{4,1,3,2,0:T(8,128)(2,1)S(1)}, bf16[1,1024,1,3,128]{4,1,3,2,0:T(8,128)(2,1)}, u32[]{:S(2)}) copy-start(bf16[1,1024,1,3,128]{4,1,3,2,0:T(8,128)(2,1)} %param.12) | copy-start | bytes 2359300
  428.5 377.3 %reduce-scatter.7.cloned.1.call-start = ((), (), s32[]{:S(2)}) async-start(), calls=%async_computation.7 | async-start | bytes 37748736 | tf_op jit(solution)/shard_map/reduce_scatter | solution.py:27
  500.0 18.2 %copy-start.7 = (bf16[1,1,128,1024]{3,2,1,0:T(8,128)(2,1)S(1)}, bf16[1,1,128,1024]{3,2,1,0:T(8,128)(2,1)}, u32[]{:S(2)}) copy-start(bf16[1,1,128,1024]{3,2,1,0:T(8,128)(2,1)} %param.13) | copy-start | bytes 786436
  518.2 13.1 %copy-start.5 = (bf16[8,1024,128]{2,1,0:T(8,128)(2,1)}, bf16[8,1024,128]{2,1,0:T(8,128)(2,1)S(1)}, u32[]{:S(2)}) copy-start(bf16[8,1024,128]{2,1,0:T(8,128)(2,1)S(1)} %fusion.38) | copy-start | bytes 6291460
  531.3 274.4 %copy-start.11 = (f32[8,128]{1,0:T(8,128)S(1)}, f32[8,128]{1,0:T(8,128)}, u32[]{:S(2)}) copy-start(f32[8,128]{1,0:T(8,128)} %copy-done.10) | copy-start | bytes 12292
  531.4 274.4 %copy-start.13 = (f32[8,128]{1,0:T(8,128)S(1)}, f32[8,128]{1,0:T(8,128)}, u32[]{:S(2)}) copy-start(f32[8,128]{1,0:T(8,128)} %get-tuple-element.23) | copy-start | bytes 12292
  531.4 366.0 %all-gather.11.cloned.1.call-start = ((), (), s32[]{:S(2)}) async-start(), calls=%async_computation.10 | async-start | bytes 18874368 | tf_op jit(solution)/shard_map/all_gather | solution.py:23
  816.4 383.7 %reduce-scatter.11.cloned.1.call-start = ((), (), s32[]{:S(2)}) async-start(), calls=%async_computation.11 | async-start | bytes 37748736 | tf_op jit(solution)/shard_map/reduce_scatter | solution.py:27
  1008.7 9.9 copy-start.16
  1008.7 9.9 copy-start.17
  1008.7 9.9 copy-start.19
  1017.2 1.4 copy-start.21
  1048.8 19.2 %copy-start.18 = (bf16[1,8,1,1024,128]{4,3,1,2,0:T(8,128)(2,1)S(1)}, bf16[1,8,1,1024,128]{4,3,1,2,0:T(8,128)(2,1)}, u32[]{:S(2)}) copy-start(bf16[1,8,1,1024,128]{4,3,1,2,0:T(8,128)(2,1)} %convert_bitcast_fusion.3) | copy-start | bytes 6291460
  1048.8 19.2 %copy-start.20 = (bf16[1,8,1,1024,128]{4,3,1,2,0:T(8,128)(2,1)S(1)}, bf16[1,8,1,1024,128]{4,3,1,2,0:T(8,128)(2,1)}, u32[]{:S(2)}) copy-start(bf16[1,8,1,1024,128]{4,3,1,2,0:T(8,128)(2,1)} %convert_bitcast_fusion.2) | copy-start | bytes 6291460
  1048.8 19.2 %copy-start.22 = (bf16[1,8,1,1024,128]{4,3,1,2,0:T(8,128)(2,1)S(1)}, bf16[1,8,1,1024,128]{4,3,1,2,0:T(8,128)(2,1)}, u32[]{:S(2)}) copy-start(bf16[1,8,1,1024,128]{4,3,1,2,0:T(8,128)(2,1)} %copy-done.21) | copy-start | bytes 6291460
  1068.0 16.1 %copy-start.6 = (bf16[8,1024,128]{2,1,0:T(8,128)(2,1)S(1)}, bf16[8,1024,128]{2,1,0:T(8,128)(2,1)}, u32[]{:S(2)}) copy-start(bf16[8,1024,128]{2,1,0:T(8,128)(2,1)} %copy-done.5) | copy-start | bytes 6291460
  1093.0 111.2 %copy-start.9 = (f32[8,128]{1,0:T(8,128)S(1)}, f32[8,128]{1,0:T(8,128)}, u32[]{:S(2)}) copy-start(f32[8,128]{1,0:T(8,128)} %copy-done.8) | copy-start | bytes 12292
  1093.0 111.2 %copy-start.12 = (f32[8,128]{1,0:T(8,128)S(1)}, f32[8,128]{1,0:T(8,128)}, u32[]{:S(2)}) copy-start(f32[8,128]{1,0:T(8,128)} %get-tuple-element.21) | copy-start | bytes 12292
  1200.1 4.6 copy-start.3
  1200.1 5.9 copy-start.4
  1204.2 6.0 copy-start.1
Sparse Core Ops, SparseCore 0:
  15.1 83.9 all-gather.4
  134.6 166.9 reduce-scatter.4
  303.7 80.7 all-gather.8
  386.5 81.6 all-gather.6
  470.4 166.9 reduce-scatter.8
  639.6 166.0 reduce-scatter.6
  816.5 80.7 all-gather.10
  1033.1 166.9 reduce-scatter.10
where the time goes:
time: 1230 us; the launch traced here: 1220 us
  waiting for transfers between devices  802 us (65%)
  matrix products  350 us (28%)
  other arithmetic  39.8 us (3%)
  between operations  14.8 us (1%)
    reduce_scatter x4, waiting for transfers between devices, scatter_positions(): return lax.psum_scatter(tensor, 'tp', scatter_dimension=1, tiled=True)  541 us
    all_gather x4, waiting for transfers between devices, gather_positions(): return lax.all_gather(tensor, 'tp', axis=1, tiled=True)  261 us
    dot_general x1, matrix products, local_backward(): jnp.einsum('bnqk,bnkd->bnqd', d_scores, k_heads, preferred_element_type=j...  44.2 us
    dot_general x1, matrix products, local_backward(): jnp.einsum('bnqk,bnqd->bnkd', d_scores, q_heads, preferred_element_type=j...  44.1 us
    sub x2, matrix products, local_backward(): attn_prob = jax.nn.softmax(scores, axis=-1)  36.2 us
    dot_general x1, matrix products, local_backward(): jnp.einsum('bsh,fh->bsf', cot_mlp, wd_layer, preferred_element_type=jnp.f...  25.1 us
  transfers between devices with their start and end apart: 8, of which 8 were waited for; matrix products, arithmetic and copies ran while one was open for 16% of the time, Pallas kernels for 0%

commit v1 on v0

v1 whole, which is shorter than its diff:
```python
import jax
import jax.numpy as jnp
from jax import lax
from jax.sharding import PartitionSpec as P

RMS_EPS = 1e-6


def inv_rms(tensor):
    return lax.rsqrt(jnp.mean(tensor * tensor, axis=-1, keepdims=True) + RMS_EPS)


def rms_norm(tensor):
    return tensor * inv_rms(tensor)


def rms_back(tensor, grad_in):
    scale = inv_rms(tensor)
    return scale * grad_in - tensor * (scale * scale * scale) * jnp.mean(grad_in * tensor, axis=-1, keepdims=True)


def gelu_tanh(tensor):
    return jax.nn.gelu(tensor, approximate=True)


def to_sequences(tensor):
    return lax.all_to_all(tensor, "tp", split_axis=0, concat_axis=1, tiled=True)


def to_positions(tensor):
    return lax.all_to_all(tensor, "tp", split_axis=1, concat_axis=0, tiled=True)


def dot32(spec, left, right):
    return jnp.einsum(spec, left, right, preferred_element_type=jnp.float32)


def local_backward(y_one, y_two, dy_one, dy_two, w_qkv, w_out, w_up, w_down):
    bf16 = jnp.bfloat16
    attn_scale = w_qkv.shape[4] ** -0.5
    up_full = lax.all_gather(w_up[0], "tp", axis=1, tiled=True)
    down_full = lax.all_gather(w_down[0], "tp", axis=0, tiled=True)
    qkv_full = lax.all_gather(w_qkv[0], "tp", axis=1, tiled=True)
    out_full = lax.all_gather(w_out[0], "tp", axis=0, tiled=True)

    u_mlp = rms_norm(y_one).astype(bf16)
    hidden, gelu_pull = jax.vjp(gelu_tanh, dot32("bsh,hf->bsf", u_mlp, up_full))
    hidden_b = hidden.astype(bf16)
    x_two = y_two - dot32("bsf,fh->bsh", hidden_b, down_full)
    cot_mlp = dy_two.astype(bf16)
    d_pre = gelu_pull(dot32("bsh,fh->bsf", cot_mlp, down_full))[0].astype(bf16)
    dy_one = dy_one + rms_back(y_one, dot32("bsf,hf->bsh", d_pre, up_full))

    u_att = to_sequences(rms_norm(x_two).astype(bf16))
    cot_att = to_sequences(dy_one.astype(bf16))

    dw_down = lax.psum_scatter(dot32("bsf,bsh->fh", hidden_b, cot_mlp), "tp", scatter_dimension=0, tiled=True)
    dw_up = lax.psum_scatter(dot32("bsh,bsf->fh", u_mlp, d_pre), "tp", scatter_dimension=0, tiled=True).T

    qkv_all = dot32("bsh,hnjd->jbnsd", u_att, qkv_full).astype(bf16)
    q_heads, k_heads, v_heads = qkv_all[0], qkv_all[1], qkv_all[2]
    scores = dot32("bnqd,bnkd->bnqk", q_heads, k_heads) * attn_scale
    attn_prob = jax.nn.softmax(scores, axis=-1)
    prob_b = attn_prob.astype(bf16)
    context = dot32("bnqk,bnkd->bnqd", prob_b, v_heads).astype(bf16)
    context_pos = to_positions(jnp.swapaxes(context, 1, 2).reshape(u_att.shape))
    x_one = y_one - dot32("bsm,mh->bsh", context_pos, out_full.reshape(-1, out_full.shape[-1]))
    dw_out = lax.psum_scatter(dot32("bnqd,bqh->ndh", context, cot_att), "tp", scatter_dimension=0, tiled=True)
    d_context = dot32("bqh,ndh->bnqd", cot_att, out_full).astype(bf16)
    d_prob = dot32("bnqd,bnkd->bnqk", d_context, v_heads)
    d_value = dot32("bnqk,bnqd->bnkd", prob_b, d_context)
    d_scores = (attn_prob * (d_prob - jnp.sum(d_prob * attn_prob, axis=-1, keepdims=True)) * attn_scale).astype(bf16)
    d_query = dot32("bnqk,bnkd->bnqd", d_scores, k_heads)
    d_key = dot32("bnqk,bnqd->bnkd", d_scores, q_heads)
    d_qkv = jnp.stack([d_query.astype(bf16), d_key.astype(bf16), d_value.astype(bf16)])
    dw_qkv_rows = dot32("jbnsd,bsh->njdh", d_qkv, u_att)
    dw_qkv = lax.psum_scatter(dw_qkv_rows.reshape(-1, dw_qkv_rows.shape[-1]), "tp", scatter_dimension=0, tiled=True)
    dw_qkv = jnp.moveaxis(dw_qkv.reshape(-1, *dw_qkv_rows.shape[1:]), 3, 0)
    du_att = to_positions(dot32("jbnsd,hnjd->bsh", d_qkv, qkv_full))
    dx_two = dy_two + rms_back(x_two, du_att)
    return (x_one, x_two, dy_one, dx_two, dw_qkv[None], dw_out[None], dw_up[None], dw_down[None])


def solution(mesh):
    state_spec = P("dp", "tp", None)
    in_specs = (state_spec, state_spec, state_spec, state_spec, P(None, None, "tp", None, None), P(None, "tp", None, None), P(None, None, "tp"), P(None, "tp", None))
    out_specs = (state_spec, state_spec, state_spec, state_spec, P("dp", None, "tp", None, None), P("dp", "tp", None, None), P("dp", None, "tp"), P("dp", "tp", None))
    return jax.shard_map(local_backward, mesh=mesh, in_specs=in_specs, out_specs=out_specs, check_vma=False)
```

time: 1230 us -> 737 us (0.60)
  waiting for transfers between devices: 802 us -> 289 us
  local copies, waits for them, and re-layouts: 10 us -> 58 us
  matrix products: 350 us -> 323 us
  starting transfers between devices: 0.9 us -> 19.7 us
  other arithmetic: 39.8 us -> 24 us
    reduce_scatter x4, waiting for transfers between devices: 541 us -> 133 us  [the longest x1 89.5 us: local_backward(): lax.psum_scatter(dot32('bsf,bsh->fh', hidden_b, cot_mlp), 'tp', scatter_d...]
    all_gather x4, waiting for transfers between devices: 261 us -> 76.5 us  [the longest x1 45.1 us: local_backward(): up_full = lax.all_gather(w_up[0], 'tp', axis=1, tiled=True)]
    all_to_all x0 -> x4, waiting for transfers between devices: none -> 77 us  [the longest x2 76.9 us: to_positions(): return lax.all_to_all(tensor, 'tp', split_axis=1, concat_axis=0, tiled=True)]
    dot_general x17, matrix products: 314 us -> 287 us  [dot32(): return jnp.einsum(spec, left, right, preferred_element_type=jnp.float32)]
    all_to_all x0 -> x4, starting transfers between devices: none -> 19.2 us  [the longest x2 10.1 us: to_positions(): return lax.all_to_all(tensor, 'tp', split_axis=1, concat_axis=0, tiled=True)]
    unnamed x47 -> x44, local copies, waits for them, and re-layouts: 10 us -> 25.3 us
    convert_element_type x4 -> x2, other arithmetic: 19.9 us -> 5.08 us  [the longest x1 3.47 us: local_backward(): cot_att = to_sequences(dy_one.astype(bf16))]
    unnamed x0 -> x1, other arithmetic: none -> 12.8 us
  transfers between devices with their start and end apart: 8 -> 12, of which waited for: 8 -> 7; matrix products, arithmetic and copies ran while one was open for 16% -> 33% of each run, Pallas kernels for 0% -> 0%
where the time goes in v1:
time: 737 us; the launch traced here: 729 us
  matrix products  323 us (44%)
  waiting for transfers between devices  289 us (39%)
  local copies, waits for them, and re-layouts  58 us (8%)
  other arithmetic  24 us (3%)
  starting transfers between devices  19.7 us (3%)
  between operations  14.9 us (2%)
    dot_general x17, matrix products, dot32(): return jnp.einsum(spec, left, right, preferred_element_type=jnp.float32)  287 us
    reduce_scatter x1, waiting for transfers between devices, local_backward(): lax.psum_scatter(dot32('bsf,bsh->fh', hidden_b, cot_mlp), 'tp', scatter_d...  89.5 us
    all_to_all x2, waiting for transfers between devices, to_positions(): return lax.all_to_all(tensor, 'tp', split_axis=1, concat_axis=0, tiled=True)  76.9 us
    all_gather x1, waiting for transfers between devices, local_backward(): up_full = lax.all_gather(w_up[0], 'tp', axis=1, tiled=True)  45.1 us
    sub x2, matrix products, local_backward(): attn_prob = jax.nn.softmax(scores, axis=-1)  36.1 us
    reduce_scatter x1, waiting for transfers between devices, local_backward(): lax.psum_scatter(dot32('bnqd,bqh->ndh', context, cot_att), 'tp', scatter_...  33.7 us
    all_gather x1, waiting for transfers between devices, local_backward(): down_full = lax.all_gather(w_down[0], 'tp', axis=0, tiled=True)  31.4 us
    unnamed x44, local copies, waits for them, and re-layouts  25.3 us
  transfers between devices with their start and end apart: 12, of which 7 were waited for; matrix products, arithmetic and copies ran while one was open for 33% of the time, Pallas kernels for 0%

profile of v1, /device:TPU:112, one launch (start us, length us, event | category | flops | bytes accessed | tf_op | source)
XLA Modules:
  0.0 729.3 jit_solution(421029420600437548)
XLA Ops:
  10.2 2.5 multiply_reduce_fusion.5
  12.8 45.1 %all-gather.9.cloned.1.call-done = bf16[1,1024,4096]{2,1,0:T(8,128)(2,1)} async-done(((bf16[1,1024,512]{2,1,0:T(8,128)(2,1)}), bf16[1,1024,4096]{2,1,0:T(8,128)(2,1)}) %all-gather.9.cloned.1.call-update) | async-done | bytes 8388624 | tf_op jit(solution)/shard_map/all_gather | solution.py:41
  57.9 15.9 %fusion.22 = f32[8,128,4096]{2,1,0:T(8,128)} fusion(bf16[1,1024,4096]{2,1,0:T(8,128)(2,1)} %all-gather.9.cloned.1.call-done, f32[8,128,1024]{2,1,0:T(8,128)} %param.8, f32[8,128]{1,0:T(8,128)S(1)} %get-tuple-element.45), kind=kOutput, calls=%fused_computation.28 | convolution fusion | flops 8592031744 | bytes 29364224 | tf_op jit(solution)/shard_map/bsh,hf->bsf/dot_general | solution.py:35
  73.8 31.4 %all-gather.11.cloned.1.call-done = bf16[1,4096,1024]{2,1,0:T(8,128)(2,1)} async-done(((bf16[1,512,1024]{2,1,0:T(8,128)(2,1)}), bf16[1,4096,1024]{2,1,0:T(8,128)(2,1)}) %all-gather.11.cloned.1.call-update) | async-done | bytes 8388624 | tf_op jit(solution)/shard_map/all_gather | solution.py:42
  105.2 16.9 %multiply_reduce_fusion.4 = (f32[8,128]{1,0:T(8,128)S(1)}, f32[8,128,1024]{2,1,0:T(8,128)S(1)}) fusion(f32[8,128,1024]{2,1,0:T(8,128)} %param.9, bf16[1,4096,1024]{2,1,0:T(8,128)(2,1)} %all-gather.11.cloned.1.call-done, f32[8,128,4096]{2,1,0:T(8,128)} %fusion.22), kind=kOutput, calls=%fused_computation.46 | convolution fusion | flops 8630828032 | bytes 33558528 | tf_op jit(solution)/shard_map/bsf,fh->bsh/dot_general | solution.py:35
  122.8 1.4 copy-done
  124.2 1.6 multiply_convert_fusion.2
  125.8 4.3 all-to-all-start
  130.1 25.4 %fusion.14 = bf16[8,128,4096]{2,1,0:T(8,128)(2,1)} fusion(f32[8,128,4096]{2,1,0:T(8,128)} %fusion.22, bf16[1,4096,1024]{2,1,0:T(8,128)(2,1)} %all-gather.11.cloned.1.call-done, f32[8,128,1024]{2,1,0:T(8,128)} %param.11), kind=kOutput, calls=%fused_computation.16 | convolution fusion | flops 8674869248 | bytes 37748736 | tf_op jit(solution)/shard_map/bsh,fh->bsf/dot_general | solution.py:35
  155.5 14.6 %multiply_reduce_fusion.3 = (f32[8,128]{1,0:T(8,128)S(1)}, f32[8,128,1024]{2,1,0:T(8,128)S(1)}) fusion(f32[8,128,1024]{2,1,0:T(8,128)} %param.8, bf16[8,128,4096]{2,1,0:T(8,128)(2,1)} %fusion.14, bf16[1,1024,4096]{2,1,0:T(8,128)(2,1)} %all-gather.9.cloned.1.call-done), kind=kOutput, calls=%fused_computation.44 | convolution fusion | flops 8592030720 | bytes 25169920 | tf_op jit(solution)/shard_map/bsf,hf->bsh/dot_general | solution.py:35
  170.2 3.5 fusion.92
  173.6 1.3 copy-done.9
  174.9 4.7 all-to-all-start.2
  179.8 11.1 %convert_bitcast_fusion = bf16[3,1,8,1024,128]{4,3,0,2,1:T(8,128)(2,1)} fusion(bf16[1024,1024,1,1]{1,0,3,2:T(8,128)(2,1)} %bitcast.199, bf16[1,1024,8,3,128]{4,1,3,0,2:T(8,128)(2,1)} %all-gather.13.cloned.1.call-done), kind=kOutput, calls=%fused_computation.37 | convolution fusion | flops 6445596672 | bytes 14680064 | tf_op jit(solution)/shard_map/bsh,hnjd->jbnsd/dot_general | solution.py:35
  190.8 17.6 %fusion.93 = (f32[8,1024]{1,0:T(8,128)S(1)}, f32[8,1024,1024]{1,2,0:T(8,128)}) fusion(bf16[3,1,8,1024,128]{4,3,0,2,1:T(8,128)(2,1)} %convert_bitcast_fusion), kind=kOutput, calls=%fused_computation.84 | convolution fusion | flops 2172650496 | bytes 37781504 | tf_op jit(solution)/shard_map/sub | solution.py:63
  208.5 5.0 fusion.55
  213.5 15.5 %fusion.42 = f32[8,1024,1024]{1,2,0:T(8,128)} fusion(bf16[1024,8,128]{2,0,1:T(8,128)(2,1)S(1)} %fusion.55, bf16[3,1,8,1024,128]{4,3,0,2,1:T(8,128)(2,1)} %convert_bitcast_fusion), kind=kOutput, calls=%fused_computation.54 | convolution fusion | flops 2147483648 | bytes 37748736 | tf_op jit(solution)/shard_map/bnqd,bnkd->bnqk/dot_general | solution.py:35
  229.0 44.4 %convert_bitcast_fusion.3 = bf16[1,1,8,1024,128]{4,3,2,1,0:T(8,128)(2,1)} fusion(f32[8,1024,1024]{1,2,0:T(8,128)} %fusion.42, bf16[3,1,8,1024,128]{4,3,0,2,1:T(8,128)(2,1)} %convert_bitcast_fusion, f32[8,1024,1024]{1,2,0:T(8,128)} %get-tuple-element.49, f32[8,1024]{1,0:T(8,128)S(1)} %get-tuple-element.48), kind=kOutput, calls=%fused_computation.60 | convolution fusion | flops 2207261696 | bytes 138477568 | tf_op jit(solution)/shard_map/bnqk,bnkd->bnqd/dot_general | solution.py:35
  273.4 43.9 %convert_bitcast_fusion.2 = bf16[1,1,8,1024,128]{4,3,2,1,0:T(8,128)(2,1)} fusion(f32[8,1024,1024]{1,2,0:T(8,128)} %fusion.42, bf16[3,1,8,1024,128]{4,3,0,2,1:T(8,128)(2,1)} %convert_bitcast_fusion, f32[8,1024,1024]{1,2,0:T(8,128)} %get-tuple-element.49, f32[8,1024]{1,0:T(8,128)S(1)} %get-tuple-element.48), kind=kOutput, calls=%fused_computation.59 | convolution fusion | flops 2207261696 | bytes 138477568 | tf_op jit(solution)/shard_map/bnqk,bnqd->bnkd/dot_general | solution.py:35
  317.3 18.5 %fusion.114 = bf16[8,1024,1024]{1,2,0:T(8,128)(2,1)} fusion(f32[8,1024]{1,0:T(8,128)S(1)} %get-tuple-element.48, bf16[3,1,8,1024,128]{4,3,0,2,1:T(8,128)(2,1)} %convert_bitcast_fusion), kind=kOutput, calls=%fused_computation.31.clone.clone.clone.1 | convolution fusion | flops 2181047296 | bytes 21004288 | tf_op jit(solution)/shard_map/sub | solution.py:63
  335.8 8.5 %convert_bitcast_fusion.1 = bf16[1,1,8,1024,128]{4,3,2,1,0:T(8,128)(2,1)S(1)} fusion(bf16[1024,8,128]{2,0,1:T(8,128)(2,1)S(1)} %copy-done.5, bf16[8,1024,1024]{1,2,0:T(8,128)(2,1)} %fusion.114), kind=kOutput, calls=%fused_computation.58 | convolution fusion | flops 2148532224 | bytes 20971520 | tf_op jit(solution)/shard_map/bnqk,bnqd->bnkd/dot_general | solution.py:35
  344.3 1.3 copy-done.17
  345.6 11.3 %convolution_bitcast_fusion.2 = f32[8,3,128,1024]{3,2,0,1:T(8,128)} fusion(bf16[1024,1024,1,1]{1,0,3,2:T(8,128)(2,1)S(1)} %bitcast.200, bf16[1,1,8,1024,128]{4,3,2,1,0:T(8,128)(2,1)S(1)} %convert_bitcast_fusion.1, bf16[1,1,8,1024,128]{4,3,2,1,0:T(8,128)(2,1)} %convert_bitcast_fusion.2, bf16[1,1,8,1024,128]{4,3,2,1,0:T(8,128)(2,1)S(1)} %copy-done.18), kind=kOutput, calls=%fused_computation.40 | convolution fusion | flops 6461325312 | bytes 20971520 | tf_op jit(solution)/shard_map/jbnsd,bsh->njdh/dot_general | solution.py:35
  356.9 11.8 %copy.59 = f32[8,3,128,1024]{3,2,1,0:T(8,128)} copy(f32[8,3,128,1024]{3,2,0,1:T(8,128)} %convolution_bitcast_fusion.2) | data formatting | bytes 25165824 | tf_op jit(solution)/shard_map/jbnsd,bsh->njdh/transpose | solution.py:35
  369.4 16.7 %convolution_bitcast_fusion.1 = f32[4096,1024]{1,0:T(8,128)} fusion(bf16[8,128,4096]{2,1,0:T(8,128)(2,1)} %fusion.14, f32[8,128,1024]{2,1,0:T(8,128)} %param.8, f32[8,128]{1,0:T(8,128)S(1)} %copy-done.15), kind=kOutput, calls=%fused_computation.21 | convolution fusion | flops 8592031744 | bytes 29364224 | tf_op jit(solution)/shard_map/bsh,bsf->fh/dot_general | solution.py:35
  386.2 16.1 %fusion.58 = bf16[8,1024,128]{1,2,0:T(8,128)(2,1)S(1)} fusion(bf16[3,1,8,1024,128]{4,3,0,2,1:T(8,128)(2,1)} %convert_bitcast_fusion, f32[8,1024]{1,0:T(8,128)S(1)} %get-tuple-element.48), kind=kOutput, calls=%fused_computation.65 | convolution fusion | flops 4329579520 | bytes 8421376 | tf_op jit(solution)/shard_map/bnqk,bnkd->bnqd/dot_general | solution.py:35
  402.3 5.9 fusion.94
  408.4 19.8 %convolution_bitcast_fusion = f32[4096,1024]{1,0:T(8,128)} fusion(f32[8,128,1024]{2,1,0:T(8,128)} %param.11, f32[8,128,4096]{2,1,0:T(8,128)} %fusion.22), kind=kOutput, calls=%fused_computation.20 | convolution fusion | flops 8628731904 | bytes 37748736 | tf_op jit(solution)/shard_map/bsf,bsh->fh/dot_general | solution.py:35
  428.2 7.5 %copy.54 = bf16[1,1024,1024]{2,0,1:T(2,128)(2,1)} copy(bf16[1,1024,1024]{1,2,0:T(8,128)(2,1)S(1)} %bitcast.194) | data formatting | bytes 4194304 | tf_op jit(solution)/shard_map/reshape | solution.py:66
  436.3 12.8 %reduce.6 = bf16[1024,1024]{1,0:T(8,128)(2,1)S(1)} reduce(bf16[1024,1,1024]{2,1,0:T(2,128)(2,1)} %bitcast.192, bf16[]{:T(256)} %broadcast.151), dimensions={1}, to_apply=%bitcast.148.reduce_sub_computation | reduce | bytes 4194306
  449.1 3.8 reshape.191
  452.8 5.1 all-to-all-start.1
  458.0 12.0 %fusion.38 = f32[1,1024,1024]{2,1,0:T(8,128)} fusion(bf16[1,1,8,1024,128]{4,3,2,1,0:T(8,128)(2,1)} %copy-done.17, bf16[1,1,8,1024,128]{4,3,2,1,0:T(8,128)(2,1)} %convert_bitcast_fusion.2, bf16[1,1,8,1024,128]{4,3,2,1,0:T(8,128)(2,1)} %convert_bitcast_fusion.3, bf16[1,1024,8,3,128]{4,1,3,0,2:T(8,128)(2,1)} %all-gather.13.cloned.1.call-done), kind=kOutput, calls=%fused_computation.49 | convolution fusion | flops 6448742400 | bytes 16777216 | tf_op jit(solution)/shard_map/jbnsd,hnjd->bsh/dot_general | solution.py:35
  470.0 8.6 %copy.57 = f32[1,1024,1024]{2,0,1:T(1,128)} copy(f32[1,1024,1024]{2,1,0:T(8,128)} %fusion.38) | data formatting | bytes 8388608 | tf_op jit(solution)/shard_map/jbnsd,hnjd->bsh/dot_general | solution.py:35
  478.5 17.8 %all-to-all-done.1 = bf16[8,2,65536]{2,1,0:T(2,128)(2,1)S(1)} async-done(((bf16[8,2,65536]{2,1,0:T(2,128)(2,1)}), bf16[8,2,65536]{2,1,0:T(2,128)(2,1)S(1)}, u32[]{:S(2)}, u32[]{:S(2)}) %all-to-all-start.1) | async-done | bytes 2097184 | tf_op jit(solution)/shard_map/all_to_all | solution.py:31
  496.3 5.0 all-to-all-start.3
  501.4 4.3 reshape.192
  505.7 3.2 copy.72
  509.8 4.3 convolution_subtract_fusion
  514.2 59.2 %all-to-all-done.3 = f32[1,1024,1024]{2,0,1:T(1,128)} async-done(((f32[1,1024,1024]{2,0,1:T(1,128)}), f32[1,1024,1024]{2,0,1:T(1,128)}, u32[]{:S(2)}, u32[]{:S(2)}) %all-to-all-start.3) | async-done | bytes 4194336 | tf_op jit(solution)/shard_map/all_to_all | solution.py:31
  573.3 3.4 copy.73
  577.2 1.7 copy-done.7
  578.9 2.5 subtract_add_fusion
  581.4 4.8 copy.60
  586.2 9.6 %reduce-scatter.9.cloned.1.call-done = f32[512,1024]{1,0:T(8,128)} async-done(((f32[4096,1024]{1,0:T(8,128)}), f32[512,1024]{1,0:T(8,128)}) %reduce-scatter.9.cloned.1.call-update) | async-done | bytes 2097168 | tf_op jit(solution)/shard_map/reduce_scatter | solution.py:58
  595.8 2.9 copy.63
  598.7 33.7 %reduce-scatter.7.cloned.1.call-done = f32[1,128,1024]{2,1,0:T(8,128)} async-done(((f32[8,128,1024]{2,1,0:T(8,128)}), f32[1,128,1024]{2,1,0:T(8,128)}) %reduce-scatter.7.cloned.1.call-update) | async-done | bytes 524304 | tf_op jit(solution)/shard_map/reduce_scatter | solution.py:68
  632.4 89.5 %reduce-scatter.11.cloned.1.call-done = f32[512,1024]{1,0:T(8,128)} async-done(((f32[4096,1024]{1,0:T(8,128)}), f32[512,1024]{1,0:T(8,128)}) %reduce-scatter.11.cloned.1.call-update) | async-done | bytes 2097168 | tf_op jit(solution)/shard_map/reduce_scatter | solution.py:57
  (61 shorter events, 6.7 us)
Async XLA Ops:
  7.2 50.7 %all-gather.9.cloned.1.call-start = ((), (), s32[]{:S(2)}) async-start(), calls=%async_computation.12 | async-start | bytes 9437184 | tf_op jit(solution)/shard_map/all_gather | solution.py:41
  8.0 97.2 %all-gather.11.cloned.1.call-start = ((), (), s32[]{:S(2)}) async-start(), calls=%async_computation.13 | async-start | bytes 9437184 | tf_op jit(solution)/shard_map/all_gather | solution.py:42
  8.8 171.0 %all-gather.13.cloned.1.call-start = ((), (), s32[]{:S(2)}) async-start(), calls=%async_computation.14 | async-start | bytes 7077888 | tf_op jit(solution)/shard_map/all_gather | solution.py:43
  9.6 198.9 %all-gather.15.cloned.1.call-start = ((), (), s32[]{:S(2)}) async-start(), calls=%async_computation.15 | async-start | bytes 2359296 | tf_op jit(solution)/shard_map/all_gather | solution.py:44
  12.8 157.4 %copy-start.14 = (f32[8,128]{1,0:T(8,128)}, f32[8,128]{1,0:T(8,128)S(1)}, u32[]{:S(2)}) copy-start(f32[8,128]{1,0:T(8,128)S(1)} %get-tuple-element.45) | copy-start | bytes 12292
  122.1 2.0 copy-start
  122.8 1.4 copy-start.11
  125.8 47.9 %all-to-all-start = ((bf16[8,128,1024]{2,1,0:T(8,128)(2,1)}), bf16[8,128,1024]{2,1,0:T(8,128)(2,1)S(1)}, u32[]{:S(2)}, u32[]{:S(2)}) async-start(bf16[8,128,1024]{2,1,0:T(8,128)(2,1)} %multiply_convert_fusion.2), calls=%async_computation | async-start | bytes 4194304 | tf_op jit(solution)/shard_map/all_to_all | solution.py:27
  155.5 14.7 %copy-start.2 = (f32[8,128,1024]{2,1,0:T(8,128)S(1)}, f32[8,128,1024]{2,1,0:T(8,128)}, u32[]{:S(2)}) copy-start(f32[8,128,1024]{2,1,0:T(8,128)} %param.8) | copy-start | bytes 12582916
  155.5 14.7 %copy-start.6 = (f32[8,128,1024]{2,1,0:T(8,128)S(1)}, f32[8,128,1024]{2,1,0:T(8,128)}, u32[]{:S(2)}) copy-start(f32[8,128,1024]{2,1,0:T(8,128)} %param.10) | copy-start | bytes 12582916
  173.6 1.3 copy-start.9
  174.9 33.5 %all-to-all-start.2 = ((bf16[8,128,1024]{2,1,0:T(8,128)(2,1)}), bf16[8,128,1024]{2,1,0:T(8,128)(2,1)S(1)}, u32[]{:S(2)}, u32[]{:S(2)}) async-start(bf16[8,128,1024]{2,1,0:T(8,128)(2,1)} %get-tuple-element.40), calls=%async_computation.2 | async-start | bytes 4194304 | tf_op jit(solution)/shard_map/all_to_all | solution.py:27
  179.7 401.7 %reduce-scatter.5.cloned.1.call-start = ((), (), s32[]{:S(2)}) async-start(), calls=%async_computation.8 | async-start | bytes 14155776 | tf_op jit(solution)/shard_map/reduce_scatter | solution.py:77
  208.5 5.0 copy-start.8
  213.5 15.5 %copy-start.4 = (bf16[1024,8,128]{2,0,1:T(8,128)(2,1)}, bf16[1024,8,128]{2,0,1:T(8,128)(2,1)S(1)}, u32[]{:S(2)}) copy-start(bf16[1024,8,128]{2,0,1:T(8,128)(2,1)S(1)} %fusion.55) | copy-start | bytes 6291460
  317.3 18.5 %copy-start.5 = (bf16[1024,8,128]{2,0,1:T(8,128)(2,1)S(1)}, bf16[1024,8,128]{2,0,1:T(8,128)(2,1)}, u32[]{:S(2)}) copy-start(bf16[1024,8,128]{2,0,1:T(8,128)(2,1)} %copy-done.4) | copy-start | bytes 6291460
  335.8 9.8 %copy-start.10 = (bf16[8,128,1024]{2,1,0:T(8,128)(2,1)S(1)}, bf16[8,128,1024]{2,1,0:T(8,128)(2,1)}, u32[]{:S(2)}) copy-start(bf16[8,128,1024]{2,1,0:T(8,128)(2,1)} %copy-done.9) | copy-start | bytes 6291460
  335.8 9.8 %copy-start.18 = (bf16[1,1,8,1024,128]{4,3,2,1,0:T(8,128)(2,1)S(1)}, bf16[1,1,8,1024,128]{4,3,2,1,0:T(8,128)(2,1)}, u32[]{:S(2)}) copy-start(bf16[1,1,8,1024,128]{4,3,2,1,0:T(8,128)(2,1)} %convert_bitcast_fusion.3) | copy-start | bytes 6291460
  344.3 1.3 copy-start.17
  368.7 0.7 copy-start.15
  368.7 227.1 %reduce-scatter.9.cloned.1.call-start = ((), (), s32[]{:S(2)}) async-start(), calls=%async_computation.10 | async-start | bytes 18874368 | tf_op jit(solution)/shard_map/reduce_scatter | solution.py:58
  386.1 246.3 %reduce-scatter.7.cloned.1.call-start = ((), (), s32[]{:S(2)}) async-start(), calls=%async_computation.9 | async-start | bytes 4718592 | tf_op jit(solution)/shard_map/reduce_scatter | solution.py:68
  408.3 313.6 %reduce-scatter.11.cloned.1.call-start = ((), (), s32[]{:S(2)}) async-start(), calls=%async_computation.11 | async-start | bytes 18874368 | tf_op jit(solution)/shard_map/reduce_scatter | solution.py:57
  452.8 43.5 %all-to-all-start.1 = ((bf16[8,2,65536]{2,1,0:T(2,128)(2,1)}), bf16[8,2,65536]{2,1,0:T(2,128)(2,1)S(1)}, u32[]{:S(2)}, u32[]{:S(2)}) async-start(bf16[8,2,65536]{2,1,0:T(2,128)(2,1)} %reshape.191), calls=%async_computation.1 | async-start | bytes 4194304 | tf_op jit(solution)/shard_map/all_to_all | solution.py:31
  496.3 77.0 %all-to-all-start.3 = ((f32[1,1024,1024]{2,0,1:T(1,128)}), f32[1,1024,1024]{2,0,1:T(1,128)}, u32[]{:S(2)}, u32[]{:S(2)}) async-start(f32[1,1024,1024]{2,0,1:T(1,128)} %copy.57), calls=%async_computation.3 | async-start | bytes 8388608 | tf_op jit(solution)/shard_map/all_to_all | solution.py:31
  505.7 3.4 copy-start.3
  505.7 4.1 copy-start.16
  573.3 3.4 copy-start.1
  576.7 2.2 copy-start.7
  576.7 2.2 copy-start.12
  576.7 2.2 copy-start.13
Sparse Core Ops, SparseCore 0:
  9.6 48.2 all-gather.8
  59.5 45.6 all-gather.10
  106.8 47.6 all-gather.12
  156.0 21.1 all-gather.14
  368.9 70.0 reduce-scatter.4
  441.1 154.6 reduce-scatter.8
  598.7 33.7 reduce-scatter.6
  635.4 86.5 reduce-scatter.10

commit v2 on v1

v2 whole, which is shorter than its diff:
```python
import functools

import jax
import jax.numpy as jnp
from jax import lax
from jax.experimental import pallas as pl
from jax.experimental.pallas import tpu as pltpu
from jax.sharding import PartitionSpec as P

RMS_EPS = 1e-6
MESH = pl.DeviceIdType.MESH
BF16, F32 = jnp.bfloat16, jnp.float32
VMEM_LIMIT = 64 * 1024 * 1024 - 65536


def inv_rms(tensor):
    return lax.rsqrt(jnp.mean(tensor * tensor, axis=-1, keepdims=True) + RMS_EPS)


def rms_norm(tensor):
    return tensor * inv_rms(tensor)


def rms_back(tensor, grad_in):
    scale = inv_rms(tensor)
    return scale * grad_in - tensor * (scale * scale * scale) * jnp.mean(grad_in * tensor, axis=-1, keepdims=True)


def gelu_and_slope(tensor):
    root = (2.0 / jnp.pi) ** 0.5
    squared = tensor * tensor
    tanh = jnp.tanh(root * (tensor + 0.044715 * (tensor * squared)))
    cdf = 0.5 * (1.0 + tanh)
    slope = cdf + (0.5 * root) * tensor * ((1.0 - tanh * tanh) * (1.0 + (3 * 0.044715) * squared))
    return tensor * cdf, slope


def dot_nn(left, right):
    return lax.dot_general(left, right, (((1,), (0,)), ((), ())), preferred_element_type=F32)


def dot_nt(left, right):
    return lax.dot_general(left, right, (((1,), (1,)), ((), ())), preferred_element_type=F32)


def dot_tn(left, right):
    return lax.dot_general(left, right, (((0,), (0,)), ((), ())), preferred_element_type=F32)


class Ring:
    def __init__(self):
        me = lax.axis_index("tp")
        chip, core = me // 2, me % 2
        self.me, self.chip, self.core = me, chip, core
        self.chips = (chip, chip + 1 - 2 * (chip % 2), 3 - chip, (chip + 2) % 4)

    def at(self, slot):
        core = self.core if slot % 2 == 0 else 1 - self.core
        return self.chips[slot // 2] * 2 + core

    def at_traced(self, slot):
        relation, other = slot // 2, slot % 2
        own, near_t, near_f, opposite = self.chips
        chip = jnp.where(relation == 0, own, jnp.where(relation == 1, near_t, jnp.where(relation == 2, near_f, opposite)))
        return chip * 2 + (self.core + other) % 2

    def barrier(self):
        barrier = pltpu.get_barrier_semaphore()
        for slot in (1, 2, 3, 4, 5):
            pl.semaphore_signal(barrier, inc=1, device_id={"tp": self.at(slot)}, device_id_type=MESH)
        pl.semaphore_wait(barrier, 5)

    def copy(self, src, dst, send_sem, recv_sem, slot):
        return pltpu.make_async_remote_copy(src_ref=src, dst_ref=dst, send_sem=send_sem, recv_sem=recv_sem, device_id={"tp": self.at(slot)}, device_id_type=MESH)


PARTNER, SAME_T, OTHER_T, SAME_F, OTHER_F, SAME_O, OTHER_O = 1, 2, 3, 4, 5, 6, 7


def mlp_kernel(
    y_one, y_two, dy_one, dy_two, w_up, w_down, w_att,
    x_two, dx_one, uc_seq, att_full, part_own, part_near,
    u_all, c_all, up_all, down_all, acc, uc_own, relay, y_buf, x_buf,
    load_sem, y_sem, x_sem, w_send, w_recv, uc_send, uc_recv, att_send, att_recv, a2a_send, a2a_recv, relay_recv,
):
    ring = Ring()
    half = 512
    slab = 128

    def weight(which, src_slot, dst_slot, to, index):
        buf = (up_all, down_all)[which]
        return ring.copy(buf.at[src_slot], buf.at[dst_slot], w_send.at[index], w_recv.at[dst_slot, which], to)

    def weight_pair(src_slot, dst_slot, to, index):
        return [weight(which, src_slot, dst_slot, to, index + which) for which in (0, 1)]

    w_own = weight_pair(0, 1, PARTNER, 0) + weight_pair(0, 2, SAME_T, 2) + weight_pair(0, 4, SAME_F, 4)
    w_near_t = weight_pair(2, 6, SAME_F, 6) + weight_pair(2, 3, PARTNER, 8)
    w_near_f = weight_pair(4, 5, PARTNER, 10)
    w_far = weight_pair(6, 7, PARTNER, 12)

    def uc_pair(src_slot, dst_slot, to, index):
        return [ring.copy(buf.at[src_slot], buf.at[dst_slot], uc_send.at[index + which], uc_recv.at[dst_slot, which], to) for which, buf in enumerate((u_all, c_all))]

    uc_out = uc_pair(0, 2, SAME_T, 0) + uc_pair(0, 1, PARTNER, 2)
    uc_pass = uc_pair(2, 3, PARTNER, 4)

    def att(src, dst_slot, to, index):
        return ring.copy(src, att_full.at[dst_slot], att_send.at[index], att_recv.at[dst_slot], to)

    att_out = [att(w_att, 4, SAME_F, 0), att(w_att, 2, SAME_T, 1), att(w_att, 1, PARTNER, 2)]
    att_near_t = [att(att_full.at[2], 6, SAME_F, 3), att(att_full.at[2], 3, PARTNER, 4)]
    att_near_f = [att(att_full.at[4], 5, PARTNER, 5)]
    att_far = [att(att_full.at[6], 7, PARTNER, 6)]

    a2a_out = {slot: ring.copy(uc_own.at[slot], uc_seq.at[slot], a2a_send.at[slot], a2a_recv.at[slot], slot) for slot in (1, 2, 3, 4, 5)}
    a2a_out[SAME_O] = ring.copy(uc_own.at[SAME_O], relay.at[0], a2a_send.at[SAME_O], relay_recv.at[0], SAME_T)
    a2a_out[OTHER_O] = ring.copy(uc_own.at[OTHER_O], relay.at[1], a2a_send.at[OTHER_O], relay_recv.at[1], SAME_F)
    a2a_pass = [
        ring.copy(relay.at[0], uc_seq.at[SAME_O], a2a_send.at[8], a2a_recv.at[SAME_O], SAME_F),
        ring.copy(relay.at[1], uc_seq.at[OTHER_O], a2a_send.at[9], a2a_recv.at[OTHER_O], OTHER_T),
    ]
    uc_keep = pltpu.make_async_copy(uc_own.at[0], uc_seq.at[0], load_sem.at[4])

    def start(copies):
        for copy in copies:
            copy.start()

    loads = [
        pltpu.make_async_copy(w_up, up_all.at[0], load_sem.at[0]),
        pltpu.make_async_copy(w_down, down_all.at[0], load_sem.at[1]),
        pltpu.make_async_copy(y_one, acc.at[0], load_sem.at[2]),
        pltpu.make_async_copy(dy_two, acc.at[1], load_sem.at[3]),
    ]
    start(loads)
    ring.barrier()
    loads[0].wait()
    loads[1].wait()
    start(w_own)
    loads[2].wait()
    loads[3].wait()

    def normalize(step, carry):
        rows = pl.ds(pl.multiple_of(step * slab, slab), slab)
        u_all[0, rows, :] = rms_norm(acc[0, rows, :]).astype(BF16)
        c_all[0, rows, :] = acc[1, rows, :].astype(BF16)
        acc[0, rows, :] = jnp.zeros((slab, acc.shape[2]), F32)
        acc[1, rows, :] = jnp.zeros((slab, acc.shape[2]), F32)
        return carry

    lax.fori_loop(0, acc.shape[1] // slab, normalize, 0)
    start(uc_out)

    def y_loads(step, buf):
        seq = ring.at_traced(7 - step)
        rows = pl.ds(pl.multiple_of(seq * slab, slab), slab)
        return [pltpu.make_async_copy(src.at[rows], y_buf.at[buf, which], y_sem.at[buf, which]) for which, src in enumerate((y_one, y_two, dy_one))]

    def x_stores(step, buf):
        seq = ring.at_traced(7 - step)
        rows = pl.ds(pl.multiple_of(seq * slab, slab), slab)
        return [pltpu.make_async_copy(x_buf.at[buf, which], dst.at[rows], x_sem.at[buf, which]) for which, dst in enumerate((x_two, dx_one))]

    def feed_forward(step, carry):
        slot = jnp.where(step == 3, 4, jnp.where(step == 4, 3, step))

        @pl.when(step >= 1)
        def _():
            for which, buf in enumerate((up_all, down_all)):
                ring.copy(buf.at[slot], buf.at[slot], w_send.at[0], w_recv.at[slot, which], PARTNER).wait_recv()

        @pl.when(step == 2)
        def _():
            start(w_near_t)
            start(att_out)

        @pl.when(step == 3)
        def _():
            start(w_near_f)

        @pl.when(step == 6)
        def _():
            start(w_far)

        @pl.when(step == 7)
        def _():
            start(y_loads(0, 0))

        def rows_step(part, carry):
            rows = pl.ds(pl.multiple_of(part * half, half), half)
            hidden, slope = gelu_and_slope(dot_nt(u_all[0, rows, :], up_all[slot]))
            d_pre = (slope * dot_nt(c_all[0, rows, :], down_all[slot])).astype(BF16)
            acc[0, rows, :] += dot_nn(hidden.astype(BF16), down_all[slot])
            acc[1, rows, :] += dot_nn(d_pre, up_all[slot])
            return carry

        lax.fori_loop(0, acc.shape[1] // half, rows_step, 0)
        return carry

    lax.fori_loop(0, 8, feed_forward, 0)

    def finish(step, carry):
        slot = 7 - step
        buf = step % 2
        seq = ring.at_traced(slot)
        rows = pl.ds(pl.multiple_of(seq * slab, slab), slab)
        for copy in y_loads(step, buf):
            copy.wait()

        @pl.when(step < 7)
        def _():
            start(y_loads(step + 1, 1 - buf))

        @pl.when(step >= 2)
        def _():
            for copy in x_stores(step - 2, buf):
                copy.wait()

        y_first = y_buf[buf, 0]
        x_second = y_buf[buf, 1] - acc[0, rows, :]
        dy_first = y_buf[buf, 2] + rms_back(y_first, acc[1, rows, :])
        x_buf[buf, 0] = x_second
        x_buf[buf, 1] = dy_first
        uc_own[slot, 0] = rms_norm(x_second).astype(BF16)
        uc_own[slot, 1] = dy_first.astype(BF16)
        acc[0, rows, :] = jnp.zeros((slab, acc.shape[2]), F32)
        acc[1, rows, :] = jnp.zeros((slab, acc.shape[2]), F32)
        start(x_stores(step, buf))
        return carry

    lax.fori_loop(0, 8, finish, 0)
    for slot in (7, 6, 5, 4, 3, 2, 1):
        a2a_out[slot].start()
    uc_keep.start()
    for step in (6, 7):
        for copy in x_stores(step, step % 2):
            copy.wait()

    def gradients(step, carry):
        first = step // 8
        tokens = (step % 8) // 2
        slot = 4 - 4 * first

        @pl.when((step == 2) | (step == 4) | (step == 6))
        def _():
            for which, buf in enumerate((u_all, c_all)):
                ring.copy(buf.at[tokens], buf.at[tokens], uc_send.at[0], uc_recv.at[tokens, which], PARTNER).wait_recv()

        @pl.when(step == 4)
        def _():
            start(uc_pass)

        @pl.when(step == 5)
        def _():
            ring.copy(w_att, att_full.at[2], att_send.at[0], att_recv.at[2], PARTNER).wait_recv()
            start(att_near_t)
            ring.copy(w_att, att_full.at[4], att_send.at[0], att_recv.at[4], PARTNER).wait_recv()
            start(att_near_f)

        @pl.when(step == 10)
        def _():
            for index in (0, 1):
                ring.copy(relay.at[index], relay.at[index], a2a_send.at[0], relay_recv.at[index], PARTNER).wait_recv()
            start(a2a_pass)

        rows = pl.ds(pl.multiple_of((step % 2) * half, half), half)
        u_part, c_part = u_all[tokens, rows, :], c_all[tokens, rows, :]
        hidden, slope = gelu_and_slope(dot_nt(up_all[slot], u_part))
        d_pre = (slope * dot_nt(down_all[slot], c_part)).astype(BF16)
        acc[first, pl.ds(0, half), :] += dot_nn(d_pre, u_part)
        acc[first, pl.ds(half, half), :] += dot_nn(hidden.astype(BF16), c_part)
        return carry

    lax.fori_loop(0, 16, gradients, 0)
    out_near = pltpu.make_async_copy(acc.at[0], part_near, load_sem.at[0])
    out_own = pltpu.make_async_copy(acc.at[1], part_own, load_sem.at[1])
    out_near.start()
    out_own.start()

    ring.copy(w_att, att_full.at[6], att_send.at[0], att_recv.at[6], PARTNER).wait_recv()
    start(att_far)
    for slot in (1, 3, 5, 7):
        ring.copy(w_att, att_full.at[slot], att_send.at[0], att_recv.at[slot], PARTNER).wait_recv()
    for slot in range(1, 8):
        ring.copy(uc_own.at[slot], uc_seq.at[slot], a2a_send.at[0], a2a_recv.at[slot], PARTNER).wait_recv()
    for copy in w_own + w_near_t + w_near_f + w_far + uc_out + uc_pass + att_out + att_near_t + att_near_f + att_far + list(a2a_out.values()) + a2a_pass:
        copy.wait_send()
    uc_keep.wait()
    out_near.wait()
    out_own.wait()


def mlp_call(y_one, y_two, dy_one, dy_two, w_up, w_down, w_att):
    tokens, hidden = y_one.shape
    ffn = w_up.shape[0]
    any_spec = pl.BlockSpec(memory_space=pl.ANY)
    dma, vmem = pltpu.SemaphoreType.DMA, pltpu.VMEM
    out_shape = (
        jax.ShapeDtypeStruct((tokens, hidden), F32),
        jax.ShapeDtypeStruct((tokens, hidden), F32),
        jax.ShapeDtypeStruct((8, 2, tokens // 8, hidden), BF16),
        jax.ShapeDtypeStruct((8, *w_att.shape), BF16),
        jax.ShapeDtypeStruct((2 * ffn, hidden), F32),
        jax.ShapeDtypeStruct((2 * ffn, hidden), F32),
    )
    scratch = [
        vmem((4, tokens, hidden), BF16), vmem((4, tokens, hidden), BF16),
        vmem((8, ffn, hidden), BF16), vmem((8, ffn, hidden), BF16),
        vmem((2, tokens, hidden), F32),
        vmem((8, 2, tokens // 8, hidden), BF16), vmem((2, 2, tokens // 8, hidden), BF16),
        vmem((2, 3, tokens // 8, hidden), F32), vmem((2, 2, tokens // 8, hidden), F32),
        dma((5,)), dma((2, 3)), dma((2, 2)), dma((14,)), dma((8, 2)), dma((6,)), dma((4, 2)), dma((7,)), dma((8,)), dma((10,)), dma((8,)), dma((2,)),
    ]
    return pl.pallas_call(
        mlp_kernel,
        out_shape=out_shape,
        in_specs=[any_spec] * 7,
        out_specs=(any_spec,) * 6,
        scratch_shapes=scratch,
        compiler_params=pltpu.CompilerParams(collective_id=0, has_side_effects=True, vmem_limit_bytes=VMEM_LIMIT),
        cost_estimate=pl.CostEstimate(flops=70 * 10**9, bytes_accessed=64 * 2**20, transcendentals=0),
        name="feed_forward",
    )(y_one, y_two, dy_one, dy_two, w_up, w_down, w_att)


def attention_kernel(
    scale, uc_seq, w_att, att_full, part_near,
    near_recv, d_att, o_pos, du_pos, wo_full,
    uc_all, w_buf, qkv, d_ctx, d_qkv, o_all, du_all, part_send, part_keep, part_core, part_t, part_f, o_relay, du_relay,
    load_sem, w_sem, wo_sem, near_sem, core_send, core_recv, t_send, t_recv, f_sem, o_send, o_recv, du_send, du_recv, o_relay_recv, du_relay_recv,
):
    ring = Ring()
    slab, hidden = uc_seq.shape[2], uc_seq.shape[3]
    seq_len = 8 * slab
    dim = w_att.shape[0] // 4
    tile = 256

    def head_slot(step):
        pair = step // 2
        relation = jnp.where(pair == 0, 1, jnp.where(pair == 1, 3, jnp.where(pair == 2, 2, 0)))
        return relation * 2 + 1 - step % 2

    def w_load(step, buf):
        return pltpu.make_async_copy(att_full.at[head_slot(step)], w_buf.at[buf], w_sem.at[buf])

    w_load_own = pltpu.make_async_copy(w_att, w_buf.at[1], w_sem.at[1])
    near = ring.copy(part_near, near_recv, near_sem.at[0], near_sem.at[1], SAME_F)

    def core_copy(step, buf):
        relation = head_slot(step) // 2
        return ring.copy(part_send.at[buf], part_core.at[relation], core_send.at[buf], core_recv.at[relation], PARTNER)

    t_copies = [
        ring.copy(part_keep.at[1], part_t.at[0], t_send.at[0], t_recv.at[0], SAME_T),
        ring.copy(part_keep.at[3], part_t.at[1], t_send.at[1], t_recv.at[1], SAME_T),
    ]
    f_copy = ring.copy(part_keep.at[2], part_f, f_sem.at[0], f_sem.at[1], SAME_F)

    def rows_of(slot):
        return pl.ds(slot * slab, slab)

    def to_positions(src, dst, relay, send_sem, recv_sem, relay_sem):
        near_t, near_f = ring.at(SAME_T), ring.at(SAME_F)
        out = [
            ring.copy(src.at[rows_of(SAME_O)], relay.at[0], send_sem.at[6], relay_sem.at[0], SAME_T),
            ring.copy(src.at[rows_of(OTHER_O)], relay.at[1], send_sem.at[7], relay_sem.at[1], SAME_F),
        ] + [ring.copy(src.at[rows_of(slot)], dst.at[ring.me], send_sem.at[slot], recv_sem.at[slot], slot) for slot in (5, 4, 3, 2, 1)]
        onward = [
            ring.copy(relay.at[0], dst.at[near_t], send_sem.at[8], recv_sem.at[SAME_O], SAME_F),
            ring.copy(relay.at[1], dst.at[near_f], send_sem.at[9], recv_sem.at[OTHER_O], OTHER_T),
        ]
        keep = pltpu.make_async_copy(src.at[rows_of(0)], dst.at[ring.me], send_sem.at[0])
        return out, onward, keep

    o_out, o_pass, o_keep = to_positions(o_all, o_pos, o_relay, o_send, o_recv, o_relay_recv)
    du_out, du_pass, du_keep = to_positions(du_all, du_pos, du_relay, du_send, du_recv, du_relay_recv)

    def start(copies):
        for copy in copies:
            copy.start()

    loads = [pltpu.make_async_copy(uc_seq.at[slot, which], uc_all.at[which, rows_of(slot)], load_sem.at[slot, which]) for slot in range(8) for which in (0, 1)]
    start(loads)
    w_load(0, 0).start()
    ring.barrier()
    near.start()
    du_all[...] = jnp.zeros_like(du_all)
    for copy in loads:
        copy.wait()

    def head_step(step, carry):
        buf = step % 2
        slot = head_slot(step)
        relation = slot // 2
        w_load(step, buf).wait()

        @pl.when(step < 6)
        def _():
            w_load(step + 1, 1 - buf).start()

        @pl.when(step == 6)
        def _():
            w_load_own.start()

        head = ring.at_traced(slot)
        columns = pl.ds(pl.multiple_of(head * dim, dim), dim)
        wo_copy = pltpu.make_async_copy(w_buf.at[buf, pl.ds(3 * dim, dim)], wo_full.at[head], wo_sem.at[0])
        wo_copy.start()
        qkv[...] = dot_nt(uc_all[0], w_buf[buf, pl.ds(0, 3 * dim), :]).astype(BF16)
        d_ctx[...] = dot_nt(uc_all[1], w_buf[buf, pl.ds(3 * dim, dim), :]).astype(BF16)

        def query_tile(part, carry):
            d_key, d_value = carry
            rows = pl.ds(pl.multiple_of(part * tile, tile), tile)
            query, key, value = qkv[rows, pl.ds(0, dim)], qkv[:, pl.ds(dim, dim)], qkv[:, pl.ds(2 * dim, dim)]
            scores = dot_nt(query, key) * scale
            grown = jnp.exp(scores - jnp.max(scores, axis=-1, keepdims=True))
            prob = grown / jnp.sum(grown, axis=-1, keepdims=True)
            prob_b = prob.astype(BF16)
            o_all[rows, columns] = dot_nn(prob_b, value).astype(BF16)
            d_out = d_ctx[rows, :]
            d_prob = dot_nt(d_out, value)
            d_score = (prob * (d_prob - jnp.sum(d_prob * prob, axis=-1, keepdims=True)) * scale).astype(BF16)
            d_qkv[rows, pl.ds(0, dim)] = dot_nn(d_score, key).astype(BF16)
            return d_key + dot_tn(d_score, query), d_value + dot_tn(prob_b, d_out)

        zeros = jnp.zeros((seq_len, dim), F32)
        d_key, d_value = lax.fori_loop(0, seq_len // tile, query_tile, (zeros, zeros))
        d_qkv[:, pl.ds(dim, dim)] = d_key.astype(BF16)
        d_qkv[:, pl.ds(2 * dim, dim)] = d_value.astype(BF16)

        def du_tile(part, carry):
            rows = pl.ds(pl.multiple_of(part * tile, tile), tile)
            du_all[rows, :] += dot_nn(d_qkv[rows, :], w_buf[buf, pl.ds(0, 3 * dim), :])
            return carry

        lax.fori_loop(0, seq_len // tile, du_tile, 0)

        def write_part(dst, index):
            dst[index, pl.ds(0, 3 * dim), :] = dot_tn(d_qkv[...], uc_all[0])
            dst[index, pl.ds(3 * dim, dim), :] = dot_tn(o_all[:, columns], uc_all[1])

        @pl.when(step % 2 == 0)
        def _():
            send = (step // 2) % 2

            @pl.when(step >= 4)
            def _():
                core_copy(step - 4, send).wait_send()

            write_part(part_send, send)
            core_copy(step, send).start()

        @pl.when(step % 2 == 1)
        def _():
            write_part(part_keep, relation)
            core_copy(step - 1, 0).wait_recv()
            part_keep[relation] += part_core[relation]

        @pl.when(step == 1)
        def _():
            t_copies[0].start()

        @pl.when(step == 3)
        def _():
            t_copies[1].start()

        @pl.when(step == 5)
        def _():
            t_copies[1].wait_recv()
            part_keep[2] += part_t[1]
            f_copy.start()

        wo_copy.wait()
        return carry

    lax.fori_loop(0, 8, head_step, 0)
    start(o_out)
    start(du_out)
    o_keep.start()
    du_keep.start()
    for copy in o_out[:2]:
        copy.wait_recv()
    start(o_pass)
    t_copies[0].wait_recv()
    part_keep[0] += part_t[0]
    f_copy.wait_recv()
    part_keep[0] += part_f[...]
    d_att_copy = pltpu.make_async_copy(part_keep.at[0], d_att, load_sem.at[0, 0])
    d_att_copy.start()
    for copy in du_out[:2]:
        copy.wait_recv()
    start(du_pass)

    for dst, recv_sem in ((o_pos, o_recv), (du_pos, du_recv)):
        for slot in range(1, 8):
            ring.copy(dst.at[0], dst.at[ring.at(slot)], near_sem.at[0], recv_sem.at[slot], PARTNER).wait_recv()
    for copy in o_out + du_out + o_pass + du_pass + t_copies + [f_copy, near, core_copy(4, 0), core_copy(6, 1)]:
        copy.wait_send()
    near.wait_recv()
    o_keep.wait()
    du_keep.wait()
    d_att_copy.wait()


def attention_call(uc_seq, w_att, att_full, part_near):
    slab, hidden = uc_seq.shape[2:]
    rows = w_att.shape[0]
    dim = rows // 4
    seq_len = 8 * slab
    any_spec = pl.BlockSpec(memory_space=pl.ANY)
    dma, vmem = pltpu.SemaphoreType.DMA, pltpu.VMEM
    out_shape = (
        jax.ShapeDtypeStruct(part_near.shape, F32),
        jax.ShapeDtypeStruct(w_att.shape, F32),
        jax.ShapeDtypeStruct((8, slab, hidden), BF16),
        jax.ShapeDtypeStruct((8, slab, hidden), F32),
        jax.ShapeDtypeStruct((8, dim, hidden), BF16),
    )
    scratch = [
        vmem((2, seq_len, hidden), BF16), vmem((2, rows, hidden), BF16), vmem((seq_len, 3 * dim), BF16), vmem((seq_len, dim), BF16), vmem((seq_len, 3 * dim), BF16),
        vmem((seq_len, hidden), BF16), vmem((seq_len, hidden), F32),
        vmem((2, rows, hidden), F32), vmem((4, rows, hidden), F32), vmem((4, rows, hidden), F32), vmem((2, rows, hidden), F32), vmem((rows, hidden), F32),
        vmem((2, slab, hidden), BF16), vmem((2, slab, hidden), F32),
        dma((8, 2)), dma((2,)), dma((1,)), dma((2,)), dma((2,)), dma((4,)), dma((2,)), dma((2,)), dma((2,)), dma((10,)), dma((8,)), dma((10,)), dma((8,)), dma((2,)), dma((2,)),
    ]
    return pl.pallas_call(
        functools.partial(attention_kernel, dim ** -0.5),
        out_shape=out_shape,
        in_specs=[any_spec] * 4,
        out_specs=(any_spec,) * 5,
        scratch_shapes=scratch,
        compiler_params=pltpu.CompilerParams(collective_id=1, has_side_effects=True, vmem_limit_bytes=VMEM_LIMIT),
        cost_estimate=pl.CostEstimate(flops=40 * 10**9, bytes_accessed=64 * 2**20, transcendentals=0),
        name="attention",
    )(uc_seq, w_att, att_full, part_near)


def local_backward(y_one, y_two, dy_one, dy_two, w_qkv, w_out, w_up, w_down):
    shape = y_one.shape
    hidden = shape[2]
    _, _, _, parts, dim = w_qkv.shape
    flat = [tensor.reshape(-1, hidden) for tensor in (y_one, y_two, dy_one, dy_two)]
    w_att = jnp.concatenate([w_qkv.reshape(hidden, parts * dim).T, w_out.reshape(dim, hidden)])
    x_two, dx_one, uc_seq, att_full, part_own, part_near = mlp_call(*flat, w_up[0].T, w_down[0], w_att)
    near_recv, d_att, o_pos, du_pos, wo_full = attention_call(uc_seq, w_att, att_full, part_near)
    grads = part_own + near_recv
    ffn = w_down.shape[1]
    x_one = y_one - jnp.einsum("bsm,mh->bsh", o_pos, wo_full.reshape(-1, hidden), preferred_element_type=F32)
    x_two = x_two.reshape(shape)
    dx_two = dy_two + rms_back(x_two, du_pos)
    dw_qkv = d_att[: parts * dim].T.reshape(1, hidden, 1, parts, dim)
    dw_out = d_att[parts * dim :].reshape(1, 1, dim, hidden)
    return (x_one, x_two, dx_one.reshape(shape), dx_two, dw_qkv, dw_out, grads[:ffn].T[None], grads[ffn:][None])


def solution(mesh):
    state_spec = P("dp", "tp", None)
    in_specs = (state_spec, state_spec, state_spec, state_spec, P(None, None, "tp", None, None), P(None, "tp", None, None), P(None, None, "tp"), P(None, "tp", None))
    out_specs = (state_spec, state_spec, state_spec, state_spec, P("dp", None, "tp", None, None), P("dp", "tp", None, None), P("dp", None, "tp"), P("dp", "tp", None))
    return jax.shard_map(local_backward, mesh=mesh, in_specs=in_specs, out_specs=out_specs, check_vma=False)
```

time: 737 us -> 483 us (0.66); the launches traced: 729 us -> 483 us
  Pallas kernels: 0 us -> 442 us
  matrix products: 323 us -> 4.37 us
  waiting for transfers between devices: 289 us -> 0 us
  local copies, waits for them, and re-layouts: 58 us -> 25.7 us
  starting transfers between devices: 19.7 us -> 0 us
  between operations: 14.9 us -> 0.74 us
  other arithmetic: 24 us -> 9.89 us
    pallas_call x0 -> x2, Pallas kernels: none -> 442 us  [the longest x1 235 us: attention_call(): pl.pallas_call(functools.partial(attention_kernel, dim ** (-0.5)), out_sh...]
    dot_general x17 -> x1, matrix products: 287 us -> 4.37 us  [local_backward(): jnp.einsum('bsm,mh->bsh', o_pos, wo_full.reshape(-1, hidden), preferred_e...]
    reduce_scatter x4 -> x0, waiting for transfers between devices: 133 us -> none  [the longest x1 89.5 us: local_backward(): lax.psum_scatter(dot32('bsf,bsh->fh', hidden_b, cot_mlp), 'tp', scatter_d...]
    all_to_all x4 -> x0, waiting for transfers between devices: 77 us -> none  [the longest x2 76.9 us: to_positions(): return lax.all_to_all(tensor, 'tp', split_axis=1, concat_axis=0, tiled=True)]
    all_gather x4 -> x0, waiting for transfers between devices: 76.5 us -> none  [the longest x1 45.1 us: local_backward(): up_full = lax.all_gather(w_up[0], 'tp', axis=1, tiled=True)]
    sub x2 -> x0, matrix products: 36.1 us -> none  [local_backward(): attn_prob = jax.nn.softmax(scores, axis=-1)]
    all_to_all x4 -> x0, starting transfers between devices: 19.2 us -> none  [the longest x2 10.1 us: to_positions(): return lax.all_to_all(tensor, 'tp', split_axis=1, concat_axis=0, tiled=True)]
    unnamed x1 -> x0, other arithmetic: 12.8 us -> none
  transfers between devices with their start and end apart: 12 -> 0, of which waited for: 7 -> 0; matrix products, arithmetic and copies ran while one was open for 33% -> 0% of each run, Pallas kernels for 0% -> 0%
where the time goes in v2:
time: 483 us
  Pallas kernels  442 us (92%)
  local copies, waits for them, and re-layouts  25.7 us (5%)
  other arithmetic  9.89 us (2%)
    pallas_call x1, Pallas kernels, attention_call(): pl.pallas_call(functools.partial(attention_kernel, dim ** (-0.5)), out_sh...  235 us
    pallas_call x1, Pallas kernels, mlp_call(): pl.pallas_call(mlp_kernel, out_shape=out_shape, in_specs=[any_spec] * 7,...  208 us
    unnamed x24, local copies, waits for them, and re-layouts  21.8 us

profile of v2, /device:TPU:112, one launch (start us, length us, event | category | flops | bytes accessed | tf_op | source)
XLA Modules:
  0.0 482.9 jit_solution(8623316256616427215)
XLA Ops:
  0.6 0.0 copy-start.5
  0.6 1.5 copy.17
  2.1 2.0 pad_maximum_fusion.w_att
  4.1 0.0 copy-done.5
  4.1 1.3 copy.16
  5.4 207.5 %feed_forward.1 = (f32[1024,1024]{1,0:T(8,128)}, f32[1024,1024]{1,0:T(8,128)}, bf16[8,2,128,1024]{3,2,1,0:T(8,128)(2,1)}, bf16[8,512,1024]{2,1,0:T(8,128)(2,1)},...) custom-call(f32[1024,1024]{1,0:T(8,128)} %bitcast.45, f32[1024,1024]{1,0:T(8,128)} %bitcast.43, f32[1024,1024]{1,0:T(8,128)} %bitcast.44, ...), custom_call_target="tpu_custom_call" | custom-call | flops 70000001024 | bytes 67108864 | tf_op jit(solution)/shard_map/feed_forward/pallas_call | solution.py:314
  213.0 234.8 %attention.1 = (f32[1024,1024]{1,0:T(8,128)}, f32[512,1024]{1,0:T(8,128)}, bf16[8,128,1024]{2,1,0:T(8,128)(2,1)}, f32[8,128,1024]{2,1,0:T(8,128)}, bf16[8,128,1024]{2,1,0:T(8,128)(2,1)}) custom-call(bf16[8,2,128,1024]{3,2,1,0:T(8,128)(2,1)} %get-tuple-element.19.uc_seq, bf16[512,1024]{1,0:T(8,128)(2,1)} %pad_maximum_fusion.w_att, ...), custom_call_target="tpu_custom_call" | custom-call | flops 40000000000 | bytes 67108864 | tf_op jit(solution)/shard_map/attention/pallas_call | solution.py:527
  447.7 0.0 copy-start.6
  447.8 0.0 copy-start.7
  447.8 0.0 copy-start.8
  447.8 4.6 add.24
  452.4 0.0 copy-done.6
  452.4 0.7 copy-done.7
  453.1 0.6 copy-done.8
  453.7 4.4 convolution_subtract_fusion
  458.1 0.0 copy-start
  458.1 1.7 slice_bitcast_fusion
  459.8 0.0 copy-start.1
  459.8 1.2 copy-done
  461.0 0.3 multiply_reduce_fusion.1
  461.4 1.2 copy-done.1
  462.5 0.0 copy-start.3
  462.5 0.4 multiply_reduce_fusion
  463.0 1.7 copy-done.3
  464.7 0.0 copy-start.4
  464.7 2.5 subtract_add_fusion
  467.2 0.0 copy-done.4
  467.2 0.8 slice_bitcast_fusion.2
  468.0 1.3 slice.12
  469.4 4.8 copy.18
  474.2 1.8 copy.19
  476.0 0.0 copy-start.2
  476.0 4.9 %copy.22 = f32[8,128,1024]{2,1,0:T(8,128)} copy(f32[8,128,1024]{2,1,0:T(8,128)} %bitcast.35) | data formatting | bytes 8388608
  480.9 0.0 copy-done.2
  480.9 2.0 copy.23
  (2 shorter events, 0.0 us)
Async XLA Ops:
  0.6 3.5 copy-start.5
  447.7 4.6 copy-start.6
  447.8 5.3 %copy-start.7 = (bf16[8,128,1024]{2,1,0:T(8,128)(2,1)S(1)}, bf16[8,128,1024]{2,1,0:T(8,128)(2,1)}, u32[]{:S(2)}) copy-start(bf16[8,128,1024]{2,1,0:T(8,128)(2,1)} %get-tuple-element.23) | copy-start | bytes 6291460
  447.8 5.9 %copy-start.8 = (bf16[8,128,1024]{2,1,0:T(8,128)(2,1)S(1)}, bf16[8,128,1024]{2,1,0:T(8,128)(2,1)}, u32[]{:S(2)}) copy-start(bf16[8,128,1024]{2,1,0:T(8,128)(2,1)} %get-tuple-element.22) | copy-start | bytes 6291460
  458.1 2.9 copy-start
  459.8 2.7 copy-start.1
  462.5 2.2 copy-start.3
  464.7 2.5 copy-start.4
  476.0 4.9 %copy-start.2 = (f32[1024,1024]{1,0:T(8,128)S(1)}, f32[1024,1024]{1,0:T(8,128)}, u32[]{:S(2)}) copy-start(f32[1024,1024]{1,0:T(8,128)} %get-tuple-element.25) | copy-start | bytes 12582916

commit v3 on v2

--- a/solution.py
+++ b/solution.py
@@ -78,10 +78,10 @@
 
 
 def mlp_kernel(
-    y_one, y_two, dy_one, dy_two, w_up, w_down, w_att,
-    x_two, dx_one, uc_seq, att_full, part_own, part_near,
-    u_all, c_all, up_all, down_all, acc, uc_own, relay, y_buf, x_buf,
-    load_sem, y_sem, x_sem, w_send, w_recv, uc_send, uc_recv, att_send, att_recv, a2a_send, a2a_recv, relay_recv,
+    y_one, y_two, dy_one, dy_two, w_up, w_down, w_qkv, w_out,
+    x_two, dx_one, uc_seq, att_full, part_own, part_near, near_recv,
+    u_all, c_all, up_all, down_all, acc, uc_own, relay, y_buf, x_buf, up_raw, qkv_raw, att_own,
+    load_sem, y_sem, x_sem, w_send, w_recv, uc_send, uc_recv, att_send, att_recv, a2a_send, a2a_recv, relay_recv, near_sem,
 ):
     ring = Ring()
     half = 512
@@ -108,7 +108,8 @@
     def att(src, dst_slot, to, index):
         return ring.copy(src, att_full.at[dst_slot], att_send.at[index], att_recv.at[dst_slot], to)
 
-    att_out = [att(w_att, 4, SAME_F, 0), att(w_att, 2, SAME_T, 1), att(w_att, 1, PARTNER, 2)]
+    att_out = [att(att_own, 4, SAME_F, 0), att(att_own, 2, SAME_T, 1), att(att_own, 1, PARTNER, 2)]
+    att_keep = pltpu.make_async_copy(att_own, att_full.at[0], load_sem.at[6])
     att_near_t = [att(att_full.at[2], 6, SAME_F, 3), att(att_full.at[2], 3, PARTNER, 4)]
     att_near_f = [att(att_full.at[4], 5, PARTNER, 5)]
     att_far = [att(att_full.at[6], 7, PARTNER, 6)]
@@ -126,17 +127,26 @@
         for copy in copies:
             copy.start()
 
+    dim = w_out.shape[0]
+    near_rows = near_recv.shape[0]
+    near = ring.copy(acc.at[0, pl.ds(0, near_rows)], near_recv, near_sem.at[0], near_sem.at[1], SAME_F)
+
     loads = [
-        pltpu.make_async_copy(w_up, up_all.at[0], load_sem.at[0]),
-        pltpu.make_async_copy(w_down, down_all.at[0], load_sem.at[1]),
+        pltpu.make_async_copy(w_down, down_all.at[0], load_sem.at[0]),
+        pltpu.make_async_copy(w_up, up_raw, load_sem.at[1]),
         pltpu.make_async_copy(y_one, acc.at[0], load_sem.at[2]),
         pltpu.make_async_copy(dy_two, acc.at[1], load_sem.at[3]),
+        pltpu.make_async_copy(w_qkv, qkv_raw, load_sem.at[5]),
+        pltpu.make_async_copy(w_out, att_own.at[pl.ds(3 * dim, dim)], load_sem.at[7]),
     ]
     start(loads)
     ring.barrier()
     loads[0].wait()
+    start(w_own[1::2])
     loads[1].wait()
-    start(w_own)
+    for part in range(up_raw.shape[1] // dim):
+        up_all[0, pl.ds(part * dim, dim), :] = up_raw[:, pl.ds(part * dim, dim)].T
+    start(w_own[0::2])
     loads[2].wait()
     loads[3].wait()
 
@@ -150,6 +160,11 @@
 
     lax.fori_loop(0, acc.shape[1] // slab, normalize, 0)
     start(uc_out)
+    loads[4].wait()
+    for part in range(3):
+        att_own[pl.ds(part * dim, dim), :] = qkv_raw[part].T
+    loads[5].wait()
+    att_keep.start()
 
     def y_loads(step, buf):
         seq = ring.at_traced(7 - step)
@@ -252,10 +267,14 @@
 
         @pl.when(step == 5)
         def _():
-            ring.copy(w_att, att_full.at[2], att_send.at[0], att_recv.at[2], PARTNER).wait_recv()
+            ring.copy(att_own, att_full.at[2], att_send.at[0], att_recv.at[2], PARTNER).wait_recv()
             start(att_near_t)
-            ring.copy(w_att, att_full.at[4], att_send.at[0], att_recv.at[4], PARTNER).wait_recv()
+            ring.copy(att_own, att_full.at[4], att_send.at[0], att_recv.at[4], PARTNER).wait_recv()
             start(att_near_f)
+
+        @pl.when(step == 8)
+        def _():
+            near.start()
 
         @pl.when(step == 10)
         def _():
@@ -272,36 +291,41 @@
         return carry
 
     lax.fori_loop(0, 16, gradients, 0)
-    out_near = pltpu.make_async_copy(acc.at[0], part_near, load_sem.at[0])
+    out_near = pltpu.make_async_copy(acc.at[0, pl.ds(near_rows, acc.shape[1] - near_rows)], part_near, load_sem.at[0])
     out_own = pltpu.make_async_copy(acc.at[1], part_own, load_sem.at[1])
     out_near.start()
     out_own.start()
 
-    ring.copy(w_att, att_full.at[6], att_send.at[0], att_recv.at[6], PARTNER).wait_recv()
+    ring.copy(att_own, att_full.at[6], att_send.at[0], att_recv.at[6], PARTNER).wait_recv()
     start(att_far)
     for slot in (1, 3, 5, 7):
-        ring.copy(w_att, att_full.at[slot], att_send.at[0], att_recv.at[slot], PARTNER).wait_recv()
+        ring.copy(att_own, att_full.at[slot], att_send.at[0], att_recv.at[slot], PARTNER).wait_recv()
     for slot in range(1, 8):
         ring.copy(uc_own.at[slot], uc_seq.at[slot], a2a_send.at[0], a2a_recv.at[slot], PARTNER).wait_recv()
     for copy in w_own + w_near_t + w_near_f + w_far + uc_out + uc_pass + att_out + att_near_t + att_near_f + att_far + list(a2a_out.values()) + a2a_pass:
         copy.wait_send()
+    near.wait()
     uc_keep.wait()
+    att_keep.wait()
     out_near.wait()
     out_own.wait()
 
 
-def mlp_call(y_one, y_two, dy_one, dy_two, w_up, w_down, w_att):
+def mlp_call(y_one, y_two, dy_one, dy_two, w_up, w_down, w_qkv, w_out):
     tokens, hidden = y_one.shape
-    ffn = w_up.shape[0]
+    ffn = w_down.shape[0]
+    dim = w_out.shape[0]
+    near_rows = ffn // 2
     any_spec = pl.BlockSpec(memory_space=pl.ANY)
     dma, vmem = pltpu.SemaphoreType.DMA, pltpu.VMEM
     out_shape = (
         jax.ShapeDtypeStruct((tokens, hidden), F32),
         jax.ShapeDtypeStruct((tokens, hidden), F32),
         jax.ShapeDtypeStruct((8, 2, tokens // 8, hidden), BF16),
-        jax.ShapeDtypeStruct((8, *w_att.shape), BF16),
+        jax.ShapeDtypeStruct((8, 4 * dim, hidden), BF16),
         jax.ShapeDtypeStruct((2 * ffn, hidden), F32),
-        jax.ShapeDtypeStruct((2 * ffn, hidden), F32),
+        jax.ShapeDtypeStruct((2 * ffn - near_rows, hidden), F32),
+        jax.ShapeDtypeStruct((near_rows, hidden), F32),
     )
     scratch = [
         vmem((4, tokens, hidden), BF16), vmem((4, tokens, hidden), BF16),
@@ -309,30 +333,31 @@
         vmem((2, tokens, hidden), F32),
         vmem((8, 2, tokens // 8, hidden), BF16), vmem((2, 2, tokens // 8, hidden), BF16),
         vmem((2, 3, tokens // 8, hidden), F32), vmem((2, 2, tokens // 8, hidden), F32),
-        dma((5,)), dma((2, 3)), dma((2, 2)), dma((14,)), dma((8, 2)), dma((6,)), dma((4, 2)), dma((7,)), dma((8,)), dma((10,)), dma((8,)), dma((2,)),
+        vmem((hidden, ffn), BF16), vmem((3, hidden, dim), BF16), vmem((4 * dim, hidden), BF16),
+        dma((8,)), dma((2, 3)), dma((2, 2)), dma((14,)), dma((8, 2)), dma((6,)), dma((4, 2)), dma((7,)), dma((8,)), dma((10,)), dma((8,)), dma((2,)), dma((2,)),
     ]
     return pl.pallas_call(
         mlp_kernel,
         out_shape=out_shape,
-        in_specs=[any_spec] * 7,
-        out_specs=(any_spec,) * 6,
+        in_specs=[any_spec] * 8,
+        out_specs=(any_spec,) * 7,
         scratch_shapes=scratch,
         compiler_params=pltpu.CompilerParams(collective_id=0, has_side_effects=True, vmem_limit_bytes=VMEM_LIMIT),
         cost_estimate=pl.CostEstimate(flops=70 * 10**9, bytes_accessed=64 * 2**20, transcendentals=0),
         name="feed_forward",
-    )(y_one, y_two, dy_one, dy_two, w_up, w_down, w_att)
+    )(y_one, y_two, dy_one, dy_two, w_up, w_down, w_qkv, w_out)
 
 
 def attention_kernel(
-    scale, uc_seq, w_att, att_full, part_near,
+    scale, uc_seq, att_full, part_near,
     near_recv, d_att, o_pos, du_pos, wo_full,
-    uc_all, w_buf, qkv, d_ctx, d_qkv, o_all, du_all, part_send, part_keep, part_core, part_t, part_f, o_relay, du_relay,
+    uc_all, w_buf, qkv, d_ctx, d_qkv, o_all, du_all, part_send, part_keep, part_core, part_t, part_f, o_relay, du_relay, near_buf,
     load_sem, w_sem, wo_sem, near_sem, core_send, core_recv, t_send, t_recv, f_sem, o_send, o_recv, du_send, du_recv, o_relay_recv, du_relay_recv,
 ):
     ring = Ring()
     slab, hidden = uc_seq.shape[2], uc_seq.shape[3]
     seq_len = 8 * slab
-    dim = w_att.shape[0] // 4
+    dim = att_full.shape[1] // 4
     tile = 256
 
     def head_slot(step):
@@ -343,8 +368,8 @@
     def w_load(step, buf):
         return pltpu.make_async_copy(att_full.at[head_slot(step)], w_buf.at[buf], w_sem.at[buf])
 
-    w_load_own = pltpu.make_async_copy(w_att, w_buf.at[1], w_sem.at[1])
-    near = ring.copy(part_near, near_recv, near_sem.at[0], near_sem.at[1], SAME_F)
+    near_load = pltpu.make_async_copy(part_near, near_buf, near_sem.at[2])
+    near = ring.copy(near_buf, near_recv, near_sem.at[0], near_sem.at[1], SAME_F)
 
     def core_copy(step, buf):
         relation = head_slot(step) // 2
@@ -380,9 +405,11 @@
             copy.start()
 
     loads = [pltpu.make_async_copy(uc_seq.at[slot, which], uc_all.at[which, rows_of(slot)], load_sem.at[slot, which]) for slot in range(8) for which in (0, 1)]
+    near_load.start()
     start(loads)
     w_load(0, 0).start()
     ring.barrier()
+    near_load.wait()
     near.start()
     du_all[...] = jnp.zeros_like(du_all)
     for copy in loads:
@@ -394,13 +421,9 @@
         relation = slot // 2
         w_load(step, buf).wait()
 
-        @pl.when(step < 6)
+        @pl.when(step < 7)
         def _():
             w_load(step + 1, 1 - buf).start()
-
-        @pl.when(step == 6)
-        def _():
-            w_load_own.start()
 
         head = ring.at_traced(slot)
         columns = pl.ds(pl.multiple_of(head * dim, dim), dim)
@@ -503,16 +526,16 @@
     d_att_copy.wait()
 
 
-def attention_call(uc_seq, w_att, att_full, part_near):
+def attention_call(uc_seq, att_full, part_near):
     slab, hidden = uc_seq.shape[2:]
-    rows = w_att.shape[0]
+    rows = att_full.shape[1]
     dim = rows // 4
     seq_len = 8 * slab
     any_spec = pl.BlockSpec(memory_space=pl.ANY)
     dma, vmem = pltpu.SemaphoreType.DMA, pltpu.VMEM
     out_shape = (
         jax.ShapeDtypeStruct(part_near.shape, F32),
-        jax.ShapeDtypeStruct(w_att.shape, F32),
+        jax.ShapeDtypeStruct((rows, hidden), F32),
         jax.ShapeDtypeStruct((8, slab, hidden), BF16),
         jax.ShapeDtypeStruct((8, slab, hidden), F32),
         jax.ShapeDtypeStruct((8, dim, hidden), BF16),
@@ -521,37 +544,82 @@
         vmem((2, seq_len, hidden), BF16), vmem((2, rows, hidden), BF16), vmem((seq_len, 3 * dim), BF16), vmem((seq_len, dim), BF16), vmem((seq_len, 3 * dim), BF16),
         vmem((seq_len, hidden), BF16), vmem((seq_len, hidden), F32),
         vmem((2, rows, hidden), F32), vmem((4, rows, hidden), F32), vmem((4, rows, hidden), F32), vmem((2, rows, hidden), F32), vmem((rows, hidden), F32),
-        vmem((2, slab, hidden), BF16), vmem((2, slab, hidden), F32),
-        dma((8, 2)), dma((2,)), dma((1,)), dma((2,)), dma((2,)), dma((4,)), dma((2,)), dma((2,)), dma((2,)), dma((10,)), dma((8,)), dma((10,)), dma((8,)), dma((2,)), dma((2,)),
+        vmem((2, slab, hidden), BF16), vmem((2, slab, hidden), F32), vmem(part_near.shape, F32),
+        dma((8, 2)), dma((2,)), dma((1,)), dma((3,)), dma((2,)), dma((4,)), dma((2,)), dma((2,)), dma((2,)), dma((10,)), dma((8,)), dma((10,)), dma((8,)), dma((2,)), dma((2,)),
     ]
     return pl.pallas_call(
         functools.partial(attention_kernel, dim ** -0.5),
         out_shape=out_shape,
-        in_specs=[any_spec] * 4,
+        in_specs=[any_spec] * 3,
         out_specs=(any_spec,) * 5,
         scratch_shapes=scratch,
         compiler_params=pltpu.CompilerParams(collective_id=1, has_side_effects=True, vmem_limit_bytes=VMEM_LIMIT),
         cost_estimate=pl.CostEstimate(flops=40 * 10**9, bytes_accessed=64 * 2**20, transcendentals=0),
         name="attention",
-    )(uc_seq, w_att, att_full, part_near)
+    )(uc_seq, att_full, part_near)
+
+
+def finish_kernel(
+    y_one, o_pos, wo_full, x_two, dx_one, dy_two, du_pos, up_own, up_near, up_rest, down_own, down_rest, d_qkv, d_out,
+    x_one_out, x_two_out, dx_one_out, dx_two_out, dw_up, dw_down, dw_qkv, dw_out,
+):
+    x_one_out[0] = y_one[0] - dot_nn(o_pos[0], wo_full[...])
+    x_two_out[0] = x_two[...]
+    dx_one_out[0] = dx_one[...]
+    dx_two_out[0] = dy_two[0] + rms_back(x_two[...], du_pos[0])
+    half = up_near.shape[0]
+    dw_up[:, pl.ds(0, half)] = (up_own[pl.ds(0, half), :] + up_near[...]).T
+    dw_up[:, pl.ds(half, half)] = (up_own[pl.ds(half, half), :] + up_rest[...]).T
+    dw_down[...] = down_own[...] + down_rest[...]
+    dim = dw_qkv.shape[2]
+    for part in range(3):
+        dw_qkv[pl.ds(part, dw_qkv.shape[0] // 3, stride=3), 0, :] = d_qkv[pl.ds(part * dim, dim), :].T
+    dw_out[...] = d_out[...]
+
+
+def finish_call(y_one, o_pos, wo_full, x_two, dx_one, dy_two, du_pos, part_own, near_first, near_rest, d_att):
+    seqs, slab, hidden = y_one.shape
+    ffn = part_own.shape[0] // 2
+    dim = d_att.shape[0] // 4
+    half = near_first.shape[0]
+    state = pl.BlockSpec((1, slab, hidden), lambda step: (step, 0, 0))
+    flat = pl.BlockSpec((slab, hidden), lambda step: (step, 0))
+    up_first = pl.BlockSpec((half, slab), lambda step: (0, step))
+    rows = ffn // seqs
+    in_specs = [
+        state, state, pl.BlockSpec((hidden, hidden), lambda step: (0, 0)), flat, flat, state, state,
+        pl.BlockSpec((ffn, slab), lambda step: (0, step)), up_first, up_first,
+        pl.BlockSpec((rows, hidden), lambda step: (seqs + step, 0)), pl.BlockSpec((rows, hidden), lambda step: (half // rows + step, 0)),
+        pl.BlockSpec((3 * dim, slab), lambda step: (0, step)), pl.BlockSpec((dim // seqs, hidden), lambda step: (3 * seqs + step, 0)),
+    ]
+    out_specs = [state] * 4 + [
+        pl.BlockSpec((slab, ffn), lambda step: (step, 0)), pl.BlockSpec((rows, hidden), lambda step: (step, 0)),
+        pl.BlockSpec((3 * slab, 1, dim), lambda step: (step, 0, 0)), pl.BlockSpec((dim // seqs, hidden), lambda step: (step, 0)),
+    ]
+    out_shape = [jax.ShapeDtypeStruct(y_one.shape, F32)] * 4 + [jax.ShapeDtypeStruct(shape, F32) for shape in ((hidden, ffn), (ffn, hidden), (3 * hidden, 1, dim), (dim, hidden))]
+    return pl.pallas_call(
+        finish_kernel,
+        out_shape=out_shape,
+        grid=(seqs,),
+        in_specs=in_specs,
+        out_specs=out_specs,
+        compiler_params=pltpu.CompilerParams(dimension_semantics=("arbitrary",), vmem_limit_bytes=VMEM_LIMIT),
+        cost_estimate=pl.CostEstimate(flops=2 * 10**9, bytes_accessed=60 * 2**20, transcendentals=0),
+        name="finish",
+    )(y_one, o_pos, wo_full, x_two, dx_one, dy_two, du_pos, part_own, near_first, near_rest, part_own, near_rest, d_att, d_att)
 
 
 def local_backward(y_one, y_two, dy_one, dy_two, w_qkv, w_out, w_up, w_down):
-    shape = y_one.shape
-    hidden = shape[2]
+    hidden = y_one.shape[2]
     _, _, _, parts, dim = w_qkv.shape
     flat = [tensor.reshape(-1, hidden) for tensor in (y_one, y_two, dy_one, dy_two)]
-    w_att = jnp.concatenate([w_qkv.reshape(hidden, parts * dim).T, w_out.reshape(dim, hidden)])
-    x_two, dx_one, uc_seq, att_full, part_own, part_near = mlp_call(*flat, w_up[0].T, w_down[0], w_att)
-    near_recv, d_att, o_pos, du_pos, wo_full = attention_call(uc_seq, w_att, att_full, part_near)
-    grads = part_own + near_recv
-    ffn = w_down.shape[1]
-    x_one = y_one - jnp.einsum("bsm,mh->bsh", o_pos, wo_full.reshape(-1, hidden), preferred_element_type=F32)
-    x_two = x_two.reshape(shape)
-    dx_two = dy_two + rms_back(x_two, du_pos)
-    dw_qkv = d_att[: parts * dim].T.reshape(1, hidden, 1, parts, dim)
-    dw_out = d_att[parts * dim :].reshape(1, 1, dim, hidden)
-    return (x_one, x_two, dx_one.reshape(shape), dx_two, dw_qkv, dw_out, grads[:ffn].T[None], grads[ffn:][None])
+    qkv_parts = jnp.swapaxes(w_qkv[0, :, 0], 0, 1)
+    x_two, dx_one, uc_seq, att_full, part_own, part_near, near_first = mlp_call(*flat, w_up[0], w_down[0], qkv_parts, w_out[0, 0])
+    near_rest, d_att, o_pos, du_pos, wo_full = attention_call(uc_seq, att_full, part_near)
+    x_one, x_two, dx_one, dx_two, dw_up, dw_down, dw_qkv, dw_out = finish_call(
+        y_one, o_pos, wo_full.reshape(-1, hidden), x_two, dx_one, dy_two, du_pos, part_own, near_first, near_rest, d_att
+    )
+    return (x_one, x_two, dx_one, dx_two, dw_qkv.reshape(1, hidden, 1, parts, dim), dw_out[None, None], dw_up[None], dw_down[None])
 
 
 def solution(mesh):

time: 483 us -> 475 us (0.983)
  Pallas kernels: 442 us -> 474 us
  local copies, waits for them, and re-layouts: 25.7 us -> 0 us
  other arithmetic: 9.89 us -> 0 us
    pallas_call x1 -> x2, Pallas kernels: 208 us -> 243 us  [the longest x1 222 us: mlp_call(): pl.pallas_call(mlp_kernel, out_shape=out_shape, in_specs=[any_spec] * 8,...]
    unnamed x24 -> x0, local copies, waits for them, and re-layouts: 21.8 us -> none
    add x2 -> x0, other arithmetic: 7.11 us -> none  [the longest x1 4.61 us: local_backward(): grads = part_own + near_recv]
where the time goes in v3:
time: 475 us
  Pallas kernels  474 us (100%)
    pallas_call x1, Pallas kernels, attention_call(): pl.pallas_call(functools.partial(attention_kernel, dim ** (-0.5)), out_sh...  231 us
    pallas_call x1, Pallas kernels, mlp_call(): pl.pallas_call(mlp_kernel, out_shape=out_shape, in_specs=[any_spec] * 8,...  222 us
    pallas_call x1, Pallas kernels, finish_call(): pl.pallas_call(finish_kernel, out_shape=out_shape, grid=(seqs,), in_specs...  20.8 us

profile of v3, /device:TPU:112, one launch (start us, length us, event | category | flops | bytes accessed | tf_op | source)
XLA Modules:
  0.0 474.8 jit_solution(15481384689458776465)
XLA Ops:
  0.6 221.9 %feed_forward.1 = (f32[1024,1024]{1,0:T(8,128)}, f32[1024,1024]{1,0:T(8,128)}, bf16[8,2,128,1024]{3,2,1,0:T(8,128)(2,1)}, bf16[8,512,1024]{2,1,0:T(8,128)(2,1)},...) custom-call(f32[1024,1024]{1,0:T(8,128)} %bitcast.17, f32[1024,1024]{1,0:T(8,128)} %bitcast.20, ...), custom_call_target="tpu_custom_call" | custom-call | flops 70000001024 | bytes 67108864 | tf_op jit(solution)/shard_map/feed_forward/pallas_call | solution.py:339
  222.5 231.4 %attention.1 = (f32[768,1024]{1,0:T(8,128)}, f32[512,1024]{1,0:T(8,128)}, bf16[8,128,1024]{2,1,0:T(8,128)(2,1)}, f32[8,128,1024]{2,1,0:T(8,128)}, bf16[8,128,1024]{2,1,0:T(8,128)(2,1)}) custom-call(bf16[8,2,128,1024]{3,2,1,0:T(8,128)(2,1)} %get-tuple-element.28.uc_seq, bf16[8,512,1024]{2,1,0:T(8,128)(2,1)} %get-tuple-element.29.att_full, ...), custom_call_target="tpu_custom_call" | custom-call | flops 40000000000 | bytes 67108864 | tf_op jit(solution)/shard_map/attention/pallas_call | solution.py:550
  454.0 20.8 %finish.1 = (f32[8,128,1024]{2,1,0:T(8,128)}, f32[8,128,1024]{2,1,0:T(8,128)}, f32[8,128,1024]{2,1,0:T(8,128)}, f32[8,128,1024]{2,1,0:T(8,128)}, f32[1024,512]{1...) custom-call(f32[8,128,1024]{2,1,0:T(8,128)} %y_one.1, ...), custom_call_target="tpu_custom_call" | custom-call | flops 2000000000 | bytes 62914560 | tf_op jit(solution)/shard_map/finish/pallas_call | solution.py:600

commit v4 on v3

--- a/solution.py
+++ b/solution.py
@@ -110,9 +110,8 @@
 
     att_out = [att(att_own, 4, SAME_F, 0), att(att_own, 2, SAME_T, 1), att(att_own, 1, PARTNER, 2)]
     att_keep = pltpu.make_async_copy(att_own, att_full.at[0], load_sem.at[6])
-    att_near_t = [att(att_full.at[2], 6, SAME_F, 3), att(att_full.at[2], 3, PARTNER, 4)]
-    att_near_f = [att(att_full.at[4], 5, PARTNER, 5)]
-    att_far = [att(att_full.at[6], 7, PARTNER, 6)]
+    att_near_f = [att(att_full.at[4], 5, PARTNER, 3)]
+    att_near_t = [att(att_full.at[2], 3, PARTNER, 4)]
 
     a2a_out = {slot: ring.copy(uc_own.at[slot], uc_seq.at[slot], a2a_send.at[slot], a2a_recv.at[slot], slot) for slot in (1, 2, 3, 4, 5)}
     a2a_out[SAME_O] = ring.copy(uc_own.at[SAME_O], relay.at[0], a2a_send.at[SAME_O], relay_recv.at[0], SAME_T)
@@ -265,18 +264,15 @@
         def _():
             start(uc_pass)
 
-        @pl.when(step == 5)
-        def _():
+        @pl.when(step == 8)
+        def _():
+            near.start()
+            ring.copy(att_own, att_full.at[4], att_send.at[0], att_recv.at[4], PARTNER).wait_recv()
+            start(att_near_f)
             ring.copy(att_own, att_full.at[2], att_send.at[0], att_recv.at[2], PARTNER).wait_recv()
             start(att_near_t)
-            ring.copy(att_own, att_full.at[4], att_send.at[0], att_recv.at[4], PARTNER).wait_recv()
-            start(att_near_f)
-
-        @pl.when(step == 8)
-        def _():
-            near.start()
-
-        @pl.when(step == 10)
+
+        @pl.when(step == 9)
         def _():
             for index in (0, 1):
                 ring.copy(relay.at[index], relay.at[index], a2a_send.at[0], relay_recv.at[index], PARTNER).wait_recv()
@@ -296,13 +292,11 @@
     out_near.start()
     out_own.start()
 
-    ring.copy(att_own, att_full.at[6], att_send.at[0], att_recv.at[6], PARTNER).wait_recv()
-    start(att_far)
-    for slot in (1, 3, 5, 7):
+    for slot in (1, 3, 5):
         ring.copy(att_own, att_full.at[slot], att_send.at[0], att_recv.at[slot], PARTNER).wait_recv()
     for slot in range(1, 8):
         ring.copy(uc_own.at[slot], uc_seq.at[slot], a2a_send.at[0], a2a_recv.at[slot], PARTNER).wait_recv()
-    for copy in w_own + w_near_t + w_near_f + w_far + uc_out + uc_pass + att_out + att_near_t + att_near_f + att_far + list(a2a_out.values()) + a2a_pass:
+    for copy in w_own + w_near_t + w_near_f + w_far + uc_out + uc_pass + att_out + att_near_t + att_near_f + list(a2a_out.values()) + a2a_pass:
         copy.wait_send()
     near.wait()
     uc_keep.wait()
@@ -315,14 +309,14 @@
     tokens, hidden = y_one.shape
     ffn = w_down.shape[0]
     dim = w_out.shape[0]
-    near_rows = ffn // 2
+    near_rows = ffn
     any_spec = pl.BlockSpec(memory_space=pl.ANY)
     dma, vmem = pltpu.SemaphoreType.DMA, pltpu.VMEM
     out_shape = (
         jax.ShapeDtypeStruct((tokens, hidden), F32),
         jax.ShapeDtypeStruct((tokens, hidden), F32),
         jax.ShapeDtypeStruct((8, 2, tokens // 8, hidden), BF16),
-        jax.ShapeDtypeStruct((8, 4 * dim, hidden), BF16),
+        jax.ShapeDtypeStruct((6, 4 * dim, hidden), BF16),
         jax.ShapeDtypeStruct((2 * ffn, hidden), F32),
         jax.ShapeDtypeStruct((2 * ffn - near_rows, hidden), F32),
         jax.ShapeDtypeStruct((near_rows, hidden), F32),
@@ -334,7 +328,7 @@
         vmem((8, 2, tokens // 8, hidden), BF16), vmem((2, 2, tokens // 8, hidden), BF16),
         vmem((2, 3, tokens // 8, hidden), F32), vmem((2, 2, tokens // 8, hidden), F32),
         vmem((hidden, ffn), BF16), vmem((3, hidden, dim), BF16), vmem((4 * dim, hidden), BF16),
-        dma((8,)), dma((2, 3)), dma((2, 2)), dma((14,)), dma((8, 2)), dma((6,)), dma((4, 2)), dma((7,)), dma((8,)), dma((10,)), dma((8,)), dma((2,)), dma((2,)),
+        dma((8,)), dma((2, 3)), dma((2, 2)), dma((14,)), dma((8, 2)), dma((6,)), dma((4, 2)), dma((5,)), dma((6,)), dma((10,)), dma((8,)), dma((2,)), dma((2,)),
     ]
     return pl.pallas_call(
         mlp_kernel,
@@ -350,9 +344,9 @@
 
 def attention_kernel(
     scale, uc_seq, att_full, part_near,
-    near_recv, d_att, o_pos, du_pos, wo_full,
-    uc_all, w_buf, qkv, d_ctx, d_qkv, o_all, du_all, part_send, part_keep, part_core, part_t, part_f, o_relay, du_relay, near_buf,
-    load_sem, w_sem, wo_sem, near_sem, core_send, core_recv, t_send, t_recv, f_sem, o_send, o_recv, du_send, du_recv, o_relay_recv, du_relay_recv,
+    near_recv, d_att, o_pos, du_pos, wo_full, att_far,
+    uc_all, w_buf, qkv, d_ctx, d_qkv, o_all, du_all, part_send, part_keep, part_core, own_t, far_t, own_f, far_f, o_relay, du_relay, near_buf,
+    load_sem, w_sem, wo_sem, near_sem, core_send, core_recv, part_out, part_in, far_sem, o_send, o_recv, du_send, du_recv, o_relay_recv, du_relay_recv,
 ):
     ring = Ring()
     slab, hidden = uc_seq.shape[2], uc_seq.shape[3]
@@ -361,12 +355,16 @@
     tile = 256
 
     def head_slot(step):
-        pair = step // 2
-        relation = jnp.where(pair == 0, 1, jnp.where(pair == 1, 3, jnp.where(pair == 2, 2, 0)))
-        return relation * 2 + 1 - step % 2
+        return (step // 2 + 1) % 4 * 2 + 1 - step % 2
 
     def w_load(step, buf):
         return pltpu.make_async_copy(att_full.at[head_slot(step)], w_buf.at[buf], w_sem.at[buf])
+
+    def w_load_far(step, buf):
+        return pltpu.make_async_copy(att_far.at[1 - step % 2], w_buf.at[buf], w_sem.at[buf])
+
+    far_from_t = ring.copy(att_full.at[SAME_F], att_far.at[0], far_sem.at[0], far_sem.at[1], SAME_T)
+    far_from_core = ring.copy(att_far.at[0], att_far.at[1], far_sem.at[2], far_sem.at[3], PARTNER)
 
     near_load = pltpu.make_async_copy(part_near, near_buf, near_sem.at[2])
     near = ring.copy(near_buf, near_recv, near_sem.at[0], near_sem.at[1], SAME_F)
@@ -375,11 +373,17 @@
         relation = head_slot(step) // 2
         return ring.copy(part_send.at[buf], part_core.at[relation], core_send.at[buf], core_recv.at[relation], PARTNER)
 
-    t_copies = [
-        ring.copy(part_keep.at[1], part_t.at[0], t_send.at[0], t_recv.at[0], SAME_T),
-        ring.copy(part_keep.at[3], part_t.at[1], t_send.at[1], t_recv.at[1], SAME_T),
-    ]
-    f_copy = ring.copy(part_keep.at[2], part_f, f_sem.at[0], f_sem.at[1], SAME_F)
+    rows_a, rows_b = pl.ds(0, 3 * dim), pl.ds(3 * dim, dim)
+
+    def part(src, dst, index, slot):
+        return ring.copy(src, dst, part_out.at[index], part_in.at[index], slot)
+
+    t_own_a = part(part_keep.at[1, rows_a], own_t.at[rows_a], 0, SAME_T)
+    t_far_a = part(part_keep.at[3, rows_a], far_t, 1, SAME_T)
+    t_own_b = part(part_keep.at[1, rows_b], own_t.at[rows_b], 2, SAME_T)
+    f_own_b = part(part_keep.at[2, rows_b], own_f.at[rows_b], 3, SAME_F)
+    f_far_b = part(part_keep.at[3, rows_b], far_f, 4, SAME_F)
+    f_own_a = part(part_keep.at[2, rows_a], own_f.at[rows_a], 5, SAME_F)
 
     def rows_of(slot):
         return pl.ds(slot * slab, slab)
@@ -409,6 +413,7 @@
     start(loads)
     w_load(0, 0).start()
     ring.barrier()
+    far_from_t.start()
     near_load.wait()
     near.start()
     du_all[...] = jnp.zeros_like(du_all)
@@ -419,11 +424,19 @@
         buf = step % 2
         slot = head_slot(step)
         relation = slot // 2
-        w_load(step, buf).wait()
-
-        @pl.when(step < 7)
+        pltpu.make_async_copy(att_full.at[0], w_buf.at[buf], w_sem.at[buf]).wait()
+
+        @pl.when(step == 3)
+        def _():
+            far_from_core.wait_recv()
+
+        @pl.when((step < 3) | (step == 5) | (step == 6))
         def _():
             w_load(step + 1, 1 - buf).start()
+
+        @pl.when((step == 3) | (step == 4))
+        def _():
+            w_load_far(step + 1, 1 - buf).start()
 
         head = ring.at_traced(slot)
         columns = pl.ds(pl.multiple_of(head * dim, dim), dim)
@@ -482,17 +495,21 @@
 
         @pl.when(step == 1)
         def _():
-            t_copies[0].start()
+            t_own_a.start()
+
+        @pl.when(step == 2)
+        def _():
+            far_from_t.wait_recv()
+            far_from_core.start()
 
         @pl.when(step == 3)
         def _():
-            t_copies[1].start()
+            f_own_b.start()
 
         @pl.when(step == 5)
         def _():
-            t_copies[1].wait_recv()
-            part_keep[2] += part_t[1]
-            f_copy.start()
+            t_far_a.start()
+            f_far_b.start()
 
         wo_copy.wait()
         return carry
@@ -502,23 +519,31 @@
     start(du_out)
     o_keep.start()
     du_keep.start()
+    f_far_b.wait_recv()
+    part_keep[1, rows_b] += far_f[...]
+    t_own_b.start()
+    t_far_a.wait_recv()
+    part_keep[2, rows_a] += far_t[...]
+    f_own_a.start()
     for copy in o_out[:2]:
         copy.wait_recv()
     start(o_pass)
-    t_copies[0].wait_recv()
-    part_keep[0] += part_t[0]
-    f_copy.wait_recv()
-    part_keep[0] += part_f[...]
-    d_att_copy = pltpu.make_async_copy(part_keep.at[0], d_att, load_sem.at[0, 0])
-    d_att_copy.start()
     for copy in du_out[:2]:
         copy.wait_recv()
     start(du_pass)
+    t_own_a.wait_recv()
+    t_own_b.wait_recv()
+    part_keep[0] += own_t[...]
+    f_own_a.wait_recv()
+    f_own_b.wait_recv()
+    part_keep[0] += own_f[...]
+    d_att_copy = pltpu.make_async_copy(part_keep.at[0], d_att, load_sem.at[0, 0])
+    d_att_copy.start()
 
     for dst, recv_sem in ((o_pos, o_recv), (du_pos, du_recv)):
         for slot in range(1, 8):
             ring.copy(dst.at[0], dst.at[ring.at(slot)], near_sem.at[0], recv_sem.at[slot], PARTNER).wait_recv()
-    for copy in o_out + du_out + o_pass + du_pass + t_copies + [f_copy, near, core_copy(4, 0), core_copy(6, 1)]:
+    for copy in o_out + du_out + o_pass + du_pass + [t_own_a, t_far_a, t_own_b, f_own_b, f_far_b, f_own_a, far_from_t, far_from_core, near, core_copy(4, 0), core_copy(6, 1)]:
         copy.wait_send()
     near.wait_recv()
     o_keep.wait()
@@ -539,19 +564,21 @@
         jax.ShapeDtypeStruct((8, slab, hidden), BF16),
         jax.ShapeDtypeStruct((8, slab, hidden), F32),
         jax.ShapeDtypeStruct((8, dim, hidden), BF16),
+        jax.ShapeDtypeStruct((2, rows, hidden), BF16),
     )
     scratch = [
         vmem((2, seq_len, hidden), BF16), vmem((2, rows, hidden), BF16), vmem((seq_len, 3 * dim), BF16), vmem((seq_len, dim), BF16), vmem((seq_len, 3 * dim), BF16),
         vmem((seq_len, hidden), BF16), vmem((seq_len, hidden), F32),
-        vmem((2, rows, hidden), F32), vmem((4, rows, hidden), F32), vmem((4, rows, hidden), F32), vmem((2, rows, hidden), F32), vmem((rows, hidden), F32),
+        vmem((2, rows, hidden), F32), vmem((4, rows, hidden), F32), vmem((4, rows, hidden), F32),
+        vmem((rows, hidden), F32), vmem((3 * dim, hidden), F32), vmem((rows, hidden), F32), vmem((dim, hidden), F32),
         vmem((2, slab, hidden), BF16), vmem((2, slab, hidden), F32), vmem(part_near.shape, F32),
-        dma((8, 2)), dma((2,)), dma((1,)), dma((3,)), dma((2,)), dma((4,)), dma((2,)), dma((2,)), dma((2,)), dma((10,)), dma((8,)), dma((10,)), dma((8,)), dma((2,)), dma((2,)),
+        dma((8, 2)), dma((2,)), dma((1,)), dma((3,)), dma((2,)), dma((4,)), dma((6,)), dma((6,)), dma((4,)), dma((10,)), dma((8,)), dma((10,)), dma((8,)), dma((2,)), dma((2,)),
     ]
     return pl.pallas_call(
         functools.partial(attention_kernel, dim ** -0.5),
         out_shape=out_shape,
         in_specs=[any_spec] * 3,
-        out_specs=(any_spec,) * 5,
+        out_specs=(any_spec,) * 6,
         scratch_shapes=scratch,
         compiler_params=pltpu.CompilerParams(collective_id=1, has_side_effects=True, vmem_limit_bytes=VMEM_LIMIT),
         cost_estimate=pl.CostEstimate(flops=40 * 10**9, bytes_accessed=64 * 2**20, transcendentals=0),
@@ -560,36 +587,32 @@
 
 
 def finish_kernel(
-    y_one, o_pos, wo_full, x_two, dx_one, dy_two, du_pos, up_own, up_near, up_rest, down_own, down_rest, d_qkv, d_out,
+    y_one, o_pos, wo_full, x_two, dx_one, dy_two, du_pos, up_own, up_near, down_own, down_near, d_qkv, d_out,
     x_one_out, x_two_out, dx_one_out, dx_two_out, dw_up, dw_down, dw_qkv, dw_out,
 ):
     x_one_out[0] = y_one[0] - dot_nn(o_pos[0], wo_full[...])
     x_two_out[0] = x_two[...]
     dx_one_out[0] = dx_one[...]
     dx_two_out[0] = dy_two[0] + rms_back(x_two[...], du_pos[0])
-    half = up_near.shape[0]
-    dw_up[:, pl.ds(0, half)] = (up_own[pl.ds(0, half), :] + up_near[...]).T
-    dw_up[:, pl.ds(half, half)] = (up_own[pl.ds(half, half), :] + up_rest[...]).T
-    dw_down[...] = down_own[...] + down_rest[...]
+    dw_up[...] = (up_own[...] + up_near[...]).T
+    dw_down[...] = down_own[...] + down_near[...]
     dim = dw_qkv.shape[2]
     for part in range(3):
         dw_qkv[pl.ds(part, dw_qkv.shape[0] // 3, stride=3), 0, :] = d_qkv[pl.ds(part * dim, dim), :].T
     dw_out[...] = d_out[...]
 
 
-def finish_call(y_one, o_pos, wo_full, x_two, dx_one, dy_two, du_pos, part_own, near_first, near_rest, d_att):
+def finish_call(y_one, o_pos, wo_full, x_two, dx_one, dy_two, du_pos, part_own, up_near, down_near, d_att):
     seqs, slab, hidden = y_one.shape
     ffn = part_own.shape[0] // 2
     dim = d_att.shape[0] // 4
-    half = near_first.shape[0]
     state = pl.BlockSpec((1, slab, hidden), lambda step: (step, 0, 0))
     flat = pl.BlockSpec((slab, hidden), lambda step: (step, 0))
-    up_first = pl.BlockSpec((half, slab), lambda step: (0, step))
+    up = pl.BlockSpec((ffn, slab), lambda step: (0, step))
     rows = ffn // seqs
     in_specs = [
         state, state, pl.BlockSpec((hidden, hidden), lambda step: (0, 0)), flat, flat, state, state,
-        pl.BlockSpec((ffn, slab), lambda step: (0, step)), up_first, up_first,
-        pl.BlockSpec((rows, hidden), lambda step: (seqs + step, 0)), pl.BlockSpec((rows, hidden), lambda step: (half // rows + step, 0)),
+        up, up, pl.BlockSpec((rows, hidden), lambda step: (seqs + step, 0)), pl.BlockSpec((rows, hidden), lambda step: (step, 0)),
         pl.BlockSpec((3 * dim, slab), lambda step: (0, step)), pl.BlockSpec((dim // seqs, hidden), lambda step: (3 * seqs + step, 0)),
     ]
     out_specs = [state] * 4 + [
@@ -606,7 +629,7 @@
         compiler_params=pltpu.CompilerParams(dimension_semantics=("arbitrary",), vmem_limit_bytes=VMEM_LIMIT),
         cost_estimate=pl.CostEstimate(flops=2 * 10**9, bytes_accessed=60 * 2**20, transcendentals=0),
         name="finish",
-    )(y_one, o_pos, wo_full, x_two, dx_one, dy_two, du_pos, part_own, near_first, near_rest, part_own, near_rest, d_att, d_att)
+    )(y_one, o_pos, wo_full, x_two, dx_one, dy_two, du_pos, part_own, up_near, part_own, down_near, d_att, d_att)
 
 
 def local_backward(y_one, y_two, dy_one, dy_two, w_qkv, w_out, w_up, w_down):
@@ -614,10 +637,10 @@
     _, _, _, parts, dim = w_qkv.shape
     flat = [tensor.reshape(-1, hidden) for tensor in (y_one, y_two, dy_one, dy_two)]
     qkv_parts = jnp.swapaxes(w_qkv[0, :, 0], 0, 1)
-    x_two, dx_one, uc_seq, att_full, part_own, part_near, near_first = mlp_call(*flat, w_up[0], w_down[0], qkv_parts, w_out[0, 0])
-    near_rest, d_att, o_pos, du_pos, wo_full = attention_call(uc_seq, att_full, part_near)
+    x_two, dx_one, uc_seq, att_full, part_own, part_near, up_near = mlp_call(*flat, w_up[0], w_down[0], qkv_parts, w_out[0, 0])
+    down_near, d_att, o_pos, du_pos, wo_full, _ = attention_call(uc_seq, att_full, part_near)
     x_one, x_two, dx_one, dx_two, dw_up, dw_down, dw_qkv, dw_out = finish_call(
-        y_one, o_pos, wo_full.reshape(-1, hidden), x_two, dx_one, dy_two, du_pos, part_own, near_first, near_rest, d_att
+        y_one, o_pos, wo_full.reshape(-1, hidden), x_two, dx_one, dy_two, du_pos, part_own, up_near, down_near, d_att
     )
     return (x_one, x_two, dx_one, dx_two, dw_qkv.reshape(1, hidden, 1, parts, dim), dw_out[None, None], dw_up[None], dw_down[None])
 

time: 475 us -> 443 us (0.933)
  Pallas kernels: 474 us -> 442 us
    pallas_call x1, Pallas kernels: 231 us -> 207 us  [attention_call(): pl.pallas_call(functools.partial(attention_kernel, dim ** (-0.5)), out_sh...]
    pallas_call x1, Pallas kernels: 222 us -> 213 us  [mlp_call(): pl.pallas_call(mlp_kernel, out_shape=out_shape, in_specs=[any_spec] * 8,...]
where the time goes in v4:
time: 443 us; the launch traced here: 442 us
  Pallas kernels  442 us (100%)
    pallas_call x1, Pallas kernels, mlp_call(): pl.pallas_call(mlp_kernel, out_shape=out_shape, in_specs=[any_spec] * 8,...  213 us
    pallas_call x1, Pallas kernels, attention_call(): pl.pallas_call(functools.partial(attention_kernel, dim ** (-0.5)), out_sh...  207 us
    pallas_call x1, Pallas kernels, finish_call(): pl.pallas_call(finish_kernel, out_shape=out_shape, grid=(seqs,), in_specs...  21.4 us

profile of v4, /device:TPU:112, one launch (start us, length us, event | category | flops | bytes accessed | tf_op | source)
XLA Modules:
  0.0 442.3 jit_solution(9059275916225690570)
XLA Ops:
  0.6 212.8 %feed_forward.1 = (f32[1024,1024]{1,0:T(8,128)}, f32[1024,1024]{1,0:T(8,128)}, bf16[8,2,128,1024]{3,2,1,0:T(8,128)(2,1)}, bf16[6,512,1024]{2,1,0:T(8,128)(2,1)},...) custom-call(f32[1024,1024]{1,0:T(8,128)} %bitcast.17, f32[1024,1024]{1,0:T(8,128)} %bitcast.20, ...), custom_call_target="tpu_custom_call" | custom-call | flops 70000001024 | bytes 67108864 | tf_op jit(solution)/shard_map/feed_forward/pallas_call | solution.py:333
  213.4 207.5 %attention.1 = (f32[512,1024]{1,0:T(8,128)}, f32[512,1024]{1,0:T(8,128)}, bf16[8,128,1024]{2,1,0:T(8,128)(2,1)}, f32[8,128,1024]{2,1,0:T(8,128)}, bf16[8,128,102...) custom-call(bf16[8,2,128,1024]{3,2,1,0:T(8,128)(2,1)} %get-tuple-element.28.uc_seq, ...), custom_call_target="tpu_custom_call" | custom-call | flops 40000000000 | bytes 67108864 | tf_op jit(solution)/shard_map/attention/pallas_call | solution.py:577
  420.9 21.4 %finish.1 = (f32[8,128,1024]{2,1,0:T(8,128)}, f32[8,128,1024]{2,1,0:T(8,128)}, f32[8,128,1024]{2,1,0:T(8,128)}, f32[8,128,1024]{2,1,0:T(8,128)}, f32[1024,512]{1...) custom-call(f32[8,128,1024]{2,1,0:T(8,128)} %y_one.1, ...), custom_call_target="tpu_custom_call" | custom-call | flops 2000000000 | bytes 62914560 | tf_op jit(solution)/shard_map/finish/pallas_call | solution.py:623

commit v5 on v4

--- a/solution.py
+++ b/solution.py
@@ -8,6 +8,7 @@
 from jax.sharding import PartitionSpec as P
 
 RMS_EPS = 1e-6
+LOG2_E = 1.4426950408889634
 MESH = pl.DeviceIdType.MESH
 BF16, F32 = jnp.bfloat16, jnp.float32
 VMEM_LIMIT = 64 * 1024 * 1024 - 65536
@@ -352,7 +353,7 @@
     slab, hidden = uc_seq.shape[2], uc_seq.shape[3]
     seq_len = 8 * slab
     dim = att_full.shape[1] // 4
-    tile = 256
+    tile = 512
 
     def head_slot(step):
         return (step // 2 + 1) % 4 * 2 + 1 - step % 2
@@ -445,25 +446,18 @@
         qkv[...] = dot_nt(uc_all[0], w_buf[buf, pl.ds(0, 3 * dim), :]).astype(BF16)
         d_ctx[...] = dot_nt(uc_all[1], w_buf[buf, pl.ds(3 * dim, dim), :]).astype(BF16)
 
-        def query_tile(part, carry):
-            d_key, d_value = carry
-            rows = pl.ds(pl.multiple_of(part * tile, tile), tile)
-            query, key, value = qkv[rows, pl.ds(0, dim)], qkv[:, pl.ds(dim, dim)], qkv[:, pl.ds(2 * dim, dim)]
-            scores = dot_nt(query, key) * scale
-            grown = jnp.exp(scores - jnp.max(scores, axis=-1, keepdims=True))
-            prob = grown / jnp.sum(grown, axis=-1, keepdims=True)
-            prob_b = prob.astype(BF16)
-            o_all[rows, columns] = dot_nn(prob_b, value).astype(BF16)
-            d_out = d_ctx[rows, :]
-            d_prob = dot_nt(d_out, value)
-            d_score = (prob * (d_prob - jnp.sum(d_prob * prob, axis=-1, keepdims=True)) * scale).astype(BF16)
-            d_qkv[rows, pl.ds(0, dim)] = dot_nn(d_score, key).astype(BF16)
-            return d_key + dot_tn(d_score, query), d_value + dot_tn(prob_b, d_out)
-
-        zeros = jnp.zeros((seq_len, dim), F32)
-        d_key, d_value = lax.fori_loop(0, seq_len // tile, query_tile, (zeros, zeros))
-        d_qkv[:, pl.ds(dim, dim)] = d_key.astype(BF16)
-        d_qkv[:, pl.ds(2 * dim, dim)] = d_value.astype(BF16)
+        query, key, value = (qkv[:, pl.ds(part * dim, dim)] for part in range(3))
+        d_out = d_ctx[...]
+        scores = dot_nt(query, key) * (scale * LOG2_E)
+        grown = jnp.exp2(scores - jnp.max(scores, axis=-1, keepdims=True))
+        prob = grown * (1.0 / jnp.sum(grown, axis=-1, keepdims=True))
+        prob_b = prob.astype(BF16)
+        o_all[:, columns] = dot_nn(prob_b, value).astype(BF16)
+        d_prob = dot_nt(d_out, value)
+        d_score = (prob * (d_prob - jnp.sum(d_prob * prob, axis=-1, keepdims=True)) * scale).astype(BF16)
+        d_qkv[:, pl.ds(0, dim)] = dot_nn(d_score, key).astype(BF16)
+        d_qkv[:, pl.ds(dim, dim)] = dot_nn(query.T, d_score).T.astype(BF16)
+        d_qkv[:, pl.ds(2 * dim, dim)] = dot_nn(d_out.T, prob_b).T.astype(BF16)
 
         def du_tile(part, carry):
             rows = pl.ds(pl.multiple_of(part * tile, tile), tile)

time: 443 us -> 416 us (0.939)
  Pallas kernels: 442 us -> 414 us
    pallas_call x1, Pallas kernels: 207 us -> 180 us  [attention_call(): pl.pallas_call(functools.partial(attention_kernel, dim ** (-0.5)), out_sh...]
where the time goes in v5:
time: 416 us; the launch traced here: 415 us
  Pallas kernels  414 us (100%)
    pallas_call x1, Pallas kernels, mlp_call(): pl.pallas_call(mlp_kernel, out_shape=out_shape, in_specs=[any_spec] * 8,...  213 us
    pallas_call x1, Pallas kernels, attention_call(): pl.pallas_call(functools.partial(attention_kernel, dim ** (-0.5)), out_sh...  180 us
    pallas_call x1, Pallas kernels, finish_call(): pl.pallas_call(finish_kernel, out_shape=out_shape, grid=(seqs,), in_specs...  21.4 us

profile of v5, /device:TPU:112, one launch (start us, length us, event | category | flops | bytes accessed | tf_op | source)
XLA Modules:
  0.0 414.6 jit_solution(10685006363696817880)
XLA Ops:
  0.6 212.8 %feed_forward.1 = (f32[1024,1024]{1,0:T(8,128)}, f32[1024,1024]{1,0:T(8,128)}, bf16[8,2,128,1024]{3,2,1,0:T(8,128)(2,1)}, bf16[6,512,1024]{2,1,0:T(8,128)(2,1)},...) custom-call(f32[1024,1024]{1,0:T(8,128)} %bitcast.17, f32[1024,1024]{1,0:T(8,128)} %bitcast.20, ...), custom_call_target="tpu_custom_call" | custom-call | flops 70000001024 | bytes 67108864 | tf_op jit(solution)/shard_map/feed_forward/pallas_call | solution.py:334
  213.4 179.7 %attention.1 = (f32[512,1024]{1,0:T(8,128)}, f32[512,1024]{1,0:T(8,128)}, bf16[8,128,1024]{2,1,0:T(8,128)(2,1)}, f32[8,128,1024]{2,1,0:T(8,128)}, bf16[8,128,102...) custom-call(bf16[8,2,128,1024]{3,2,1,0:T(8,128)(2,1)} %get-tuple-element.28.uc_seq, ...), custom_call_target="tpu_custom_call" | custom-call | flops 40000000000 | bytes 67108864 | tf_op jit(solution)/shard_map/attention/pallas_call | solution.py:571
  393.1 21.4 %finish.1 = (f32[8,128,1024]{2,1,0:T(8,128)}, f32[8,128,1024]{2,1,0:T(8,128)}, f32[8,128,1024]{2,1,0:T(8,128)}, f32[8,128,1024]{2,1,0:T(8,128)}, f32[1024,512]{1...) custom-call(f32[8,128,1024]{2,1,0:T(8,128)} %y_one.1, ...), custom_call_target="tpu_custom_call" | custom-call | flops 2000000000 | bytes 62914560 | tf_op jit(solution)/shard_map/finish/pallas_call | solution.py:617

commit v6 on v5

--- a/solution.py
+++ b/solution.py
@@ -344,9 +344,9 @@
 
 
 def attention_kernel(
-    scale, uc_seq, att_full, part_near,
-    near_recv, d_att, o_pos, du_pos, wo_full, att_far,
-    uc_all, w_buf, qkv, d_ctx, d_qkv, o_all, du_all, part_send, part_keep, part_core, own_t, far_t, own_f, far_f, o_relay, du_relay, near_buf,
+    scale, uc_seq, att_full, part_own, part_near, up_near,
+    d_up, d_down, d_att, o_pos, du_pos, wo_full, att_far,
+    uc_all, qkv_buf, wo_buf, qkv, d_ctx, d_qkv, o_all, du_all, part_send, part_keep, part_core, own_t, far_t, own_f, far_f, o_relay, du_relay, near_out, near_buf,
     load_sem, w_sem, wo_sem, near_sem, core_send, core_recv, part_out, part_in, far_sem, o_send, o_recv, du_send, du_recv, o_relay_recv, du_relay_recv,
 ):
     ring = Ring()
@@ -355,24 +355,33 @@
     dim = att_full.shape[1] // 4
     tile = 512
 
-    def head_slot(step):
-        return (step // 2 + 1) % 4 * 2 + 1 - step % 2
-
-    def w_load(step, buf):
-        return pltpu.make_async_copy(att_full.at[head_slot(step)], w_buf.at[buf], w_sem.at[buf])
-
-    def w_load_far(step, buf):
-        return pltpu.make_async_copy(att_far.at[1 - step % 2], w_buf.at[buf], w_sem.at[buf])
+    def relation_of(step):
+        return (step + 1) % 4
+
+    def w_loads(heads, buf):
+        copies = []
+        for index, head in enumerate(heads):
+            copies.append(pltpu.make_async_copy(head.at[pl.ds(0, 3 * dim)], qkv_buf.at[buf, pl.ds(index * 3 * dim, 3 * dim)], w_sem.at[buf, index, 0]))
+            copies.append(pltpu.make_async_copy(head.at[pl.ds(3 * dim, dim)], wo_buf.at[buf, pl.ds(index * dim, dim)], w_sem.at[buf, index, 1]))
+        return copies
 
     far_from_t = ring.copy(att_full.at[SAME_F], att_far.at[0], far_sem.at[0], far_sem.at[1], SAME_T)
     far_from_core = ring.copy(att_far.at[0], att_far.at[1], far_sem.at[2], far_sem.at[3], PARTNER)
 
-    near_load = pltpu.make_async_copy(part_near, near_buf, near_sem.at[2])
-    near = ring.copy(near_buf, near_recv, near_sem.at[0], near_sem.at[1], SAME_F)
-
-    def core_copy(step, buf):
-        relation = head_slot(step) // 2
+    near_load = pltpu.make_async_copy(part_near, near_out, near_sem.at[2])
+    near = ring.copy(near_out, near_buf, near_sem.at[0], near_sem.at[1], SAME_F)
+
+    def core_copy(relation, buf):
         return ring.copy(part_send.at[buf], part_core.at[relation], core_send.at[buf], core_recv.at[relation], PARTNER)
+
+    core_last = [core_copy(3, 0), core_copy(0, 1)]
+    rows = part_keep.shape[1]
+    ff_loads = [
+        pltpu.make_async_copy(part_own.at[pl.ds(0, rows)], part_send.at[0], load_sem.at[1, 0]),
+        pltpu.make_async_copy(part_own.at[pl.ds(rows, rows)], part_send.at[1], load_sem.at[1, 1]),
+        pltpu.make_async_copy(up_near, part_core.at[1], load_sem.at[2, 0]),
+    ]
+    ff_stores = [pltpu.make_async_copy(part_send.at[index], dst, load_sem.at[3, index]) for index, dst in enumerate((d_up, d_down))]
 
     rows_a, rows_b = pl.ds(0, 3 * dim), pl.ds(3 * dim, dim)
 
@@ -412,7 +421,7 @@
     loads = [pltpu.make_async_copy(uc_seq.at[slot, which], uc_all.at[which, rows_of(slot)], load_sem.at[slot, which]) for slot in range(8) for which in (0, 1)]
     near_load.start()
     start(loads)
-    w_load(0, 0).start()
+    start(w_loads([att_full.at[3], att_full.at[2]], 0))
     ring.barrier()
     far_from_t.start()
     near_load.wait()
@@ -421,107 +430,111 @@
     for copy in loads:
         copy.wait()
 
-    def head_step(step, carry):
+    def chip_step(step, carry):
         buf = step % 2
-        slot = head_slot(step)
-        relation = slot // 2
-        pltpu.make_async_copy(att_full.at[0], w_buf.at[buf], w_sem.at[buf]).wait()
-
-        @pl.when(step == 3)
+        relation = relation_of(step)
+        for copy in w_loads([att_far.at[0], att_far.at[0]], buf):
+            copy.wait()
+
+        @pl.when(step == 0)
+        def _():
+            start(w_loads([att_full.at[5], att_full.at[4]], 1))
+
+        @pl.when(step == 1)
         def _():
             far_from_core.wait_recv()
-
-        @pl.when((step < 3) | (step == 5) | (step == 6))
-        def _():
-            w_load(step + 1, 1 - buf).start()
-
-        @pl.when((step == 3) | (step == 4))
-        def _():
-            w_load_far(step + 1, 1 - buf).start()
-
-        head = ring.at_traced(slot)
-        columns = pl.ds(pl.multiple_of(head * dim, dim), dim)
-        wo_copy = pltpu.make_async_copy(w_buf.at[buf, pl.ds(3 * dim, dim)], wo_full.at[head], wo_sem.at[0])
-        wo_copy.start()
-        qkv[...] = dot_nt(uc_all[0], w_buf[buf, pl.ds(0, 3 * dim), :]).astype(BF16)
-        d_ctx[...] = dot_nt(uc_all[1], w_buf[buf, pl.ds(3 * dim, dim), :]).astype(BF16)
-
-        query, key, value = (qkv[:, pl.ds(part * dim, dim)] for part in range(3))
-        d_out = d_ctx[...]
-        scores = dot_nt(query, key) * (scale * LOG2_E)
-        grown = jnp.exp2(scores - jnp.max(scores, axis=-1, keepdims=True))
-        prob = grown * (1.0 / jnp.sum(grown, axis=-1, keepdims=True))
-        prob_b = prob.astype(BF16)
-        o_all[:, columns] = dot_nn(prob_b, value).astype(BF16)
-        d_prob = dot_nt(d_out, value)
-        d_score = (prob * (d_prob - jnp.sum(d_prob * prob, axis=-1, keepdims=True)) * scale).astype(BF16)
-        d_qkv[:, pl.ds(0, dim)] = dot_nn(d_score, key).astype(BF16)
-        d_qkv[:, pl.ds(dim, dim)] = dot_nn(query.T, d_score).T.astype(BF16)
-        d_qkv[:, pl.ds(2 * dim, dim)] = dot_nn(d_out.T, prob_b).T.astype(BF16)
+            start(w_loads([att_far.at[1], att_far.at[0]], 0))
+
+        @pl.when(step == 2)
+        def _():
+            start(w_loads([att_full.at[1], att_full.at[0]], 1))
+
+        heads = [ring.at_traced(relation * 2 + other) for other in (1, 0)]
+        wo_copies = [pltpu.make_async_copy(wo_buf.at[buf, pl.ds(index * dim, dim)], wo_full.at[head], wo_sem.at[index]) for index, head in enumerate(heads)]
+        start(wo_copies)
+        qkv[...] = dot_nt(uc_all[0], qkv_buf[buf]).astype(BF16)
+        d_ctx[...] = dot_nt(uc_all[1], wo_buf[buf]).astype(BF16)
+        for index, head in enumerate(heads):
+            columns = pl.ds(pl.multiple_of(head * dim, dim), dim)
+            own = pl.ds(index * 3 * dim, 3 * dim)
+            query, key, value = (qkv[:, pl.ds((index * 3 + part) * dim, dim)] for part in range(3))
+            d_out = d_ctx[:, pl.ds(index * dim, dim)]
+            scores = dot_nt(query, key) * (scale * LOG2_E)
+            grown = jnp.exp2(scores - jnp.max(scores, axis=-1, keepdims=True))
+            prob = grown * (1.0 / jnp.sum(grown, axis=-1, keepdims=True))
+            prob_b = prob.astype(BF16)
+            o_all[:, columns] = dot_nn(prob_b, value).astype(BF16)
+            d_prob = dot_nt(d_out, value)
+            d_score = (prob * (d_prob - jnp.sum(d_prob * prob, axis=-1, keepdims=True)) * scale).astype(BF16)
+            d_qkv[:, pl.ds(index * 3 * dim, dim)] = dot_nn(d_score, key).astype(BF16)
+            d_qkv[:, pl.ds((index * 3 + 1) * dim, dim)] = dot_nn(query.T, d_score).T.astype(BF16)
+            d_qkv[:, pl.ds((index * 3 + 2) * dim, dim)] = dot_nn(d_out.T, prob_b).T.astype(BF16)
+            if index == 0:
+                @pl.when(step >= 2)
+                def _():
+                    core_copy(relation, buf).wait_send()
+
+            dst = part_send.at[buf] if index == 0 else part_keep.at[relation]
+            dst[pl.ds(0, 3 * dim), :] = dot_tn(d_qkv[:, own], uc_all[0])
+            dst[pl.ds(3 * dim, dim), :] = dot_tn(o_all[:, columns], uc_all[1])
+            if index == 0:
+                core_copy(relation, buf).start()
+        core_copy(relation, buf).wait_recv()
+        part_keep[relation] += part_core[relation]
+
+        @pl.when(step == 0)
+        def _():
+            t_own_a.start()
+
+        @pl.when(step == 1)
+        def _():
+            f_own_b.start()
+
+        @pl.when(step == 2)
+        def _():
+            t_far_a.start()
+            f_far_b.start()
 
         def du_tile(part, carry):
             rows = pl.ds(pl.multiple_of(part * tile, tile), tile)
-            du_all[rows, :] += dot_nn(d_qkv[rows, :], w_buf[buf, pl.ds(0, 3 * dim), :])
+            du_all[rows, :] += dot_nn(d_qkv[rows, :], qkv_buf[buf])
             return carry
 
         lax.fori_loop(0, seq_len // tile, du_tile, 0)
 
-        def write_part(dst, index):
-            dst[index, pl.ds(0, 3 * dim), :] = dot_tn(d_qkv[...], uc_all[0])
-            dst[index, pl.ds(3 * dim, dim), :] = dot_tn(o_all[:, columns], uc_all[1])
-
-        @pl.when(step % 2 == 0)
-        def _():
-            send = (step // 2) % 2
-
-            @pl.when(step >= 4)
-            def _():
-                core_copy(step - 4, send).wait_send()
-
-            write_part(part_send, send)
-            core_copy(step, send).start()
-
-        @pl.when(step % 2 == 1)
-        def _():
-            write_part(part_keep, relation)
-            core_copy(step - 1, 0).wait_recv()
-            part_keep[relation] += part_core[relation]
-
-        @pl.when(step == 1)
-        def _():
-            t_own_a.start()
-
-        @pl.when(step == 2)
+        @pl.when(step == 0)
         def _():
             far_from_t.wait_recv()
             far_from_core.start()
 
-        @pl.when(step == 3)
-        def _():
-            f_own_b.start()
-
-        @pl.when(step == 5)
-        def _():
-            t_far_a.start()
-            f_far_b.start()
-
-        wo_copy.wait()
+        for copy in wo_copies:
+            copy.wait()
         return carry
 
-    lax.fori_loop(0, 8, head_step, 0)
+    lax.fori_loop(0, 4, chip_step, 0)
     start(o_out)
     start(du_out)
     o_keep.start()
     du_keep.start()
+    for copy in core_last:
+        copy.wait_send()
+    start(ff_loads)
     f_far_b.wait_recv()
     part_keep[1, rows_b] += far_f[...]
     t_own_b.start()
+    for copy in o_out[:2]:
+        copy.wait_recv()
+    start(o_pass)
     t_far_a.wait_recv()
     part_keep[2, rows_a] += far_t[...]
     f_own_a.start()
-    for copy in o_out[:2]:
-        copy.wait_recv()
-    start(o_pass)
+    for copy in ff_loads:
+        copy.wait()
+    part_send[0] += part_core[1]
+    near.wait_recv()
+    part_send[1] += near_buf[...]
+    for copy in ff_stores:
+        copy.start()
     for copy in du_out[:2]:
         copy.wait_recv()
     start(du_pass)
@@ -537,15 +550,16 @@
     for dst, recv_sem in ((o_pos, o_recv), (du_pos, du_recv)):
         for slot in range(1, 8):
             ring.copy(dst.at[0], dst.at[ring.at(slot)], near_sem.at[0], recv_sem.at[slot], PARTNER).wait_recv()
-    for copy in o_out + du_out + o_pass + du_pass + [t_own_a, t_far_a, t_own_b, f_own_b, f_far_b, f_own_a, far_from_t, far_from_core, near, core_copy(4, 0), core_copy(6, 1)]:
+    for copy in o_out + du_out + o_pass + du_pass + [t_own_a, t_far_a, t_own_b, f_own_b, f_far_b, f_own_a, far_from_t, far_from_core, near]:
         copy.wait_send()
-    near.wait_recv()
+    for copy in ff_stores:
+        copy.wait()
     o_keep.wait()
     du_keep.wait()
     d_att_copy.wait()
 
 
-def attention_call(uc_seq, att_full, part_near):
+def attention_call(uc_seq, att_full, part_own, part_near, up_near):
     slab, hidden = uc_seq.shape[2:]
     rows = att_full.shape[1]
     dim = rows // 4
@@ -553,6 +567,7 @@
     any_spec = pl.BlockSpec(memory_space=pl.ANY)
     dma, vmem = pltpu.SemaphoreType.DMA, pltpu.VMEM
     out_shape = (
+        jax.ShapeDtypeStruct(up_near.shape, F32),
         jax.ShapeDtypeStruct(part_near.shape, F32),
         jax.ShapeDtypeStruct((rows, hidden), F32),
         jax.ShapeDtypeStruct((8, slab, hidden), BF16),
@@ -561,69 +576,74 @@
         jax.ShapeDtypeStruct((2, rows, hidden), BF16),
     )
     scratch = [
-        vmem((2, seq_len, hidden), BF16), vmem((2, rows, hidden), BF16), vmem((seq_len, 3 * dim), BF16), vmem((seq_len, dim), BF16), vmem((seq_len, 3 * dim), BF16),
+        vmem((2, seq_len, hidden), BF16), vmem((2, 6 * dim, hidden), BF16), vmem((2, 2 * dim, hidden), BF16),
+        vmem((seq_len, 6 * dim), BF16), vmem((seq_len, 2 * dim), BF16), vmem((seq_len, 6 * dim), BF16),
         vmem((seq_len, hidden), BF16), vmem((seq_len, hidden), F32),
         vmem((2, rows, hidden), F32), vmem((4, rows, hidden), F32), vmem((4, rows, hidden), F32),
         vmem((rows, hidden), F32), vmem((3 * dim, hidden), F32), vmem((rows, hidden), F32), vmem((dim, hidden), F32),
-        vmem((2, slab, hidden), BF16), vmem((2, slab, hidden), F32), vmem(part_near.shape, F32),
-        dma((8, 2)), dma((2,)), dma((1,)), dma((3,)), dma((2,)), dma((4,)), dma((6,)), dma((6,)), dma((4,)), dma((10,)), dma((8,)), dma((10,)), dma((8,)), dma((2,)), dma((2,)),
+        vmem((2, slab, hidden), BF16), vmem((2, slab, hidden), F32), vmem(part_near.shape, F32), vmem(part_near.shape, F32),
+        dma((8, 2)), dma((2, 2, 2)), dma((2,)), dma((3,)), dma((2,)), dma((4,)), dma((6,)), dma((6,)), dma((4,)), dma((10,)), dma((8,)), dma((10,)), dma((8,)), dma((2,)), dma((2,)),
     ]
     return pl.pallas_call(
         functools.partial(attention_kernel, dim ** -0.5),
         out_shape=out_shape,
-        in_specs=[any_spec] * 3,
-        out_specs=(any_spec,) * 6,
+        in_specs=[any_spec] * 5,
+        out_specs=(any_spec,) * 7,
         scratch_shapes=scratch,
         compiler_params=pltpu.CompilerParams(collective_id=1, has_side_effects=True, vmem_limit_bytes=VMEM_LIMIT),
         cost_estimate=pl.CostEstimate(flops=40 * 10**9, bytes_accessed=64 * 2**20, transcendentals=0),
         name="attention",
-    )(uc_seq, att_full, part_near)
+    )(uc_seq, att_full, part_own, part_near, up_near)
 
 
 def finish_kernel(
-    y_one, o_pos, wo_full, x_two, dx_one, dy_two, du_pos, up_own, up_near, down_own, down_near, d_qkv, d_out,
+    y_one, o_pos, wo_full, x_two, dx_one, dy_two, du_pos, d_up, d_down, d_qkv, d_out,
     x_one_out, x_two_out, dx_one_out, dx_two_out, dw_up, dw_down, dw_qkv, dw_out,
 ):
     x_one_out[0] = y_one[0] - dot_nn(o_pos[0], wo_full[...])
     x_two_out[0] = x_two[...]
     dx_one_out[0] = dx_one[...]
     dx_two_out[0] = dy_two[0] + rms_back(x_two[...], du_pos[0])
-    dw_up[...] = (up_own[...] + up_near[...]).T
-    dw_down[...] = down_own[...] + down_near[...]
-    dim = dw_qkv.shape[2]
-    for part in range(3):
-        dw_qkv[pl.ds(part, dw_qkv.shape[0] // 3, stride=3), 0, :] = d_qkv[pl.ds(part * dim, dim), :].T
+    dw_down[...] = d_down[...]
     dw_out[...] = d_out[...]
 
-
-def finish_call(y_one, o_pos, wo_full, x_two, dx_one, dy_two, du_pos, part_own, up_near, down_near, d_att):
+    @pl.when(pl.program_id(0) % 2 == 0)
+    def _():
+        dim = dw_qkv.shape[2]
+        dw_up[...] = d_up[...].T
+        for part in range(3):
+            dw_qkv[pl.ds(part, dw_qkv.shape[0] // 3, stride=3), 0, :] = d_qkv[pl.ds(part * dim, dim), :].T
+
+
+def finish_call(y_one, o_pos, wo_full, x_two, dx_one, dy_two, du_pos, d_up, d_down, d_att):
     seqs, slab, hidden = y_one.shape
-    ffn = part_own.shape[0] // 2
+    ffn = d_up.shape[0]
     dim = d_att.shape[0] // 4
-    state = pl.BlockSpec((1, slab, hidden), lambda step: (step, 0, 0))
-    flat = pl.BlockSpec((slab, hidden), lambda step: (step, 0))
-    up = pl.BlockSpec((ffn, slab), lambda step: (0, step))
-    rows = ffn // seqs
+    steps = 2 * seqs
+    half = slab // 2
+    state = pl.BlockSpec((1, half, hidden), lambda step: (step // 2, step % 2, 0))
+    flat = pl.BlockSpec((half, hidden), lambda step: (step, 0))
+    rows, out_rows = ffn // steps, dim // steps
     in_specs = [
         state, state, pl.BlockSpec((hidden, hidden), lambda step: (0, 0)), flat, flat, state, state,
-        up, up, pl.BlockSpec((rows, hidden), lambda step: (seqs + step, 0)), pl.BlockSpec((rows, hidden), lambda step: (step, 0)),
-        pl.BlockSpec((3 * dim, slab), lambda step: (0, step)), pl.BlockSpec((dim // seqs, hidden), lambda step: (3 * seqs + step, 0)),
+        pl.BlockSpec((ffn, slab), lambda step: (0, step // 2)), pl.BlockSpec((rows, hidden), lambda step: (step, 0)),
+        pl.BlockSpec((3 * dim, slab), lambda step: (0, step // 2)), pl.BlockSpec((out_rows, hidden), lambda step: (3 * steps + step, 0)),
     ]
     out_specs = [state] * 4 + [
-        pl.BlockSpec((slab, ffn), lambda step: (step, 0)), pl.BlockSpec((rows, hidden), lambda step: (step, 0)),
-        pl.BlockSpec((3 * slab, 1, dim), lambda step: (step, 0, 0)), pl.BlockSpec((dim // seqs, hidden), lambda step: (step, 0)),
+        pl.BlockSpec((slab, ffn), lambda step: (step // 2, 0)), pl.BlockSpec((rows, hidden), lambda step: (step, 0)),
+        pl.BlockSpec((3 * slab, 1, dim), lambda step: (step // 2, 0, 0)), pl.BlockSpec((out_rows, hidden), lambda step: (step, 0)),
     ]
     out_shape = [jax.ShapeDtypeStruct(y_one.shape, F32)] * 4 + [jax.ShapeDtypeStruct(shape, F32) for shape in ((hidden, ffn), (ffn, hidden), (3 * hidden, 1, dim), (dim, hidden))]
     return pl.pallas_call(
         finish_kernel,
         out_shape=out_shape,
-        grid=(seqs,),
+        grid=(steps,),
         in_specs=in_specs,
         out_specs=out_specs,
         compiler_params=pltpu.CompilerParams(dimension_semantics=("arbitrary",), vmem_limit_bytes=VMEM_LIMIT),
         cost_estimate=pl.CostEstimate(flops=2 * 10**9, bytes_accessed=60 * 2**20, transcendentals=0),
         name="finish",
-    )(y_one, o_pos, wo_full, x_two, dx_one, dy_two, du_pos, part_own, up_near, part_own, down_near, d_att, d_att)
+    )(y_one, o_pos, wo_full, x_two, dx_one, dy_two, du_pos, d_up, d_down, d_att, d_att)
 
 
 def local_backward(y_one, y_two, dy_one, dy_two, w_qkv, w_out, w_up, w_down):
@@ -632,9 +652,9 @@
     flat = [tensor.reshape(-1, hidden) for tensor in (y_one, y_two, dy_one, dy_two)]
     qkv_parts = jnp.swapaxes(w_qkv[0, :, 0], 0, 1)
     x_two, dx_one, uc_seq, att_full, part_own, part_near, up_near = mlp_call(*flat, w_up[0], w_down[0], qkv_parts, w_out[0, 0])
-    down_near, d_att, o_pos, du_pos, wo_full, _ = attention_call(uc_seq, att_full, part_near)
+    d_up, d_down, d_att, o_pos, du_pos, wo_full, _ = attention_call(uc_seq, att_full, part_own, part_near, up_near)
     x_one, x_two, dx_one, dx_two, dw_up, dw_down, dw_qkv, dw_out = finish_call(
-        y_one, o_pos, wo_full.reshape(-1, hidden), x_two, dx_one, dy_two, du_pos, part_own, up_near, down_near, d_att
+        y_one, o_pos, wo_full.reshape(-1, hidden), x_two, dx_one, dy_two, du_pos, d_up, d_down, d_att
     )
     return (x_one, x_two, dx_one, dx_two, dw_qkv.reshape(1, hidden, 1, parts, dim), dw_out[None, None], dw_up[None], dw_down[None])
 

time: 416 us -> 420 us (level)
    pallas_call x1, Pallas kernels: 21.4 us -> 28.8 us  [finish_call(): pl.pallas_call(finish_kernel, out_shape=out_shape, grid=(steps,), in_spec...]
where the time goes in v6:
time: 420 us; the launch traced here: 419 us
  Pallas kernels  418 us (100%)
    pallas_call x1, Pallas kernels, mlp_call(): pl.pallas_call(mlp_kernel, out_shape=out_shape, in_specs=[any_spec] * 8,...  213 us
    pallas_call x1, Pallas kernels, attention_call(): pl.pallas_call(functools.partial(attention_kernel, dim ** (-0.5)), out_sh...  176 us
    pallas_call x1, Pallas kernels, finish_call(): pl.pallas_call(finish_kernel, out_shape=out_shape, grid=(steps,), in_spec...  28.8 us

profile of v6, /device:TPU:112, one launch (start us, length us, event | category | flops | bytes accessed | tf_op | source)
XLA Modules:
  0.0 418.7 jit_solution(5527930571156662114)
XLA Ops:
  0.6 212.8 %feed_forward.1 = (f32[1024,1024]{1,0:T(8,128)}, f32[1024,1024]{1,0:T(8,128)}, bf16[8,2,128,1024]{3,2,1,0:T(8,128)(2,1)}, bf16[6,512,1024]{2,1,0:T(8,128)(2,1)},...) custom-call(f32[1024,1024]{1,0:T(8,128)} %bitcast.17, f32[1024,1024]{1,0:T(8,128)} %bitcast.20, ...), custom_call_target="tpu_custom_call" | custom-call | flops 70000001024 | bytes 67108864 | tf_op jit(solution)/shard_map/feed_forward/pallas_call | solution.py:334
  213.4 176.3 %attention.1 = (f32[512,1024]{1,0:T(8,128)}, f32[512,1024]{1,0:T(8,128)}, f32[512,1024]{1,0:T(8,128)}, bf16[8,128,1024]{2,1,0:T(8,128)(2,1)}, f32[8,128,1024]{2,...) custom-call(bf16[8,2,128,1024]{3,2,1,0:T(8,128)(2,1)} %get-tuple-element.29.uc_seq, ...), custom_call_target="tpu_custom_call" | custom-call | flops 40000000000 | bytes 67108864 | tf_op jit(solution)/shard_map/attention/pallas_call | solution.py:587
  389.7 28.8 %finish.1 = (f32[8,128,1024]{2,1,0:T(8,128)}, f32[8,128,1024]{2,1,0:T(8,128)}, f32[8,128,1024]{2,1,0:T(8,128)}, f32[8,128,1024]{2,1,0:T(8,128)}, f32[1024,512]{1...) custom-call(f32[8,128,1024]{2,1,0:T(8,128)} %y_one.1, ...), custom_call_target="tpu_custom_call" | custom-call | flops 2000000000 | bytes 62914560 | tf_op jit(solution)/shard_map/finish/pallas_call | solution.py:637

commit v7 on v6

--- a/solution.py
+++ b/solution.py
@@ -597,53 +597,96 @@
 
 
 def finish_kernel(
-    y_one, o_pos, wo_full, x_two, dx_one, dy_two, du_pos, d_up, d_down, d_qkv, d_out,
+    y_one, o_pos, wo_full, x_two, dx_one, dy_two, du_pos, d_up, d_down, d_att,
     x_one_out, x_two_out, dx_one_out, dx_two_out, dw_up, dw_down, dw_qkv, dw_out,
+    y_buf, o_buf, wo_buf, x_buf, dx_buf, dy_buf, du_buf, up_buf, down_buf, att_buf, up_out, qkv_out, load_sem, store_sem,
 ):
-    x_one_out[0] = y_one[0] - dot_nn(o_pos[0], wo_full[...])
-    x_two_out[0] = x_two[...]
-    dx_one_out[0] = dx_one[...]
-    dx_two_out[0] = dy_two[0] + rms_back(x_two[...], du_pos[0])
-    dw_down[...] = d_down[...]
-    dw_out[...] = d_out[...]
-
-    @pl.when(pl.program_id(0) % 2 == 0)
-    def _():
-        dim = dw_qkv.shape[2]
-        dw_up[...] = d_up[...].T
-        for part in range(3):
-            dw_qkv[pl.ds(part, dw_qkv.shape[0] // 3, stride=3), 0, :] = d_qkv[pl.ds(part * dim, dim), :].T
+    tokens = y_buf.shape[0]
+    dim = wo_buf.shape[0] // 8
+    chunk = 256
+    chunks = [pl.ds(index * chunk, chunk) for index in range(tokens // chunk)]
+
+    def pieces(src, dst, sem, row):
+        return [pltpu.make_async_copy(src.at[rows], dst.at[rows], sem.at[row, index]) for index, rows in enumerate(chunks)]
+
+    def whole(src, dst, sem, row):
+        return pltpu.make_async_copy(src, dst, sem.at[row, 0])
+
+    x_in, dy_in, du_in = pieces(x_two, x_buf, load_sem, 0), pieces(dy_two, dy_buf, load_sem, 1), pieces(du_pos, du_buf, load_sem, 2)
+    y_in, o_in = pieces(y_one, y_buf, load_sem, 3), pieces(o_pos, o_buf, load_sem, 4)
+    wo_in, dx_in = whole(wo_full, wo_buf, load_sem, 5), whole(dx_one, dx_buf, load_sem, 6)
+    up_in, down_in, att_in = whole(d_up, up_buf, load_sem, 7), whole(d_down, down_buf, load_sem, 8), whole(d_att, att_buf, load_sem, 9)
+    for group in zip(x_in, dy_in, du_in):
+        for copy in group:
+            copy.start()
+    for copy in (dx_in, wo_in):
+        copy.start()
+    for group in zip(y_in, o_in):
+        for copy in group:
+            copy.start()
+    for copy in (up_in, att_in, down_in):
+        copy.start()
+
+    x_store, dx2_store, x1_store = pieces(x_buf, x_two_out, store_sem, 0), pieces(dy_buf, dx_two_out, store_sem, 1), pieces(y_buf, x_one_out, store_sem, 2)
+    for index, rows in enumerate(chunks):
+        x_in[index].wait()
+        x_store[index].start()
+        dy_in[index].wait()
+        du_in[index].wait()
+        dy_buf[rows, :] += rms_back(x_buf[rows, :], du_buf[rows, :])
+        dx2_store[index].start()
+    dx_in.wait()
+    dx_store = whole(dx_buf, dx_one_out, store_sem, 3)
+    dx_store.start()
+    wo_in.wait()
+    for index, rows in enumerate(chunks):
+        y_in[index].wait()
+        o_in[index].wait()
+        y_buf[rows, :] -= dot_nn(o_buf[rows, :], wo_buf[...])
+        x1_store[index].start()
+    up_in.wait()
+    ffn = up_buf.shape[0]
+    for part in range(up_out.shape[0] // ffn):
+        up_out[pl.ds(part * ffn, ffn), :] = up_buf[:, pl.ds(part * ffn, ffn)].T
+    up_store = whole(up_out, dw_up, store_sem, 4)
+    up_store.start()
+    att_in.wait()
+    for part in range(3):
+        qkv_out[pl.ds(part, tokens, stride=3), 0, :] = att_buf[pl.ds(part * dim, dim), :].T
+    qkv_store = whole(qkv_out, dw_qkv, store_sem, 5)
+    qkv_store.start()
+    out_store = whole(att_buf.at[pl.ds(3 * dim, dim)], dw_out, store_sem, 6)
+    out_store.start()
+    down_in.wait()
+    down_store = whole(down_buf, dw_down, store_sem, 7)
+    down_store.start()
+    for copy in x_store + dx2_store + x1_store + [dx_store, up_store, qkv_store, out_store, down_store]:
+        copy.wait()
 
 
 def finish_call(y_one, o_pos, wo_full, x_two, dx_one, dy_two, du_pos, d_up, d_down, d_att):
-    seqs, slab, hidden = y_one.shape
+    tokens, hidden = y_one.shape
     ffn = d_up.shape[0]
     dim = d_att.shape[0] // 4
-    steps = 2 * seqs
-    half = slab // 2
-    state = pl.BlockSpec((1, half, hidden), lambda step: (step // 2, step % 2, 0))
-    flat = pl.BlockSpec((half, hidden), lambda step: (step, 0))
-    rows, out_rows = ffn // steps, dim // steps
-    in_specs = [
-        state, state, pl.BlockSpec((hidden, hidden), lambda step: (0, 0)), flat, flat, state, state,
-        pl.BlockSpec((ffn, slab), lambda step: (0, step // 2)), pl.BlockSpec((rows, hidden), lambda step: (step, 0)),
-        pl.BlockSpec((3 * dim, slab), lambda step: (0, step // 2)), pl.BlockSpec((out_rows, hidden), lambda step: (3 * steps + step, 0)),
+    any_spec = pl.BlockSpec(memory_space=pl.ANY)
+    dma, vmem = pltpu.SemaphoreType.DMA, pltpu.VMEM
+    state = (tokens, hidden)
+    out_shape = [jax.ShapeDtypeStruct(shape, F32) for shape in (state, state, state, state, (hidden, ffn), (ffn, hidden), (3 * hidden, 1, dim), (dim, hidden))]
+    scratch = [
+        vmem(state, F32), vmem(state, BF16), vmem((hidden, hidden), BF16), vmem(state, F32), vmem(state, F32), vmem(state, F32), vmem(state, F32),
+        vmem((ffn, hidden), F32), vmem((ffn, hidden), F32), vmem(d_att.shape, F32), vmem((hidden, ffn), F32), vmem((3 * hidden, 1, dim), F32),
+        dma((10, 4)), dma((8, 4)),
     ]
-    out_specs = [state] * 4 + [
-        pl.BlockSpec((slab, ffn), lambda step: (step // 2, 0)), pl.BlockSpec((rows, hidden), lambda step: (step, 0)),
-        pl.BlockSpec((3 * slab, 1, dim), lambda step: (step // 2, 0, 0)), pl.BlockSpec((out_rows, hidden), lambda step: (step, 0)),
-    ]
-    out_shape = [jax.ShapeDtypeStruct(y_one.shape, F32)] * 4 + [jax.ShapeDtypeStruct(shape, F32) for shape in ((hidden, ffn), (ffn, hidden), (3 * hidden, 1, dim), (dim, hidden))]
     return pl.pallas_call(
         finish_kernel,
         out_shape=out_shape,
-        grid=(steps,),
-        in_specs=in_specs,
-        out_specs=out_specs,
-        compiler_params=pltpu.CompilerParams(dimension_semantics=("arbitrary",), vmem_limit_bytes=VMEM_LIMIT),
-        cost_estimate=pl.CostEstimate(flops=2 * 10**9, bytes_accessed=60 * 2**20, transcendentals=0),
+        in_specs=[any_spec] * 10,
+        out_specs=[any_spec] * 8,
+        scratch_shapes=scratch,
+        compiler_params=pltpu.CompilerParams(vmem_limit_bytes=VMEM_LIMIT),
+        cost_estimate=pl.CostEstimate(flops=2 * 10**9, bytes_accessed=52 * 2**20, transcendentals=0),
         name="finish",
-    )(y_one, o_pos, wo_full, x_two, dx_one, dy_two, du_pos, d_up, d_down, d_att, d_att)
+    )(y_one, o_pos, wo_full, x_two, dx_one, dy_two, du_pos, d_up, d_down, d_att)
 
 
 def local_backward(y_one, y_two, dy_one, dy_two, w_qkv, w_out, w_up, w_down):
@@ -653,10 +696,12 @@
     qkv_parts = jnp.swapaxes(w_qkv[0, :, 0], 0, 1)
     x_two, dx_one, uc_seq, att_full, part_own, part_near, up_near = mlp_call(*flat, w_up[0], w_down[0], qkv_parts, w_out[0, 0])
     d_up, d_down, d_att, o_pos, du_pos, wo_full, _ = attention_call(uc_seq, att_full, part_own, part_near, up_near)
-    x_one, x_two, dx_one, dx_two, dw_up, dw_down, dw_qkv, dw_out = finish_call(
-        y_one, o_pos, wo_full.reshape(-1, hidden), x_two, dx_one, dy_two, du_pos, d_up, d_down, d_att
+    tokens = flat[0].shape
+    *states, dw_up, dw_down, dw_qkv, dw_out = finish_call(
+        flat[0], o_pos.reshape(tokens), wo_full.reshape(-1, hidden), x_two, dx_one, flat[3], du_pos.reshape(tokens), d_up, d_down, d_att
     )
-    return (x_one, x_two, dx_one, dx_two, dw_qkv.reshape(1, hidden, 1, parts, dim), dw_out[None, None], dw_up[None], dw_down[None])
+    states = [tensor.reshape(y_one.shape) for tensor in states]
+    return (*states, dw_qkv.reshape(1, hidden, 1, parts, dim), dw_out[None, None], dw_up[None], dw_down[None])
 
 
 def solution(mesh):

time: 420 us -> 410 us (0.976)
  Pallas kernels: 418 us -> 408 us
    pallas_call x1, Pallas kernels: 28.8 us -> 18.8 us  [finish_call(): pl.pallas_call(finish_kernel, out_shape=out_shape, in_specs=[any_spec] *...]
where the time goes in v7:
time: 410 us; the launch traced here: 409 us
  Pallas kernels  408 us (100%)
    pallas_call x1, Pallas kernels, mlp_call(): pl.pallas_call(mlp_kernel, out_shape=out_shape, in_specs=[any_spec] * 8,...  213 us
    pallas_call x1, Pallas kernels, attention_call(): pl.pallas_call(functools.partial(attention_kernel, dim ** (-0.5)), out_sh...  176 us
    pallas_call x1, Pallas kernels, finish_call(): pl.pallas_call(finish_kernel, out_shape=out_shape, in_specs=[any_spec] *...  18.8 us

profile of v7, /device:TPU:112, one launch (start us, length us, event | category | flops | bytes accessed | tf_op | source)
XLA Modules:
  0.0 408.7 jit_solution(3812541973816084856)
XLA Ops:
  0.6 212.8 %feed_forward.1 = (f32[1024,1024]{1,0:T(8,128)}, f32[1024,1024]{1,0:T(8,128)}, bf16[8,2,128,1024]{3,2,1,0:T(8,128)(2,1)}, bf16[6,512,1024]{2,1,0:T(8,128)(2,1)},...) custom-call(f32[1024,1024]{1,0:T(8,128)} %bitcast.23, f32[1024,1024]{1,0:T(8,128)} %bitcast.30, ...), custom_call_target="tpu_custom_call" | custom-call | flops 70000001024 | bytes 67108864 | tf_op jit(solution)/shard_map/feed_forward/pallas_call | solution.py:334
  213.4 176.3 %attention.1 = (f32[512,1024]{1,0:T(8,128)}, f32[512,1024]{1,0:T(8,128)}, f32[512,1024]{1,0:T(8,128)}, bf16[8,128,1024]{2,1,0:T(8,128)(2,1)}, f32[8,128,1024]{2,...) custom-call(bf16[8,2,128,1024]{3,2,1,0:T(8,128)(2,1)} %get-tuple-element.29.uc_seq, ...), custom_call_target="tpu_custom_call" | custom-call | flops 40000000000 | bytes 67108864 | tf_op jit(solution)/shard_map/attention/pallas_call | solution.py:587
  389.7 18.8 %finish.1 = (f32[1024,1024]{1,0:T(8,128)}, f32[1024,1024]{1,0:T(8,128)}, f32[1024,1024]{1,0:T(8,128)}, f32[1024,1024]{1,0:T(8,128)}, f32[1024,512]{1,0:T(8,128)}...) custom-call(f32[1024,1024]{1,0:T(8,128)} %bitcast.24, bf16[1024,1024]{1,0:T(8,128)(2,1)} %bitcast.28, ...), custom_call_target="tpu_custom_call" | custom-call | flops 2000000000 | bytes 54525952 | tf_op jit(solution)/shard_map/finish/pallas_call | solution.py:680

commit v8 on v7

--- a/solution.py
+++ b/solution.py
@@ -345,8 +345,8 @@
 
 def attention_kernel(
     scale, uc_seq, att_full, part_own, part_near, up_near,
-    d_up, d_down, d_att, o_pos, du_pos, wo_full, att_far,
-    uc_all, qkv_buf, wo_buf, qkv, d_ctx, d_qkv, o_all, du_all, part_send, part_keep, part_core, own_t, far_t, own_f, far_f, o_relay, du_relay, near_out, near_buf,
+    d_up, d_down, d_att, o_pos, du_pos, wo_full, att_far, du_relay,
+    uc_all, qkv_buf, wo_buf, qkv, d_ctx, d_qkv, o_all, du_all, part_send, part_keep, part_core, own_t, far_t, own_f, far_f, o_relay, near_out, near_buf,
     load_sem, w_sem, wo_sem, near_sem, core_send, core_recv, part_out, part_in, far_sem, o_send, o_recv, du_send, du_recv, o_relay_recv, du_relay_recv,
 ):
     ring = Ring()
@@ -412,7 +412,7 @@
         return out, onward, keep
 
     o_out, o_pass, o_keep = to_positions(o_all, o_pos, o_relay, o_send, o_recv, o_relay_recv)
-    du_out, du_pass, du_keep = to_positions(du_all, du_pos, du_relay, du_send, du_recv, du_relay_recv)
+    du_out, _, du_keep = to_positions(du_all, du_pos, du_relay, du_send, du_recv, du_relay_recv)
 
     def start(copies):
         for copy in copies:
@@ -535,9 +535,6 @@
     part_send[1] += near_buf[...]
     for copy in ff_stores:
         copy.start()
-    for copy in du_out[:2]:
-        copy.wait_recv()
-    start(du_pass)
     t_own_a.wait_recv()
     t_own_b.wait_recv()
     part_keep[0] += own_t[...]
@@ -547,10 +544,12 @@
     d_att_copy = pltpu.make_async_copy(part_keep.at[0], d_att, load_sem.at[0, 0])
     d_att_copy.start()
 
-    for dst, recv_sem in ((o_pos, o_recv), (du_pos, du_recv)):
-        for slot in range(1, 8):
+    for copy in du_out[:2]:
+        copy.wait_recv()
+    for dst, recv_sem, slots in ((o_pos, o_recv, range(1, 8)), (du_pos, du_recv, range(1, 6))):
+        for slot in slots:
             ring.copy(dst.at[0], dst.at[ring.at(slot)], near_sem.at[0], recv_sem.at[slot], PARTNER).wait_recv()
-    for copy in o_out + du_out + o_pass + du_pass + [t_own_a, t_far_a, t_own_b, f_own_b, f_far_b, f_own_a, far_from_t, far_from_core, near]:
+    for copy in o_out + du_out + o_pass + [t_own_a, t_far_a, t_own_b, f_own_b, f_far_b, f_own_a, far_from_t, far_from_core, near]:
         copy.wait_send()
     for copy in ff_stores:
         copy.wait()
@@ -574,6 +573,7 @@
         jax.ShapeDtypeStruct((8, slab, hidden), F32),
         jax.ShapeDtypeStruct((8, dim, hidden), BF16),
         jax.ShapeDtypeStruct((2, rows, hidden), BF16),
+        jax.ShapeDtypeStruct((2, slab, hidden), F32),
     )
     scratch = [
         vmem((2, seq_len, hidden), BF16), vmem((2, 6 * dim, hidden), BF16), vmem((2, 2 * dim, hidden), BF16),
@@ -581,14 +581,14 @@
         vmem((seq_len, hidden), BF16), vmem((seq_len, hidden), F32),
         vmem((2, rows, hidden), F32), vmem((4, rows, hidden), F32), vmem((4, rows, hidden), F32),
         vmem((rows, hidden), F32), vmem((3 * dim, hidden), F32), vmem((rows, hidden), F32), vmem((dim, hidden), F32),
-        vmem((2, slab, hidden), BF16), vmem((2, slab, hidden), F32), vmem(part_near.shape, F32), vmem(part_near.shape, F32),
+        vmem((2, slab, hidden), BF16), vmem(part_near.shape, F32), vmem(part_near.shape, F32),
         dma((8, 2)), dma((2, 2, 2)), dma((2,)), dma((3,)), dma((2,)), dma((4,)), dma((6,)), dma((6,)), dma((4,)), dma((10,)), dma((8,)), dma((10,)), dma((8,)), dma((2,)), dma((2,)),
     ]
     return pl.pallas_call(
         functools.partial(attention_kernel, dim ** -0.5),
         out_shape=out_shape,
         in_specs=[any_spec] * 5,
-        out_specs=(any_spec,) * 7,
+        out_specs=(any_spec,) * 8,
         scratch_shapes=scratch,
         compiler_params=pltpu.CompilerParams(collective_id=1, has_side_effects=True, vmem_limit_bytes=VMEM_LIMIT),
         cost_estimate=pl.CostEstimate(flops=40 * 10**9, bytes_accessed=64 * 2**20, transcendentals=0),
@@ -612,11 +612,18 @@
     def whole(src, dst, sem, row):
         return pltpu.make_async_copy(src, dst, sem.at[row, 0])
 
-    x_in, dy_in, du_in = pieces(x_two, x_buf, load_sem, 0), pieces(dy_two, dy_buf, load_sem, 1), pieces(du_pos, du_buf, load_sem, 2)
+    ring = Ring()
+    slab = tokens // 8
+    slots = [pl.ds(pl.multiple_of(ring.at(slot) * slab, slab), slab) for slot in range(6)]
+
+    def slabs(src, dst, sem, row):
+        return [pltpu.make_async_copy(src.at[rows], dst.at[rows], sem.at[row, index]) for index, rows in enumerate(slots)]
+
+    x_in, dy_in, du_in = pieces(x_two, x_buf, load_sem, 0), slabs(dy_two, dy_buf, load_sem, 1), slabs(du_pos, du_buf, load_sem, 2)
     y_in, o_in = pieces(y_one, y_buf, load_sem, 3), pieces(o_pos, o_buf, load_sem, 4)
     wo_in, dx_in = whole(wo_full, wo_buf, load_sem, 5), whole(dx_one, dx_buf, load_sem, 6)
     up_in, down_in, att_in = whole(d_up, up_buf, load_sem, 7), whole(d_down, down_buf, load_sem, 8), whole(d_att, att_buf, load_sem, 9)
-    for group in zip(x_in, dy_in, du_in):
+    for group in (x_in, *zip(dy_in, du_in)):
         for copy in group:
             copy.start()
     for copy in (dx_in, wo_in):
@@ -627,10 +634,11 @@
     for copy in (up_in, att_in, down_in):
         copy.start()
 
-    x_store, dx2_store, x1_store = pieces(x_buf, x_two_out, store_sem, 0), pieces(dy_buf, dx_two_out, store_sem, 1), pieces(y_buf, x_one_out, store_sem, 2)
-    for index, rows in enumerate(chunks):
+    x_store, dx2_store, x1_store = pieces(x_buf, x_two_out, store_sem, 0), slabs(dy_buf, dx_two_out, store_sem, 1), pieces(y_buf, x_one_out, store_sem, 2)
+    for index in range(len(chunks)):
         x_in[index].wait()
         x_store[index].start()
+    for index, rows in enumerate(slots):
         dy_in[index].wait()
         du_in[index].wait()
         dy_buf[rows, :] += rms_back(x_buf[rows, :], du_buf[rows, :])
@@ -675,7 +683,7 @@
     scratch = [
         vmem(state, F32), vmem(state, BF16), vmem((hidden, hidden), BF16), vmem(state, F32), vmem(state, F32), vmem(state, F32), vmem(state, F32),
         vmem((ffn, hidden), F32), vmem((ffn, hidden), F32), vmem(d_att.shape, F32), vmem((hidden, ffn), F32), vmem((3 * hidden, 1, dim), F32),
-        dma((10, 4)), dma((8, 4)),
+        dma((10, 6)), dma((8, 6)),
     ]
     return pl.pallas_call(
         finish_kernel,
@@ -689,17 +697,59 @@
     )(y_one, o_pos, wo_full, x_two, dx_one, dy_two, du_pos, d_up, d_down, d_att)
 
 
+def last_kernel(x_two, dy_two, du_far, du_far_other, dx_two_in, dx_two_out, x_buf, dy_buf, du_buf, load_sem, store_sem):
+    ring = Ring()
+    slab = du_far.shape[0]
+    loads, stores = [], []
+    for index, (slot, du) in enumerate(((SAME_O, du_far), (OTHER_O, du_far_other))):
+        rows = pl.ds(pl.multiple_of(ring.at(slot) * slab, slab), slab)
+        sources = ((x_two.at[rows], x_buf), (dy_two.at[rows], dy_buf), (du, du_buf))
+        loads.append([pltpu.make_async_copy(src, dst.at[index], load_sem.at[index, which]) for which, (src, dst) in enumerate(sources)])
+        stores.append(pltpu.make_async_copy(dy_buf.at[index], dx_two_out.at[rows], store_sem.at[index]))
+    for copies in loads:
+        for copy in copies:
+            copy.start()
+    for index, copies in enumerate(loads):
+        for copy in copies:
+            copy.wait()
+        dy_buf[index] += rms_back(x_buf[index], du_buf[index])
+        stores[index].start()
+    for copy in stores:
+        copy.wait()
+
+
+def last_call(x_two, dy_two, du_far, du_far_other, dx_two):
+    slab, hidden = du_far.shape
+    any_spec = pl.BlockSpec(memory_space=pl.ANY)
+    buf = pltpu.VMEM((2, slab, hidden), F32)
+    return pl.pallas_call(
+        last_kernel,
+        out_shape=jax.ShapeDtypeStruct(dx_two.shape, F32),
+        in_specs=[any_spec] * 5,
+        out_specs=any_spec,
+        input_output_aliases={4: 0},
+        scratch_shapes=[buf, buf, buf, pltpu.SemaphoreType.DMA((2, 3)), pltpu.SemaphoreType.DMA((2,))],
+        cost_estimate=pl.CostEstimate(flops=10**6, bytes_accessed=4 * 2**20, transcendentals=0),
+        name="last",
+    )(x_two, dy_two, du_far, du_far_other, dx_two)
+
+
 def local_backward(y_one, y_two, dy_one, dy_two, w_qkv, w_out, w_up, w_down):
     hidden = y_one.shape[2]
     _, _, _, parts, dim = w_qkv.shape
     flat = [tensor.reshape(-1, hidden) for tensor in (y_one, y_two, dy_one, dy_two)]
     qkv_parts = jnp.swapaxes(w_qkv[0, :, 0], 0, 1)
     x_two, dx_one, uc_seq, att_full, part_own, part_near, up_near = mlp_call(*flat, w_up[0], w_down[0], qkv_parts, w_out[0, 0])
-    d_up, d_down, d_att, o_pos, du_pos, wo_full, _ = attention_call(uc_seq, att_full, part_own, part_near, up_near)
+    d_up, d_down, d_att, o_pos, du_pos, wo_full, _, du_relay = attention_call(uc_seq, att_full, part_own, part_near, up_near)
+    devices = range(lax.axis_size("tp"))
+    to_f = [(device, (3 - device // 2) * 2 + device % 2) for device in devices]
+    to_other_t = [(device, 4 * (device // 4) + 3 - device % 4) for device in devices]
+    du_far, du_far_other = lax.ppermute(du_relay[0], "tp", to_f), lax.ppermute(du_relay[1], "tp", to_other_t)
     tokens = flat[0].shape
     *states, dw_up, dw_down, dw_qkv, dw_out = finish_call(
         flat[0], o_pos.reshape(tokens), wo_full.reshape(-1, hidden), x_two, dx_one, flat[3], du_pos.reshape(tokens), d_up, d_down, d_att
     )
+    states[3] = last_call(x_two, flat[3], du_far, du_far_other, states[3])
     states = [tensor.reshape(y_one.shape) for tensor in states]
     return (*states, dw_qkv.reshape(1, hidden, 1, parts, dim), dw_out[None, None], dw_up[None], dw_down[None])
 

time: 410 us -> 407 us (level)
  Pallas kernels: 408 us -> 400 us
    pallas_call x1, Pallas kernels: 176 us -> 167 us  [attention_call(): pl.pallas_call(functools.partial(attention_kernel, dim ** (-0.5)), out_sh...]
  transfers between devices with their start and end apart: 0 -> 2, of which waited for: 0 -> 0; matrix products, arithmetic and copies ran while one was open for 0% -> 0% of each run, Pallas kernels for 0% -> 4%
where the time goes in v8:
time: 407 us; the launch traced here: 406 us
  Pallas kernels  400 us (98%)
    pallas_call x1, Pallas kernels, mlp_call(): pl.pallas_call(mlp_kernel, out_shape=out_shape, in_specs=[any_spec] * 8,...  213 us
    pallas_call x1, Pallas kernels, attention_call(): pl.pallas_call(functools.partial(attention_kernel, dim ** (-0.5)), out_sh...  167 us
    pallas_call x1, Pallas kernels, finish_call(): pl.pallas_call(finish_kernel, out_shape=out_shape, in_specs=[any_spec] *...  18.2 us
  transfers between devices with their start and end apart: 2, of which 0 were waited for; matrix products, arithmetic and copies ran while one was open for 0% of the time, Pallas kernels for 4%

profile of v8, /device:TPU:112, one launch (start us, length us, event | category | flops | bytes accessed | tf_op | source)
XLA Modules:
  0.0 406.3 jit_solution(14134727803760911440)
XLA Ops:
  0.6 212.8 %feed_forward.1 = (f32[1024,1024]{1,0:T(8,128)}, f32[1024,1024]{1,0:T(8,128)}, bf16[8,2,128,1024]{3,2,1,0:T(8,128)(2,1)}, bf16[6,512,1024]{2,1,0:T(8,128)(2,1)},...) custom-call(f32[1024,1024]{1,0:T(8,128)} %bitcast.30, f32[1024,1024]{1,0:T(8,128)} %bitcast.36, ...), custom_call_target="tpu_custom_call" | custom-call | flops 70000001024 | bytes 67108864 | tf_op jit(solution)/shard_map/feed_forward/pallas_call | solution.py:334
  213.4 166.5 %attention.1 = (f32[512,1024]{1,0:T(8,128)}, f32[512,1024]{1,0:T(8,128)}, f32[512,1024]{1,0:T(8,128)}, bf16[8,128,1024]{2,1,0:T(8,128)(2,1)}, f32[8,128,1024]{2,...) custom-call(bf16[8,2,128,1024]{3,2,1,0:T(8,128)(2,1)} %get-tuple-element.30.uc_s, ...), custom_call_target="tpu_custom_call" | custom-call | flops 40000000000 | bytes 67108864 | tf_op jit(solution)/shard_map/attention/pallas_call | solution.py:587
  379.9 2.3 slice_bitcast_fusion
  382.2 0.9 collective-permute-start.1
  383.1 1.9 collective-permute-start
  385.0 18.2 %finish.1 = (f32[1024,1024]{1,0:T(8,128)}, f32[1024,1024]{1,0:T(8,128)}, f32[1024,1024]{1,0:T(8,128)}, f32[1024,1024]{1,0:T(8,128)}, f32[1024,512]{1,0:T(8,128)}...) custom-call(f32[1024,1024]{1,0:T(8,128)} %bitcast.31, bf16[1024,1024]{1,0:T(8,128)(2,1)} %bitcast.34, ...), custom_call_target="tpu_custom_call" | custom-call | flops 2000000000 | bytes 54525952 | tf_op jit(solution)/shard_map/finish/pallas_call | solution.py:688
  403.2 0.0 collective-permute-done.1.du_far_other
  403.2 0.0 collective-permute-done.du_far
  403.2 2.9 last.1
Async XLA Ops:
  382.2 21.0 %collective-permute-start.1 = (f32[128,1024]{1,0:T(8,128)}, f32[128,1024]{1,0:T(8,128)}, u32[]{:S(2)}, u32[]{:S(2)}) collective-permute-start(f32[128,1024]{1,0:T(8,128)} %get-tuple-element.60), channel_id=1, source_target_pairs={{0,3},{1,2},{2,1},{3,0},{4,7},{5,6},{6,5},{7,4},{8,11},{9,10},{10,... | collective-permute-start | bytes 1572872 | tf_op jit(solution)/shard_map/ppermute | solution.py:747
  383.1 20.1 %collective-permute-start = (f32[128,1024]{1,0:T(8,128)}, f32[128,1024]{1,0:T(8,128)}, u32[]{:S(2)}, u32[]{:S(2)}) collective-permute-start(f32[128,1024]{1,0:T(8,128)} %get-tuple-element.61), channel_id=1, source_target_pairs={{0,6},{1,7},{2,4},{3,5},{4,2},{5,3},{6,0},{7,1},{8,14},{9,15},{10,... | collective-permute-start | bytes 1572872 | tf_op jit(solution)/shard_map/ppermute | solution.py:747

commit v9 on v8

--- a/solution.py
+++ b/solution.py
@@ -345,7 +345,7 @@
 
 def attention_kernel(
     scale, uc_seq, att_full, part_own, part_near, up_near,
-    d_up, d_down, d_att, o_pos, du_pos, wo_full, att_far, du_relay,
+    d_up, d_down, d_att, o_pos, du_pos, wo_full, att_far, to_f, to_other_t,
     uc_all, qkv_buf, wo_buf, qkv, d_ctx, d_qkv, o_all, du_all, part_send, part_keep, part_core, own_t, far_t, own_f, far_f, o_relay, near_out, near_buf,
     load_sem, w_sem, wo_sem, near_sem, core_send, core_recv, part_out, part_in, far_sem, o_send, o_recv, du_send, du_recv, o_relay_recv, du_relay_recv,
 ):
@@ -412,7 +412,18 @@
         return out, onward, keep
 
     o_out, o_pass, o_keep = to_positions(o_all, o_pos, o_relay, o_send, o_recv, o_relay_recv)
-    du_out, _, du_keep = to_positions(du_all, du_pos, du_relay, du_send, du_recv, du_relay_recv)
+    late = slab - to_f.shape[0] % slab
+    du_rows = {slot: rows_of(slot) for slot in range(1, 8)}
+    du_rows[SAME_F], du_rows[OTHER_T] = pl.ds(SAME_F * slab, late), pl.ds(OTHER_T * slab, late)
+    du_out = [
+        ring.copy(du_all.at[rows_of(SAME_O)], to_f.at[pl.ds(0, slab)], du_send.at[6], du_relay_recv.at[0], SAME_T),
+        ring.copy(du_all.at[rows_of(OTHER_O)], to_other_t.at[pl.ds(0, slab)], du_send.at[7], du_relay_recv.at[1], SAME_F),
+    ] + [ring.copy(du_all.at[du_rows[slot]], du_pos.at[ring.me, pl.ds(0, du_rows[slot].size)], du_send.at[slot], du_recv.at[slot], slot) for slot in (5, 4, 3, 2, 1)]
+    du_keep = pltpu.make_async_copy(du_all.at[rows_of(0)], du_pos.at[ring.me], du_send.at[0])
+    du_late = [
+        pltpu.make_async_copy(du_all.at[pl.ds(slot * slab + late, slab - late)], dst.at[pl.ds(slab, slab - late)], du_send.at[sem])
+        for slot, dst, sem in ((SAME_F, to_f, 8), (OTHER_T, to_other_t, 9))
+    ]
 
     def start(copies):
         for copy in copies:
@@ -514,6 +525,7 @@
     lax.fori_loop(0, 4, chip_step, 0)
     start(o_out)
     start(du_out)
+    start(du_late)
     o_keep.start()
     du_keep.start()
     for copy in core_last:
@@ -546,9 +558,12 @@
 
     for copy in du_out[:2]:
         copy.wait_recv()
-    for dst, recv_sem, slots in ((o_pos, o_recv, range(1, 8)), (du_pos, du_recv, range(1, 6))):
-        for slot in slots:
-            ring.copy(dst.at[0], dst.at[ring.at(slot)], near_sem.at[0], recv_sem.at[slot], PARTNER).wait_recv()
+    for slot in range(1, 8):
+        ring.copy(o_pos.at[0], o_pos.at[ring.at(slot)], near_sem.at[0], o_recv.at[slot], PARTNER).wait_recv()
+    for copy in du_out[2:]:
+        copy.wait_recv()
+    for copy in du_late:
+        copy.wait()
     for copy in o_out + du_out + o_pass + [t_own_a, t_far_a, t_own_b, f_own_b, f_far_b, f_own_a, far_from_t, far_from_core, near]:
         copy.wait_send()
     for copy in ff_stores:
@@ -573,7 +588,8 @@
         jax.ShapeDtypeStruct((8, slab, hidden), F32),
         jax.ShapeDtypeStruct((8, dim, hidden), BF16),
         jax.ShapeDtypeStruct((2, rows, hidden), BF16),
-        jax.ShapeDtypeStruct((2, slab, hidden), F32),
+        jax.ShapeDtypeStruct((slab + slab // 2, hidden), F32),
+        jax.ShapeDtypeStruct((slab + slab // 2, hidden), F32),
     )
     scratch = [
         vmem((2, seq_len, hidden), BF16), vmem((2, 6 * dim, hidden), BF16), vmem((2, 2 * dim, hidden), BF16),
@@ -588,7 +604,7 @@
         functools.partial(attention_kernel, dim ** -0.5),
         out_shape=out_shape,
         in_specs=[any_spec] * 5,
-        out_specs=(any_spec,) * 8,
+        out_specs=(any_spec,) * 9,
         scratch_shapes=scratch,
         compiler_params=pltpu.CompilerParams(collective_id=1, has_side_effects=True, vmem_limit_bytes=VMEM_LIMIT),
         cost_estimate=pl.CostEstimate(flops=40 * 10**9, bytes_accessed=64 * 2**20, transcendentals=0),
@@ -614,7 +630,8 @@
 
     ring = Ring()
     slab = tokens // 8
-    slots = [pl.ds(pl.multiple_of(ring.at(slot) * slab, slab), slab) for slot in range(6)]
+    sizes = (slab, slab, slab, slab // 2, slab // 2, slab)
+    slots = [pl.ds(pl.multiple_of(ring.at(slot) * slab, slab), size) for slot, size in enumerate(sizes)]
 
     def slabs(src, dst, sem, row):
         return [pltpu.make_async_copy(src.at[rows], dst.at[rows], sem.at[row, index]) for index, rows in enumerate(slots)]
@@ -699,36 +716,39 @@
 
 def last_kernel(x_two, dy_two, du_far, du_far_other, dx_two_in, dx_two_out, x_buf, dy_buf, du_buf, load_sem, store_sem):
     ring = Ring()
-    slab = du_far.shape[0]
-    loads, stores = [], []
-    for index, (slot, du) in enumerate(((SAME_O, du_far), (OTHER_O, du_far_other))):
-        rows = pl.ds(pl.multiple_of(ring.at(slot) * slab, slab), slab)
-        sources = ((x_two.at[rows], x_buf), (dy_two.at[rows], dy_buf), (du, du_buf))
-        loads.append([pltpu.make_async_copy(src, dst.at[index], load_sem.at[index, which]) for which, (src, dst) in enumerate(sources)])
-        stores.append(pltpu.make_async_copy(dy_buf.at[index], dx_two_out.at[rows], store_sem.at[index]))
+    slab = x_buf.shape[1]
+    half = slab // 2
+    loads, stores, sizes = [], [], (slab, slab, half, half)
+    for index, (slot, du, skip) in enumerate(((SAME_O, du_far, 0), (OTHER_O, du_far_other, 0), (SAME_F, du_far, half), (OTHER_T, du_far_other, half))):
+        size = sizes[index]
+        rows = pl.ds(pl.multiple_of(ring.at(slot) * slab + skip, half), size)
+        sources = ((x_two.at[rows], x_buf), (dy_two.at[rows], dy_buf), (du.at[pl.ds(2 * skip, size)], du_buf))
+        loads.append([pltpu.make_async_copy(src, dst.at[index, pl.ds(0, size)], load_sem.at[index, which]) for which, (src, dst) in enumerate(sources)])
+        stores.append(pltpu.make_async_copy(dy_buf.at[index, pl.ds(0, size)], dx_two_out.at[rows], store_sem.at[index]))
     for copies in loads:
         for copy in copies:
             copy.start()
     for index, copies in enumerate(loads):
         for copy in copies:
             copy.wait()
-        dy_buf[index] += rms_back(x_buf[index], du_buf[index])
+        rows = pl.ds(0, sizes[index])
+        dy_buf[index, rows, :] += rms_back(x_buf[index, rows, :], du_buf[index, rows, :])
         stores[index].start()
     for copy in stores:
         copy.wait()
 
 
 def last_call(x_two, dy_two, du_far, du_far_other, dx_two):
-    slab, hidden = du_far.shape
+    tokens, hidden = x_two.shape
     any_spec = pl.BlockSpec(memory_space=pl.ANY)
-    buf = pltpu.VMEM((2, slab, hidden), F32)
+    buf = pltpu.VMEM((4, tokens // 8, hidden), F32)
     return pl.pallas_call(
         last_kernel,
         out_shape=jax.ShapeDtypeStruct(dx_two.shape, F32),
         in_specs=[any_spec] * 5,
         out_specs=any_spec,
         input_output_aliases={4: 0},
-        scratch_shapes=[buf, buf, buf, pltpu.SemaphoreType.DMA((2, 3)), pltpu.SemaphoreType.DMA((2,))],
+        scratch_shapes=[buf, buf, buf, pltpu.SemaphoreType.DMA((4, 3)), pltpu.SemaphoreType.DMA((4,))],
         cost_estimate=pl.CostEstimate(flops=10**6, bytes_accessed=4 * 2**20, transcendentals=0),
         name="last",
     )(x_two, dy_two, du_far, du_far_other, dx_two)
@@ -740,11 +760,11 @@
     flat = [tensor.reshape(-1, hidden) for tensor in (y_one, y_two, dy_one, dy_two)]
     qkv_parts = jnp.swapaxes(w_qkv[0, :, 0], 0, 1)
     x_two, dx_one, uc_seq, att_full, part_own, part_near, up_near = mlp_call(*flat, w_up[0], w_down[0], qkv_parts, w_out[0, 0])
-    d_up, d_down, d_att, o_pos, du_pos, wo_full, _, du_relay = attention_call(uc_seq, att_full, part_own, part_near, up_near)
+    d_up, d_down, d_att, o_pos, du_pos, wo_full, _, du_to_f, du_to_other_t = attention_call(uc_seq, att_full, part_own, part_near, up_near)
     devices = range(lax.axis_size("tp"))
     to_f = [(device, (3 - device // 2) * 2 + device % 2) for device in devices]
     to_other_t = [(device, 4 * (device // 4) + 3 - device % 4) for device in devices]
-    du_far, du_far_other = lax.ppermute(du_relay[0], "tp", to_f), lax.ppermute(du_relay[1], "tp", to_other_t)
+    du_far, du_far_other = lax.ppermute(du_to_f, "tp", to_f), lax.ppermute(du_to_other_t, "tp", to_other_t)
     tokens = flat[0].shape
     *states, dw_up, dw_down, dw_qkv, dw_out = finish_call(
         flat[0], o_pos.reshape(tokens), wo_full.reshape(-1, hidden), x_two, dx_one, flat[3], du_pos.reshape(tokens), d_up, d_down, d_att

time: 407 us -> 400 us (0.983)
  Pallas kernels: 400 us -> 395 us
    pallas_call x1, Pallas kernels: 167 us -> 161 us  [attention_call(): pl.pallas_call(functools.partial(attention_kernel, dim ** (-0.5)), out_sh...]
  transfers between devices with their start and end apart: 2 -> 2, of which waited for: 0 -> 1; matrix products, arithmetic and copies ran while one was open for 0% -> 0% of each run, Pallas kernels for 4% -> 4%
where the time goes in v9:
time: 400 us; the launch traced here: 399 us
  Pallas kernels  395 us (99%)
    pallas_call x1, Pallas kernels, mlp_call(): pl.pallas_call(mlp_kernel, out_shape=out_shape, in_specs=[any_spec] * 8,...  213 us
    pallas_call x1, Pallas kernels, attention_call(): pl.pallas_call(functools.partial(attention_kernel, dim ** (-0.5)), out_sh...  161 us
    pallas_call x1, Pallas kernels, finish_call(): pl.pallas_call(finish_kernel, out_shape=out_shape, in_specs=[any_spec] *...  17.7 us
  transfers between devices with their start and end apart: 2, of which 1 were waited for; matrix products, arithmetic and copies ran while one was open for 0% of the time, Pallas kernels for 4%

profile of v9, /device:TPU:112, one launch (start us, length us, event | category | flops | bytes accessed | tf_op | source)
XLA Modules:
  0.0 399.0 jit_solution(1950082017768026439)
XLA Ops:
  0.6 212.8 %feed_forward.1 = (f32[1024,1024]{1,0:T(8,128)}, f32[1024,1024]{1,0:T(8,128)}, bf16[8,2,128,1024]{3,2,1,0:T(8,128)(2,1)}, bf16[6,512,1024]{2,1,0:T(8,128)(2,1)},...) custom-call(f32[1024,1024]{1,0:T(8,128)} %bitcast.26, f32[1024,1024]{1,0:T(8,128)} %bitcast.32, ...), custom_call_target="tpu_custom_call" | custom-call | flops 70000001024 | bytes 67108864 | tf_op jit(solution)/shard_map/feed_forward/pallas_call | solution.py:334
  213.4 160.9 %attention.1 = (f32[512,1024]{1,0:T(8,128)}, f32[512,1024]{1,0:T(8,128)}, f32[512,1024]{1,0:T(8,128)}, bf16[8,128,1024]{2,1,0:T(8,128)(2,1)}, f32[8,128,1024]{2,...) custom-call(bf16[8,2,128,1024]{3,2,1,0:T(8,128)(2,1)} %get-tuple-ele, ...), custom_call_target="tpu_custom_call" | custom-call | flops 40000000000 | bytes 67108864 | tf_op jit(solution)/shard_map/attention/pallas_call | solution.py:603
  374.3 1.4 collective-permute-start
  375.7 0.6 collective-permute-start.1
  376.3 17.7 %finish.1 = (f32[1024,1024]{1,0:T(8,128)}, f32[1024,1024]{1,0:T(8,128)}, f32[1024,1024]{1,0:T(8,128)}, f32[1024,1024]{1,0:T(8,128)}, f32[1024,512]{1,0:T(8,128)}...) custom-call(f32[1024,1024]{1,0:T(8,128)} %bitcast.27, bf16[1024,1024]{1,0:T(8,128)(2,1)} %bitcast.30, ...), custom_call_target="tpu_custom_call" | custom-call | flops 2000000000 | bytes 54525952 | tf_op jit(solution)/shard_map/finish/pallas_call | solution.py:705
  394.0 1.6 collective-permute-done.du_far
  395.6 0.0 collective-permute-done.1.du_far_other
  395.6 3.3 last.1
Async XLA Ops:
  374.3 21.3 %collective-permute-start = (f32[192,1024]{1,0:T(8,128)}, f32[192,1024]{1,0:T(8,128)}, u32[]{:S(2)}, u32[]{:S(2)}) collective-permute-start(f32[192,1024]{1,0:T(8,128)} %get-tuple-element.47), channel_id=1, source_target_pairs={{0,6},{1,7},{2,4},{3,5},{4,2},{5,3},{6,0},{7,1},{8,14},{9,15},{10,... | collective-permute-start | bytes 2359304 | tf_op jit(solution)/shard_map/ppermute | solution.py:767
  375.7 19.9 %collective-permute-start.1 = (f32[192,1024]{1,0:T(8,128)}, f32[192,1024]{1,0:T(8,128)}, u32[]{:S(2)}, u32[]{:S(2)}) collective-permute-start(f32[192,1024]{1,0:T(8,128)} %get-tuple-element.48), channel_id=1, source_target_pairs={{0,3},{1,2},{2,1},{3,0},{4,7},{5,6},{6,5},{7,4},{8,11},{9,10},{10,... | collective-permute-start | bytes 2359304 | tf_op jit(solution)/shard_map/ppermute | solution.py:767

commit v10 on v9

--- a/solution.py
+++ b/solution.py
@@ -80,9 +80,9 @@
 
 def mlp_kernel(
     y_one, y_two, dy_one, dy_two, w_up, w_down, w_qkv, w_out,
-    x_two, dx_one, uc_seq, att_full, part_own, part_near, near_recv,
+    x_two, dx_one, uc_seq, uc_two, att_full, part_own, part_near, near_recv,
     u_all, c_all, up_all, down_all, acc, uc_own, relay, y_buf, x_buf, up_raw, qkv_raw, att_own,
-    load_sem, y_sem, x_sem, w_send, w_recv, uc_send, uc_recv, att_send, att_recv, a2a_send, a2a_recv, relay_recv, near_sem,
+    load_sem, y_sem, x_sem, w_send, w_recv, uc_send, uc_recv, att_send, att_recv, a2a_send, a2a_recv, relay_recv, near_sem, two_sem,
 ):
     ring = Ring()
     half = 512
@@ -109,18 +109,17 @@
     def att(src, dst_slot, to, index):
         return ring.copy(src, att_full.at[dst_slot], att_send.at[index], att_recv.at[dst_slot], to)
 
-    att_out = [att(att_own, 4, SAME_F, 0), att(att_own, 2, SAME_T, 1), att(att_own, 1, PARTNER, 2)]
+    att_out = [att(att_own, 4, SAME_F, 0), att(att_own, 1, PARTNER, 1)]
     att_keep = pltpu.make_async_copy(att_own, att_full.at[0], load_sem.at[6])
-    att_near_f = [att(att_full.at[4], 5, PARTNER, 3)]
-    att_near_t = [att(att_full.at[2], 3, PARTNER, 4)]
+    att_near_f = [att(att_full.at[4], 5, PARTNER, 2)]
 
     a2a_out = {slot: ring.copy(uc_own.at[slot], uc_seq.at[slot], a2a_send.at[slot], a2a_recv.at[slot], slot) for slot in (1, 2, 3, 4, 5)}
-    a2a_out[SAME_O] = ring.copy(uc_own.at[SAME_O], relay.at[0], a2a_send.at[SAME_O], relay_recv.at[0], SAME_T)
-    a2a_out[OTHER_O] = ring.copy(uc_own.at[OTHER_O], relay.at[1], a2a_send.at[OTHER_O], relay_recv.at[1], SAME_F)
-    a2a_pass = [
-        ring.copy(relay.at[0], uc_seq.at[SAME_O], a2a_send.at[8], a2a_recv.at[SAME_O], SAME_F),
-        ring.copy(relay.at[1], uc_seq.at[OTHER_O], a2a_send.at[9], a2a_recv.at[OTHER_O], OTHER_T),
-    ]
+    a2a_out[SAME_O] = ring.copy(uc_own.at[SAME_O], relay.at[0], a2a_send.at[SAME_O], relay_recv.at[0], SAME_F)
+    a2a_out[OTHER_O] = ring.copy(uc_own.at[OTHER_O], relay.at[1], a2a_send.at[OTHER_O], relay_recv.at[1], OTHER_F)
+    a2a_pass = [ring.copy(relay.at[index], uc_seq.at[SAME_O + index], a2a_send.at[8 + index], a2a_recv.at[SAME_O + index], SAME_T) for index in (0, 1)]
+    two_out = ring.copy(uc_own.at[OTHER_T], uc_two.at[1], a2a_send.at[10], relay_recv.at[2], PARTNER)
+    two_keep = pltpu.make_async_copy(uc_own.at[SAME_T], uc_two.at[0], two_sem.at[0])
+    two_relay = pltpu.make_async_copy(relay, uc_two.at[pl.ds(2, 2)], two_sem.at[1])
     uc_keep = pltpu.make_async_copy(uc_own.at[0], uc_seq.at[0], load_sem.at[4])
 
     def start(copies):
@@ -247,6 +246,8 @@
     for slot in (7, 6, 5, 4, 3, 2, 1):
         a2a_out[slot].start()
     uc_keep.start()
+    two_out.start()
+    two_keep.start()
     for step in (6, 7):
         for copy in x_stores(step, step % 2):
             copy.wait()
@@ -264,20 +265,16 @@
         @pl.when(step == 4)
         def _():
             start(uc_pass)
+            for index in (0, 1):
+                ring.copy(relay.at[index], relay.at[index], a2a_send.at[0], relay_recv.at[index], PARTNER).wait_recv()
+            start(a2a_pass)
+            two_relay.start()
 
         @pl.when(step == 8)
         def _():
             near.start()
             ring.copy(att_own, att_full.at[4], att_send.at[0], att_recv.at[4], PARTNER).wait_recv()
             start(att_near_f)
-            ring.copy(att_own, att_full.at[2], att_send.at[0], att_recv.at[2], PARTNER).wait_recv()
-            start(att_near_t)
-
-        @pl.when(step == 9)
-        def _():
-            for index in (0, 1):
-                ring.copy(relay.at[index], relay.at[index], a2a_send.at[0], relay_recv.at[index], PARTNER).wait_recv()
-            start(a2a_pass)
 
         rows = pl.ds(pl.multiple_of((step % 2) * half, half), half)
         u_part, c_part = u_all[tokens, rows, :], c_all[tokens, rows, :]
@@ -293,14 +290,17 @@
     out_near.start()
     out_own.start()
 
-    for slot in (1, 3, 5):
+    two_out.wait_recv()
+    for slot in (1, 5):
         ring.copy(att_own, att_full.at[slot], att_send.at[0], att_recv.at[slot], PARTNER).wait_recv()
     for slot in range(1, 8):
         ring.copy(uc_own.at[slot], uc_seq.at[slot], a2a_send.at[0], a2a_recv.at[slot], PARTNER).wait_recv()
-    for copy in w_own + w_near_t + w_near_f + w_far + uc_out + uc_pass + att_out + att_near_t + att_near_f + list(a2a_out.values()) + a2a_pass:
+    for copy in w_own + w_near_t + w_near_f + w_far + uc_out + uc_pass + att_out + att_near_f + list(a2a_out.values()) + a2a_pass + [two_out]:
         copy.wait_send()
     near.wait()
     uc_keep.wait()
+    two_keep.wait()
+    two_relay.wait()
     att_keep.wait()
     out_near.wait()
     out_own.wait()
@@ -310,13 +310,14 @@
     tokens, hidden = y_one.shape
     ffn = w_down.shape[0]
     dim = w_out.shape[0]
-    near_rows = ffn
+    near_rows = ffn // 2
     any_spec = pl.BlockSpec(memory_space=pl.ANY)
     dma, vmem = pltpu.SemaphoreType.DMA, pltpu.VMEM
     out_shape = (
         jax.ShapeDtypeStruct((tokens, hidden), F32),
         jax.ShapeDtypeStruct((tokens, hidden), F32),
         jax.ShapeDtypeStruct((8, 2, tokens // 8, hidden), BF16),
+        jax.ShapeDtypeStruct((4, 2, tokens // 8, hidden), BF16),
         jax.ShapeDtypeStruct((6, 4 * dim, hidden), BF16),
         jax.ShapeDtypeStruct((2 * ffn, hidden), F32),
         jax.ShapeDtypeStruct((2 * ffn - near_rows, hidden), F32),
@@ -329,13 +330,13 @@
         vmem((8, 2, tokens // 8, hidden), BF16), vmem((2, 2, tokens // 8, hidden), BF16),
         vmem((2, 3, tokens // 8, hidden), F32), vmem((2, 2, tokens // 8, hidden), F32),
         vmem((hidden, ffn), BF16), vmem((3, hidden, dim), BF16), vmem((4 * dim, hidden), BF16),
-        dma((8,)), dma((2, 3)), dma((2, 2)), dma((14,)), dma((8, 2)), dma((6,)), dma((4, 2)), dma((5,)), dma((6,)), dma((10,)), dma((8,)), dma((2,)), dma((2,)),
+        dma((8,)), dma((2, 3)), dma((2, 2)), dma((14,)), dma((8, 2)), dma((6,)), dma((4, 2)), dma((3,)), dma((6,)), dma((11,)), dma((8,)), dma((3,)), dma((2,)), dma((2,)),
     ]
     return pl.pallas_call(
         mlp_kernel,
         out_shape=out_shape,
         in_specs=[any_spec] * 8,
-        out_specs=(any_spec,) * 7,
+        out_specs=(any_spec,) * 8,
         scratch_shapes=scratch,
         compiler_params=pltpu.CompilerParams(collective_id=0, has_side_effects=True, vmem_limit_bytes=VMEM_LIMIT),
         cost_estimate=pl.CostEstimate(flops=70 * 10**9, bytes_accessed=64 * 2**20, transcendentals=0),
@@ -344,10 +345,10 @@
 
 
 def attention_kernel(
-    scale, uc_seq, att_full, part_own, part_near, up_near,
-    d_up, d_down, d_att, o_pos, du_pos, wo_full, att_far, to_f, to_other_t,
-    uc_all, qkv_buf, wo_buf, qkv, d_ctx, d_qkv, o_all, du_all, part_send, part_keep, part_core, own_t, far_t, own_f, far_f, o_relay, near_out, near_buf,
-    load_sem, w_sem, wo_sem, near_sem, core_send, core_recv, part_out, part_in, far_sem, o_send, o_recv, du_send, du_recv, o_relay_recv, du_relay_recv,
+    scale, uc_seq, uc_two, att_full, part_own, part_near, near_first,
+    d_up, d_down, d_att, o_pos, du_pos, wo_full, att_far, uc_far, to_f, to_other_t,
+    uc_all, qkv_buf, wo_buf, qkv, d_ctx, d_qkv, o_all, du_all, part_send, part_keep, part_core, own_f, o_relay, near_out, near_buf,
+    load_sem, two_sem, w_sem, wo_sem, near_sem, core_send, core_recv, f_sem, far_sem, uc_sem, o_send, o_recv, du_send, du_recv, o_relay_recv, du_relay_recv,
 ):
     ring = Ring()
     slab, hidden = uc_seq.shape[2], uc_seq.shape[3]
@@ -356,7 +357,8 @@
     tile = 512
 
     def relation_of(step):
-        return (step + 1) % 4
+        base = step % 4
+        return jnp.where(base == 0, 2, jnp.where(base == 3, 3, base - 1))
 
     def w_loads(heads, buf):
         copies = []
@@ -365,53 +367,42 @@
             copies.append(pltpu.make_async_copy(head.at[pl.ds(3 * dim, dim)], wo_buf.at[buf, pl.ds(index * dim, dim)], w_sem.at[buf, index, 1]))
         return copies
 
-    far_from_t = ring.copy(att_full.at[SAME_F], att_far.at[0], far_sem.at[0], far_sem.at[1], SAME_T)
-    far_from_core = ring.copy(att_far.at[0], att_far.at[1], far_sem.at[2], far_sem.at[3], PARTNER)
-
+    att_t = ring.copy(att_full.at[0], att_far.at[0], far_sem.at[0], far_sem.at[1], SAME_T)
+    att_t_core = ring.copy(att_far.at[0], att_far.at[1], far_sem.at[2], far_sem.at[3], PARTNER)
+    att_o = ring.copy(att_full.at[SAME_F], att_far.at[2], far_sem.at[4], far_sem.at[5], SAME_T)
+    att_o_core = ring.copy(att_far.at[2], att_far.at[3], far_sem.at[6], far_sem.at[7], PARTNER)
+    uc_to_t = [ring.copy(uc_seq.at[pl.ds(2 * slot, 2)], uc_far.at[pl.ds(slot, 2)], uc_sem.at[slot], uc_sem.at[slot + 1], SAME_T) for slot in (0, 2)]
     near_load = pltpu.make_async_copy(part_near, near_out, near_sem.at[2])
     near = ring.copy(near_out, near_buf, near_sem.at[0], near_sem.at[1], SAME_F)
-
-    def core_copy(relation, buf):
-        return ring.copy(part_send.at[buf], part_core.at[relation], core_send.at[buf], core_recv.at[relation], PARTNER)
-
-    core_last = [core_copy(3, 0), core_copy(0, 1)]
+    core_copies = [ring.copy(part_send.at[index], part_core.at[index], core_send.at[index], core_recv.at[index], PARTNER) for index in (0, 1)]
+    f_copy = ring.copy(part_keep.at[0], own_f, f_sem.at[0], f_sem.at[1], SAME_F)
+
     rows = part_keep.shape[1]
+    first = near_first.shape[0]
     ff_loads = [
         pltpu.make_async_copy(part_own.at[pl.ds(0, rows)], part_send.at[0], load_sem.at[1, 0]),
         pltpu.make_async_copy(part_own.at[pl.ds(rows, rows)], part_send.at[1], load_sem.at[1, 1]),
-        pltpu.make_async_copy(up_near, part_core.at[1], load_sem.at[2, 0]),
+        pltpu.make_async_copy(near_first, part_core.at[0, pl.ds(0, first)], load_sem.at[2, 0]),
     ]
     ff_stores = [pltpu.make_async_copy(part_send.at[index], dst, load_sem.at[3, index]) for index, dst in enumerate((d_up, d_down))]
 
-    rows_a, rows_b = pl.ds(0, 3 * dim), pl.ds(3 * dim, dim)
-
-    def part(src, dst, index, slot):
-        return ring.copy(src, dst, part_out.at[index], part_in.at[index], slot)
-
-    t_own_a = part(part_keep.at[1, rows_a], own_t.at[rows_a], 0, SAME_T)
-    t_far_a = part(part_keep.at[3, rows_a], far_t, 1, SAME_T)
-    t_own_b = part(part_keep.at[1, rows_b], own_t.at[rows_b], 2, SAME_T)
-    f_own_b = part(part_keep.at[2, rows_b], own_f.at[rows_b], 3, SAME_F)
-    f_far_b = part(part_keep.at[3, rows_b], far_f, 4, SAME_F)
-    f_own_a = part(part_keep.at[2, rows_a], own_f.at[rows_a], 5, SAME_F)
-
     def rows_of(slot):
         return pl.ds(slot * slab, slab)
 
-    def to_positions(src, dst, relay, send_sem, recv_sem, relay_sem):
-        near_t, near_f = ring.at(SAME_T), ring.at(SAME_F)
-        out = [
-            ring.copy(src.at[rows_of(SAME_O)], relay.at[0], send_sem.at[6], relay_sem.at[0], SAME_T),
-            ring.copy(src.at[rows_of(OTHER_O)], relay.at[1], send_sem.at[7], relay_sem.at[1], SAME_F),
-        ] + [ring.copy(src.at[rows_of(slot)], dst.at[ring.me], send_sem.at[slot], recv_sem.at[slot], slot) for slot in (5, 4, 3, 2, 1)]
-        onward = [
-            ring.copy(relay.at[0], dst.at[near_t], send_sem.at[8], recv_sem.at[SAME_O], SAME_F),
-            ring.copy(relay.at[1], dst.at[near_f], send_sem.at[9], recv_sem.at[OTHER_O], OTHER_T),
-        ]
-        keep = pltpu.make_async_copy(src.at[rows_of(0)], dst.at[ring.me], send_sem.at[0])
-        return out, onward, keep
-
-    o_out, o_pass, o_keep = to_positions(o_all, o_pos, o_relay, o_send, o_recv, o_relay_recv)
+    def seq_loads(seq, row, src, src_slot, slot, sem):
+        return [pltpu.make_async_copy(src.at[src_slot, which], uc_all.at[2 * seq + which, rows_of(slot)], sem.at[row, which]) for which in (0, 1)]
+
+    o_src = o_all.at[0]
+    o_out = [
+        ring.copy(o_src.at[rows_of(SAME_O)], o_relay.at[0], o_send.at[6], o_relay_recv.at[0], SAME_T),
+        ring.copy(o_src.at[rows_of(OTHER_O)], o_relay.at[1], o_send.at[7], o_relay_recv.at[1], SAME_F),
+    ] + [ring.copy(o_src.at[rows_of(slot)], o_pos.at[ring.me], o_send.at[slot], o_recv.at[slot], slot) for slot in (5, 4, 3, 2, 1)]
+    o_pass = [
+        ring.copy(o_relay.at[0], o_pos.at[ring.at(SAME_T)], o_send.at[8], o_recv.at[SAME_O], SAME_F),
+        ring.copy(o_relay.at[1], o_pos.at[ring.at(SAME_F)], o_send.at[9], o_recv.at[OTHER_O], OTHER_T),
+    ]
+    o_keep = pltpu.make_async_copy(o_src.at[rows_of(0)], o_pos.at[ring.me], o_send.at[0])
+
     late = slab - to_f.shape[0] % slab
     du_rows = {slot: rows_of(slot) for slot in range(1, 8)}
     du_rows[SAME_F], du_rows[OTHER_T] = pl.ds(SAME_F * slab, late), pl.ds(OTHER_T * slab, late)
@@ -429,42 +420,54 @@
         for copy in copies:
             copy.start()
 
-    loads = [pltpu.make_async_copy(uc_seq.at[slot, which], uc_all.at[which, rows_of(slot)], load_sem.at[slot, which]) for slot in range(8) for which in (0, 1)]
+    loads = [copy for slot in range(8) for copy in seq_loads(0, slot, uc_seq, slot, slot, load_sem)]
+    two_loads = [copy for slot in range(4) for copy in seq_loads(1, slot, uc_two, slot, slot, two_sem)]
+    far_loads = [copy for slot in range(4) for copy in seq_loads(1, 4 + slot, uc_far, slot, 4 + slot, two_sem)]
     near_load.start()
     start(loads)
-    start(w_loads([att_full.at[3], att_full.at[2]], 0))
+    start(w_loads([att_full.at[5], att_full.at[4]], 0))
     ring.barrier()
-    far_from_t.start()
+    att_t.start()
+    att_o.start()
+    start(uc_to_t)
     near_load.wait()
     near.start()
+    start(two_loads)
     du_all[...] = jnp.zeros_like(du_all)
+    part_send[...] = jnp.zeros_like(part_send)
+    part_keep[...] = jnp.zeros_like(part_keep)
     for copy in loads:
         copy.wait()
 
     def chip_step(step, carry):
         buf = step % 2
+        seq = step // 4
         relation = relation_of(step)
-        for copy in w_loads([att_far.at[0], att_far.at[0]], buf):
+
+        @pl.when(step == 4)
+        def _():
+            for copy in uc_to_t:
+                copy.wait_recv()
+            start(far_loads)
+            for copy in two_loads + far_loads:
+                copy.wait()
+
+        for copy in w_loads([att_full.at[0], att_full.at[0]], buf):
             copy.wait()
 
-        @pl.when(step == 0)
-        def _():
-            start(w_loads([att_full.at[5], att_full.at[4]], 1))
-
-        @pl.when(step == 1)
-        def _():
-            far_from_core.wait_recv()
-            start(w_loads([att_far.at[1], att_far.at[0]], 0))
-
-        @pl.when(step == 2)
+        @pl.when((step == 0) | (step == 4))
         def _():
             start(w_loads([att_full.at[1], att_full.at[0]], 1))
+
+        @pl.when(step == 3)
+        def _():
+            start(w_loads([att_full.at[5], att_full.at[4]], 0))
 
         heads = [ring.at_traced(relation * 2 + other) for other in (1, 0)]
         wo_copies = [pltpu.make_async_copy(wo_buf.at[buf, pl.ds(index * dim, dim)], wo_full.at[head], wo_sem.at[index]) for index, head in enumerate(heads)]
         start(wo_copies)
-        qkv[...] = dot_nt(uc_all[0], qkv_buf[buf]).astype(BF16)
-        d_ctx[...] = dot_nt(uc_all[1], wo_buf[buf]).astype(BF16)
+        qkv[...] = dot_nt(uc_all[2 * seq], qkv_buf[buf]).astype(BF16)
+        d_ctx[...] = dot_nt(uc_all[2 * seq + 1], wo_buf[buf]).astype(BF16)
         for index, head in enumerate(heads):
             columns = pl.ds(pl.multiple_of(head * dim, dim), dim)
             own = pl.ds(index * 3 * dim, 3 * dim)
@@ -474,142 +477,147 @@
             grown = jnp.exp2(scores - jnp.max(scores, axis=-1, keepdims=True))
             prob = grown * (1.0 / jnp.sum(grown, axis=-1, keepdims=True))
             prob_b = prob.astype(BF16)
-            o_all[:, columns] = dot_nn(prob_b, value).astype(BF16)
+            o_all[seq, :, columns] = dot_nn(prob_b, value).astype(BF16)
             d_prob = dot_nt(d_out, value)
             d_score = (prob * (d_prob - jnp.sum(d_prob * prob, axis=-1, keepdims=True)) * scale).astype(BF16)
             d_qkv[:, pl.ds(index * 3 * dim, dim)] = dot_nn(d_score, key).astype(BF16)
             d_qkv[:, pl.ds((index * 3 + 1) * dim, dim)] = dot_nn(query.T, d_score).T.astype(BF16)
             d_qkv[:, pl.ds((index * 3 + 2) * dim, dim)] = dot_nn(d_out.T, prob_b).T.astype(BF16)
+
+            @pl.when((step < 2) | (step >= 4))
+            def _():
+                dst = (part_send, part_keep)[index].at[buf]
+                dst[pl.ds(0, 3 * dim), :] += dot_tn(d_qkv[:, own], uc_all[2 * seq])
+                dst[pl.ds(3 * dim, dim), :] += dot_tn(o_all[seq, :, columns], uc_all[2 * seq + 1])
+
             if index == 0:
-                @pl.when(step >= 2)
+                @pl.when(step == 1)
                 def _():
-                    core_copy(relation, buf).wait_send()
-
-            dst = part_send.at[buf] if index == 0 else part_keep.at[relation]
-            dst[pl.ds(0, 3 * dim), :] = dot_tn(d_qkv[:, own], uc_all[0])
-            dst[pl.ds(3 * dim, dim), :] = dot_tn(o_all[:, columns], uc_all[1])
-            if index == 0:
-                core_copy(relation, buf).start()
-        core_copy(relation, buf).wait_recv()
-        part_keep[relation] += part_core[relation]
-
-        @pl.when(step == 0)
-        def _():
-            t_own_a.start()
+                    att_t.wait_recv()
+                    att_t_core.start()
+
+                @pl.when(step == 4)
+                def _():
+                    core_copies[0].start()
+
+                @pl.when(step == 5)
+                def _():
+                    core_copies[1].start()
+
+        @pl.when(step < 4)
+        def _():
+            def du_tile(part, carry):
+                rows = pl.ds(pl.multiple_of(part * tile, tile), tile)
+                du_all[rows, :] += dot_nn(d_qkv[rows, :], qkv_buf[buf])
+                return carry
+
+            lax.fori_loop(0, seq_len // tile, du_tile, 0)
 
         @pl.when(step == 1)
         def _():
-            f_own_b.start()
+            att_t_core.wait_recv()
+            start(w_loads([att_far.at[1], att_far.at[0]], 0))
 
         @pl.when(step == 2)
         def _():
-            t_far_a.start()
-            f_far_b.start()
-
-        def du_tile(part, carry):
-            rows = pl.ds(pl.multiple_of(part * tile, tile), tile)
-            du_all[rows, :] += dot_nn(d_qkv[rows, :], qkv_buf[buf])
-            return carry
-
-        lax.fori_loop(0, seq_len // tile, du_tile, 0)
-
-        @pl.when(step == 0)
-        def _():
-            far_from_t.wait_recv()
-            far_from_core.start()
+            att_o.wait_recv()
+            att_o_core.start()
+            att_o_core.wait_recv()
+            start(w_loads([att_far.at[3], att_far.at[2]], 1))
+
+        @pl.when(step == 3)
+        def _():
+            start(o_out)
+            start(du_out)
+            start(du_late)
+            o_keep.start()
+            du_keep.start()
+
+        @pl.when(step == 4)
+        def _():
+            core_copies[0].wait_recv()
+            part_keep[0] += part_core[0]
+            f_copy.start()
 
         for copy in wo_copies:
             copy.wait()
         return carry
 
-    lax.fori_loop(0, 4, chip_step, 0)
-    start(o_out)
-    start(du_out)
-    start(du_late)
-    o_keep.start()
-    du_keep.start()
-    for copy in core_last:
-        copy.wait_send()
-    start(ff_loads)
-    f_far_b.wait_recv()
-    part_keep[1, rows_b] += far_f[...]
-    t_own_b.start()
+    lax.fori_loop(0, 6, chip_step, 0)
     for copy in o_out[:2]:
         copy.wait_recv()
     start(o_pass)
-    t_far_a.wait_recv()
-    part_keep[2, rows_a] += far_t[...]
-    f_own_a.start()
+    core_copies[1].wait_recv()
+    part_keep[1] += part_core[1]
+    for copy in core_copies:
+        copy.wait_send()
+    start(ff_loads)
     for copy in ff_loads:
         copy.wait()
-    part_send[0] += part_core[1]
     near.wait_recv()
-    part_send[1] += near_buf[...]
-    for copy in ff_stores:
-        copy.start()
-    t_own_a.wait_recv()
-    t_own_b.wait_recv()
-    part_keep[0] += own_t[...]
-    f_own_a.wait_recv()
-    f_own_b.wait_recv()
-    part_keep[0] += own_f[...]
-    d_att_copy = pltpu.make_async_copy(part_keep.at[0], d_att, load_sem.at[0, 0])
-    d_att_copy.start()
-
-    for copy in du_out[:2]:
+    part_send[0, pl.ds(0, first), :] += part_core[0, pl.ds(0, first), :]
+    part_send[0, pl.ds(first, rows - first), :] += near_buf[pl.ds(0, rows - first), :]
+    part_send[1] += near_buf[pl.ds(rows - first, rows), :]
+    start(ff_stores)
+    for copy in du_out[2:]:
         copy.wait_recv()
     for slot in range(1, 8):
         ring.copy(o_pos.at[0], o_pos.at[ring.at(slot)], near_sem.at[0], o_recv.at[slot], PARTNER).wait_recv()
-    for copy in du_out[2:]:
+    for copy in du_out[:2]:
         copy.wait_recv()
-    for copy in du_late:
-        copy.wait()
-    for copy in o_out + du_out + o_pass + [t_own_a, t_far_a, t_own_b, f_own_b, f_far_b, f_own_a, far_from_t, far_from_core, near]:
+    f_copy.wait_recv()
+    part_keep[1] += own_f[...]
+    d_att_copy = pltpu.make_async_copy(part_keep.at[1], d_att, load_sem.at[0, 0])
+    d_att_copy.start()
+
+    for copy in o_out + du_out + o_pass + uc_to_t + [f_copy, att_t, att_t_core, att_o, att_o_core, near]:
         copy.wait_send()
-    for copy in ff_stores:
+    for copy in du_late + ff_stores:
         copy.wait()
     o_keep.wait()
     du_keep.wait()
     d_att_copy.wait()
 
 
-def attention_call(uc_seq, att_full, part_own, part_near, up_near):
+def attention_call(uc_seq, uc_two, att_full, part_own, part_near, near_first):
     slab, hidden = uc_seq.shape[2:]
     rows = att_full.shape[1]
     dim = rows // 4
     seq_len = 8 * slab
     any_spec = pl.BlockSpec(memory_space=pl.ANY)
     dma, vmem = pltpu.SemaphoreType.DMA, pltpu.VMEM
+    ffn = part_own.shape[0] // 2
     out_shape = (
-        jax.ShapeDtypeStruct(up_near.shape, F32),
-        jax.ShapeDtypeStruct(part_near.shape, F32),
+        jax.ShapeDtypeStruct((ffn, hidden), F32),
+        jax.ShapeDtypeStruct((ffn, hidden), F32),
         jax.ShapeDtypeStruct((rows, hidden), F32),
         jax.ShapeDtypeStruct((8, slab, hidden), BF16),
         jax.ShapeDtypeStruct((8, slab, hidden), F32),
         jax.ShapeDtypeStruct((8, dim, hidden), BF16),
-        jax.ShapeDtypeStruct((2, rows, hidden), BF16),
+        jax.ShapeDtypeStruct((4, rows, hidden), BF16),
+        jax.ShapeDtypeStruct((4, 2, slab, hidden), BF16),
         jax.ShapeDtypeStruct((slab + slab // 2, hidden), F32),
         jax.ShapeDtypeStruct((slab + slab // 2, hidden), F32),
     )
     scratch = [
-        vmem((2, seq_len, hidden), BF16), vmem((2, 6 * dim, hidden), BF16), vmem((2, 2 * dim, hidden), BF16),
+        vmem((4, seq_len, hidden), BF16), vmem((2, 6 * dim, hidden), BF16), vmem((2, 2 * dim, hidden), BF16),
         vmem((seq_len, 6 * dim), BF16), vmem((seq_len, 2 * dim), BF16), vmem((seq_len, 6 * dim), BF16),
-        vmem((seq_len, hidden), BF16), vmem((seq_len, hidden), F32),
-        vmem((2, rows, hidden), F32), vmem((4, rows, hidden), F32), vmem((4, rows, hidden), F32),
-        vmem((rows, hidden), F32), vmem((3 * dim, hidden), F32), vmem((rows, hidden), F32), vmem((dim, hidden), F32),
+        vmem((2, seq_len, hidden), BF16), vmem((seq_len, hidden), F32),
+        vmem((2, rows, hidden), F32), vmem((2, rows, hidden), F32), vmem((2, rows, hidden), F32), vmem((rows, hidden), F32),
         vmem((2, slab, hidden), BF16), vmem(part_near.shape, F32), vmem(part_near.shape, F32),
-        dma((8, 2)), dma((2, 2, 2)), dma((2,)), dma((3,)), dma((2,)), dma((4,)), dma((6,)), dma((6,)), dma((4,)), dma((10,)), dma((8,)), dma((10,)), dma((8,)), dma((2,)), dma((2,)),
+        dma((8, 2)), dma((8, 2)), dma((2, 2, 2)), dma((2,)), dma((3,)), dma((2,)), dma((2,)), dma((2,)), dma((8,)), dma((4,)),
+        dma((10,)), dma((8,)), dma((10,)), dma((8,)), dma((2,)), dma((2,)),
     ]
     return pl.pallas_call(
         functools.partial(attention_kernel, dim ** -0.5),
         out_shape=out_shape,
-        in_specs=[any_spec] * 5,
-        out_specs=(any_spec,) * 9,
+        in_specs=[any_spec] * 6,
+        out_specs=(any_spec,) * 10,
         scratch_shapes=scratch,
         compiler_params=pltpu.CompilerParams(collective_id=1, has_side_effects=True, vmem_limit_bytes=VMEM_LIMIT),
-        cost_estimate=pl.CostEstimate(flops=40 * 10**9, bytes_accessed=64 * 2**20, transcendentals=0),
+        cost_estimate=pl.CostEstimate(flops=50 * 10**9, bytes_accessed=64 * 2**20, transcendentals=0),
         name="attention",
-    )(uc_seq, att_full, part_own, part_near, up_near)
+    )(uc_seq, uc_two, att_full, part_own, part_near, near_first)
 
 
 def finish_kernel(
@@ -759,8 +767,8 @@
     _, _, _, parts, dim = w_qkv.shape
     flat = [tensor.reshape(-1, hidden) for tensor in (y_one, y_two, dy_one, dy_two)]
     qkv_parts = jnp.swapaxes(w_qkv[0, :, 0], 0, 1)
-    x_two, dx_one, uc_seq, att_full, part_own, part_near, up_near = mlp_call(*flat, w_up[0], w_down[0], qkv_parts, w_out[0, 0])
-    d_up, d_down, d_att, o_pos, du_pos, wo_full, _, du_to_f, du_to_other_t = attention_call(uc_seq, att_full, part_own, part_near, up_near)
+    x_two, dx_one, *shared = mlp_call(*flat, w_up[0], w_down[0], qkv_parts, w_out[0, 0])
+    d_up, d_down, d_att, o_pos, du_pos, wo_full, _, _, du_to_f, du_to_other_t = attention_call(*shared)
     devices = range(lax.axis_size("tp"))
     to_f = [(device, (3 - device // 2) * 2 + device % 2) for device in devices]
     to_other_t = [(device, 4 * (device // 4) + 3 - device % 4) for device in devices]

time: 400 us -> 385 us (0.963)
  Pallas kernels: 395 us -> 382 us
    pallas_call x1, Pallas kernels: 213 us -> 190 us  [mlp_call(): pl.pallas_call(mlp_kernel, out_shape=out_shape, in_specs=[any_spec] * 8,...]
    pallas_call x1, Pallas kernels: 161 us -> 171 us  [attention_call(): pl.pallas_call(functools.partial(attention_kernel, dim ** (-0.5)), out_sh...]
  transfers between devices with their start and end apart: 2 -> 2, of which waited for: 1 -> 1; matrix products, arithmetic and copies ran while one was open for 0% -> 0% of each run, Pallas kernels for 4% -> 5%
where the time goes in v10:
time: 385 us; the launch traced here: 384 us
  Pallas kernels  382 us (99%)
    pallas_call x1, Pallas kernels, mlp_call(): pl.pallas_call(mlp_kernel, out_shape=out_shape, in_specs=[any_spec] * 8,...  190 us
    pallas_call x1, Pallas kernels, attention_call(): pl.pallas_call(functools.partial(attention_kernel, dim ** (-0.5)), out_sh...  171 us
    pallas_call x1, Pallas kernels, finish_call(): pl.pallas_call(finish_kernel, out_shape=out_shape, in_specs=[any_spec] *...  17.7 us
  transfers between devices with their start and end apart: 2, of which 1 were waited for; matrix products, arithmetic and copies ran while one was open for 0% of the time, Pallas kernels for 5%

profile of v10, /device:TPU:112, one launch (start us, length us, event | category | flops | bytes accessed | tf_op | source)
XLA Modules:
  0.0 384.5 jit_solution(17395241013759932510)
XLA Ops:
  0.6 190.3 %feed_forward.1 = (f32[1024,1024]{1,0:T(8,128)}, f32[1024,1024]{1,0:T(8,128)}, bf16[8,2,128,1024]{3,2,1,0:T(8,128)(2,1)}, bf16[4,2,128,1024]{3,2,1,0:T(8,128)(2,...) custom-call(f32[1024,1024]{1,0:T(8,128)} %bitcast.26, ...), custom_call_target="tpu_custom_call" | custom-call | flops 70000001024 | bytes 67108864 | tf_op jit(solution)/shard_map/feed_forward/pallas_call | solution.py:335
  190.9 170.6 %attention.1 = (f32[512,1024]{1,0:T(8,128)}, f32[512,1024]{1,0:T(8,128)}, f32[512,1024]{1,0:T(8,128)}, bf16[8,128,1024]{2,1,0:T(8,128)(2,1)}, f32[8,128,1024]{2,...) custom-call(bf16[8,2,128,1024]{3,2,1,0:T(8,128)(2,1)} %get-tuple-ele, ...), custom_call_target="tpu_custom_call" | custom-call | flops 49999998976 | bytes 67108864 | tf_op jit(solution)/shard_map/attention/pallas_call | solution.py:611
  361.5 1.4 collective-permute-start
  362.9 0.0 collective-permute-start.1
  362.9 17.7 %finish.1 = (f32[1024,1024]{1,0:T(8,128)}, f32[1024,1024]{1,0:T(8,128)}, f32[1024,1024]{1,0:T(8,128)}, f32[1024,1024]{1,0:T(8,128)}, f32[1024,512]{1,0:T(8,128)}...) custom-call(f32[1024,1024]{1,0:T(8,128)} %bitcast.27, bf16[1024,1024]{1,0:T(8,128)(2,1)} %bitcast.30, ...), custom_call_target="tpu_custom_call" | custom-call | flops 2000000000 | bytes 54525952 | tf_op jit(solution)/shard_map/finish/pallas_call | solution.py:713
  380.6 0.0 collective-permute-done.du_far
  380.6 0.4 collective-permute-done.1.du_far_other
  381.0 3.3 last.1
Async XLA Ops:
  361.5 19.1 %collective-permute-start = (f32[192,1024]{1,0:T(8,128)}, f32[192,1024]{1,0:T(8,128)}, u32[]{:S(2)}, u32[]{:S(2)}) collective-permute-start(f32[192,1024]{1,0:T(8,128)} %get-tuple-element.49), channel_id=1, source_target_pairs={{0,6},{1,7},{2,4},{3,5},{4,2},{5,3},{6,0},{7,1},{8,14},{9,15},{10,... | collective-permute-start | bytes 2359304 | tf_op jit(solution)/shard_map/ppermute | solution.py:775
  362.9 18.1 %collective-permute-start.1 = (f32[192,1024]{1,0:T(8,128)}, f32[192,1024]{1,0:T(8,128)}, u32[]{:S(2)}, u32[]{:S(2)}) collective-permute-start(f32[192,1024]{1,0:T(8,128)} %get-tuple-element.50), channel_id=1, source_target_pairs={{0,3},{1,2},{2,1},{3,0},{4,7},{5,6},{6,5},{7,4},{8,11},{9,10},{10,... | collective-permute-start | bytes 2359304 | tf_op jit(solution)/shard_map/ppermute | solution.py:775

commit v11 on v10

v11 whole, which is shorter than its diff:
```python
import functools

import jax
import jax.numpy as jnp
from jax import lax
from jax.experimental import pallas as pl
from jax.experimental.pallas import tpu as pltpu
from jax.sharding import PartitionSpec as P

RMS_EPS = 1e-6
LOG2_E = 1.4426950408889634
MESH = pl.DeviceIdType.MESH
BF16, F32 = jnp.bfloat16, jnp.float32
VMEM_LIMIT = 64 * 1024 * 1024 - 65536


def inv_rms(tensor):
    return lax.rsqrt(jnp.mean(tensor * tensor, axis=-1, keepdims=True) + RMS_EPS)


def rms_norm(tensor):
    return tensor * inv_rms(tensor)


def rms_back(tensor, grad_in):
    scale = inv_rms(tensor)
    return scale * grad_in - tensor * (scale * scale * scale) * jnp.mean(grad_in * tensor, axis=-1, keepdims=True)


def gelu_and_slope(tensor):
    root = (2.0 / jnp.pi) ** 0.5
    squared = tensor * tensor
    tanh = jnp.tanh(root * (tensor + 0.044715 * (tensor * squared)))
    cdf = 0.5 * (1.0 + tanh)
    slope = cdf + (0.5 * root) * tensor * ((1.0 - tanh * tanh) * (1.0 + (3 * 0.044715) * squared))
    return tensor * cdf, slope


def dot_nn(left, right):
    return lax.dot_general(left, right, (((1,), (0,)), ((), ())), preferred_element_type=F32)


def dot_nt(left, right):
    return lax.dot_general(left, right, (((1,), (1,)), ((), ())), preferred_element_type=F32)


def dot_tn(left, right):
    return lax.dot_general(left, right, (((0,), (0,)), ((), ())), preferred_element_type=F32)


class Ring:
    def __init__(self):
        me = lax.axis_index("tp")
        chip, core = me // 2, me % 2
        self.me, self.chip, self.core = me, chip, core
        self.chips = (chip, chip + 1 - 2 * (chip % 2), 3 - chip, (chip + 2) % 4)

    def at(self, slot):
        core = self.core if slot % 2 == 0 else 1 - self.core
        return self.chips[slot // 2] * 2 + core

    def at_traced(self, slot):
        relation, other = slot // 2, slot % 2
        own, near_t, near_f, opposite = self.chips
        chip = jnp.where(relation == 0, own, jnp.where(relation == 1, near_t, jnp.where(relation == 2, near_f, opposite)))
        return chip * 2 + (self.core + other) % 2

    def barrier(self):
        barrier = pltpu.get_barrier_semaphore()
        for slot in (1, 2, 3, 4, 5):
            pl.semaphore_signal(barrier, inc=1, device_id={"tp": self.at(slot)}, device_id_type=MESH)
        pl.semaphore_wait(barrier, 5)

    def copy(self, src, dst, send_sem, recv_sem, slot):
        return pltpu.make_async_remote_copy(src_ref=src, dst_ref=dst, send_sem=send_sem, recv_sem=recv_sem, device_id={"tp": self.at(slot)}, device_id_type=MESH)


PARTNER, SAME_T, OTHER_T, SAME_F, OTHER_F, SAME_O, OTHER_O = 1, 2, 3, 4, 5, 6, 7


def block_kernel(
    scale,
    y_one, y_two, dy_one, dy_two, w_up, w_down, w_qkv, w_out,
    x_two, dx_one, part_own, near_recv, d_att, o_pos, du_pos, wo_full, to_f, to_other_t,
    uc_seq, uc_two, uc_far, att_full, part_core, own_f, o_relay,
    u_all, c_all, up_all, down_all, acc, spare, part_keep, uc_own, att_own,
    load_sem, y_sem, x_sem, w_send, w_recv, uc_send, uc_recv, att_send, att_recv, a2a_send, a2a_recv, relay_recv, near_sem, two_sem,
    seq_sem, head_sem, wo_sem, core_send, core_recv, f_sem, far_sem, o_send, o_recv, du_send, du_recv, o_relay_recv, du_relay_recv, free_slot,
):
    ring = Ring()
    slabs, slab, hidden = acc.shape[1:]
    seq_len = slabs * slab
    half = seq_len // 2
    dim = w_out.shape[0]
    fours = slabs // 2

    def start(copies):
        for copy in copies:
            copy.start()

    rooms = (0, 1, 2, 3, 4, 5, 1, 3)

    def room(slot):
        return pl.ds(rooms[slot] * half, half)

    def weight_pair(src_slot, dst_slot, to, index):
        return [
            ring.copy(buf.at[room(src_slot)], buf.at[room(dst_slot)], w_send.at[index + which], w_recv.at[dst_slot, which], to)
            for which, buf in enumerate((up_all, down_all))
        ]

    w_own = weight_pair(0, 1, PARTNER, 0) + weight_pair(0, 2, SAME_T, 2) + weight_pair(0, 4, SAME_F, 4)
    w_near_t = weight_pair(2, 6, SAME_F, 6)
    w_near_t_core = weight_pair(2, 3, PARTNER, 8)
    w_near_f = weight_pair(4, 5, PARTNER, 10)
    w_far = weight_pair(6, 7, PARTNER, 12)

    def uc_pair(src_slot, dst_slot, to, index):
        return [ring.copy(buf.at[src_slot], buf.at[dst_slot], uc_send.at[index + which], uc_recv.at[dst_slot, which], to) for which, buf in enumerate((u_all, c_all))]

    uc_out = uc_pair(0, 2, SAME_T, 0) + uc_pair(0, 1, PARTNER, 2)
    uc_pass = uc_pair(2, 3, PARTNER, 4)

    def att(src, dst_slot, to, index):
        return ring.copy(src, att_full.at[dst_slot], att_send.at[index], att_recv.at[dst_slot], to)

    att_keep = pltpu.make_async_copy(att_own, att_full.at[0], load_sem.at[6])
    att_out = [att(att_own, 4, SAME_F, 0), att(att_own, 1, PARTNER, 1)]
    att_t, att_o = att(att_own, 2, SAME_T, 2), att(att_full.at[4], 6, SAME_T, 3)
    att_f_core, att_t_core, att_o_core = att(att_full.at[4], 5, PARTNER, 4), att(att_full.at[2], 3, PARTNER, 5), att(att_full.at[6], 7, PARTNER, 6)

    a2a_out = {slot: ring.copy(uc_own.at[slot], uc_seq.at[slot], a2a_send.at[slot], a2a_recv.at[slot], slot) for slot in (1, 2, 3, 4, 5)}
    a2a_out[SAME_O] = ring.copy(uc_own.at[SAME_O], uc_two.at[2], a2a_send.at[SAME_O], relay_recv.at[0], SAME_F)
    a2a_out[OTHER_O] = ring.copy(uc_own.at[OTHER_O], uc_two.at[3], a2a_send.at[OTHER_O], relay_recv.at[1], OTHER_F)
    a2a_pass = [ring.copy(uc_two.at[2 + index], uc_seq.at[SAME_O + index], a2a_send.at[8 + index], a2a_recv.at[SAME_O + index], SAME_T) for index in (0, 1)]
    uc_keep = pltpu.make_async_copy(uc_own.at[0], uc_seq.at[0], load_sem.at[4])
    two_out = ring.copy(uc_own.at[OTHER_T], uc_two.at[1], a2a_send.at[10], relay_recv.at[2], PARTNER)
    two_keep = pltpu.make_async_copy(uc_own.at[SAME_T], uc_two.at[0], two_sem.at[0])
    near = ring.copy(acc.at[0], near_recv, near_sem.at[0], near_sem.at[1], SAME_F)

    loads = [
        pltpu.make_async_copy(w_down, down_all.at[room(0)], load_sem.at[0]),
        pltpu.make_async_copy(w_up, uc_own.at[:, 0, :, pl.ds(0, half)], load_sem.at[1]),
        pltpu.make_async_copy(y_one, acc.at[0], load_sem.at[2]),
        pltpu.make_async_copy(dy_two, acc.at[1], load_sem.at[3]),
        pltpu.make_async_copy(w_out, att_own.at[pl.ds(3 * dim, dim)], load_sem.at[7]),
    ]
    qkv_loads = [pltpu.make_async_copy(w_qkv.at[part], uc_own.at[:, 1, :, pl.ds(part * dim, dim)], y_sem.at[0, part]) for part in range(3)]
    start(loads)
    start(qkv_loads)
    ring.barrier()
    loads[0].wait()
    start(w_own[1::2])
    loads[1].wait()
    for part in range(half // dim):
        up_all[pl.ds(part * dim, dim), :] = uc_own[:, 0, :, pl.ds(part * dim, dim)].reshape(hidden, dim).T
    start(w_own[0::2])
    loads[2].wait()
    loads[3].wait()

    def normalize(step, carry):
        rows = pl.ds(pl.multiple_of(step * slab, slab), slab)
        u_all[0, rows, :] = rms_norm(acc[0, step]).astype(BF16)
        c_all[0, rows, :] = acc[1, step].astype(BF16)
        acc[0, step] = jnp.zeros((slab, hidden), F32)
        acc[1, step] = jnp.zeros((slab, hidden), F32)
        return carry

    lax.fori_loop(0, slabs, normalize, 0)
    start(uc_out)
    for part in range(3):
        qkv_loads[part].wait()
        att_own[pl.ds(part * dim, dim), :] = uc_own[:, 1, :, pl.ds(part * dim, dim)].reshape(hidden, dim).T
    loads[4].wait()
    att_keep.start()

    def y_loads(step, buf):
        seq = ring.at_traced(7 - step)
        return [pltpu.make_async_copy(src.at[seq], spare.at[buf, which], y_sem.at[buf, which]) for which, src in enumerate((y_one, y_two, dy_one))]

    def x_stores(step, buf):
        seq = ring.at_traced(7 - step)
        return [pltpu.make_async_copy(spare.at[buf, 3 + which], dst.at[seq], x_sem.at[buf, which]) for which, dst in enumerate((x_two, dx_one))]

    def feed_forward(step, carry):
        slot = jnp.where(step == 3, 4, jnp.where(step == 4, 3, step))
        place = pl.ds(pl.multiple_of(jnp.where(step == 6, 1, jnp.where(step == 7, 3, slot)) * half, half), half)

        @pl.when(step >= 1)
        def _():
            for which, buf in enumerate((up_all, down_all)):
                ring.copy(buf.at[place], buf.at[place], w_send.at[0], w_recv.at[slot, which], PARTNER).wait_recv()

        @pl.when(step == 2)
        def _():
            pl.semaphore_wait(free_slot.at[0], 1)
            start(w_near_t)
            start(w_near_t_core)
            start(att_out)

        @pl.when(step == 3)
        def _():
            start(w_near_f)

        @pl.when(step == 6)
        def _():
            pl.semaphore_wait(free_slot.at[1], 1)
            start(w_far)

        @pl.when(step == 7)
        def _():
            start(y_loads(0, 0))

        def rows_step(part, carry):
            rows = pl.ds(pl.multiple_of(part * half, half), half)
            quarter = pl.ds(part * fours, fours)
            hidden_act, slope = gelu_and_slope(dot_nt(u_all[0, rows, :], up_all[place, :]))
            d_pre = (slope * dot_nt(c_all[0, rows, :], down_all[place, :])).astype(BF16)
            acc[0, quarter] += dot_nn(hidden_act.astype(BF16), down_all[place, :]).reshape(fours, slab, hidden)
            acc[1, quarter] += dot_nn(d_pre, up_all[place, :]).reshape(fours, slab, hidden)
            return carry

        lax.fori_loop(0, 2, rows_step, 0)

        @pl.when(step == 1)
        def _():
            pl.semaphore_signal(free_slot.at[0], inc=1, device_id={"tp": ring.at(SAME_F)}, device_id_type=MESH)

        @pl.when(step == 4)
        def _():
            pl.semaphore_signal(free_slot.at[1], inc=1, device_id={"tp": ring.at(PARTNER)}, device_id_type=MESH)

        return carry

    lax.fori_loop(0, 8, feed_forward, 0)

    def finish(step, carry):
        slot = 7 - step
        buf = step % 2
        seq = ring.at_traced(slot)
        for copy in y_loads(step, buf):
            copy.wait()

        @pl.when(step < 7)
        def _():
            start(y_loads(step + 1, 1 - buf))

        @pl.when(step >= 2)
        def _():
            for copy in x_stores(step - 2, buf):
                copy.wait()

        y_first = spare[buf, 0]
        x_second = spare[buf, 1] - acc[0, seq]
        dy_first = spare[buf, 2] + rms_back(y_first, acc[1, seq])
        spare[buf, 3] = x_second
        spare[buf, 4] = dy_first
        uc_own[slot, 0] = rms_norm(x_second).astype(BF16)
        uc_own[slot, 1] = dy_first.astype(BF16)
        acc[0, seq] = jnp.zeros((slab, hidden), F32)
        acc[1, seq] = jnp.zeros((slab, hidden), F32)
        start(x_stores(step, buf))
        return carry

    lax.fori_loop(0, 8, finish, 0)
    for slot in (7, 6, 5, 4, 3, 2, 1):
        a2a_out[slot].start()
    uc_keep.start()
    two_out.start()
    two_keep.start()
    for step in (6, 7):
        for copy in x_stores(step, step % 2):
            copy.wait()

    def gradients(step, carry):
        first = step // 8
        tokens = (step % 8) // 2
        place = pl.ds(pl.multiple_of((4 - 4 * first) * half, half), half)

        @pl.when((step == 2) | (step == 4) | (step == 6))
        def _():
            for which, buf in enumerate((u_all, c_all)):
                ring.copy(buf.at[tokens], buf.at[tokens], uc_send.at[0], uc_recv.at[tokens, which], PARTNER).wait_recv()

        @pl.when(step == 4)
        def _():
            start(uc_pass)
            for index in (0, 1):
                a2a_out[SAME_O + index].wait_recv()
            start(a2a_pass)

        @pl.when(step == 8)
        def _():
            near.start()
            att_out[0].wait_recv()
            att_f_core.start()
            att_t.start()
            att_o.start()

        rows = pl.ds(pl.multiple_of((step % 2) * half, half), half)
        u_part, c_part = u_all[tokens, rows, :], c_all[tokens, rows, :]
        hidden_act, slope = gelu_and_slope(dot_nt(up_all[place, :], u_part))
        d_pre = (slope * dot_nt(down_all[place, :], c_part)).astype(BF16)
        acc[first, pl.ds(0, fours)] += dot_nn(d_pre, u_part).reshape(fours, slab, hidden)
        acc[first, pl.ds(fours, fours)] += dot_nn(hidden_act.astype(BF16), c_part).reshape(fours, slab, hidden)
        return carry

    lax.fori_loop(0, 16, gradients, 0)
    out_own = pltpu.make_async_copy(acc.at[1], part_own, load_sem.at[1])
    out_own.start()
    for copy in w_own + w_near_t + w_near_t_core + w_near_f + w_far + uc_out + uc_pass:
        copy.wait_send()

    def relation_of(step):
        base = step % 4
        return jnp.where(base == 0, 2, jnp.where(base == 3, 3, base - 1))

    def qkv_rows(buf):
        return pl.ds(pl.multiple_of(buf * 6 * dim, 2 * dim), 6 * dim)

    def wo_rows(buf):
        return pl.ds(pl.multiple_of(12 * dim + buf * 2 * dim, 2 * dim), 2 * dim)

    def head_loads(relation, buf):
        copies = []
        for index in (0, 1):
            head = att_full.at[relation * 2 + 1 - index]
            first, second = (pl.ds(pl.multiple_of(base + index * size, dim), size) for base, size in ((buf * 6 * dim, 3 * dim), (12 * dim + buf * 2 * dim, dim)))
            copies.append(pltpu.make_async_copy(head.at[pl.ds(0, 3 * dim)], up_all.at[first], head_sem.at[buf, index, 0]))
            copies.append(pltpu.make_async_copy(head.at[pl.ds(3 * dim, dim)], up_all.at[second], head_sem.at[buf, index, 1]))
        return copies

    def rows_of(slot):
        return pl.ds(slot * slab, slab)

    def seq_loads(seq, src, src_slot, slot):
        return [pltpu.make_async_copy(src.at[src_slot, which], u_all.at[2 * seq + which, rows_of(slot)], seq_sem.at[2 * seq + which, slot]) for which in (0, 1)]

    seq_own = [copy for slot in range(8) for copy in seq_loads(0, uc_seq, slot, slot)]
    seq_two = [copy for slot in range(4) for copy in seq_loads(1, uc_two, slot, slot)]
    seq_far = [copy for slot in range(4) for copy in seq_loads(1, uc_far, slot, 4 + slot)]
    uc_to_t = [ring.copy(uc_seq.at[pl.ds(2 * slot, 2)], uc_far.at[pl.ds(slot, 2)], far_sem.at[slot], far_sem.at[slot + 1], SAME_T) for slot in (0, 2)]
    core_copies = [ring.copy(spare.at[index, pl.ds(0, 4)], part_core.at[index], core_send.at[index], core_recv.at[index], PARTNER) for index in (0, 1)]
    f_copy = ring.copy(part_keep.at[0], own_f, f_sem.at[0], f_sem.at[1], SAME_F)
    core_loads = [pltpu.make_async_copy(part_core.at[index], acc.at[0, pl.ds(0, 4)], load_sem.at[2]) for index in (0, 1)]
    own_f_load = pltpu.make_async_copy(own_f, acc.at[0, pl.ds(4, 4)], load_sem.at[3])

    o_src = c_all.at[0]
    o_out = [
        ring.copy(o_src.at[rows_of(SAME_O)], o_relay.at[0], o_send.at[6], o_relay_recv.at[0], SAME_T),
        ring.copy(o_src.at[rows_of(OTHER_O)], o_relay.at[1], o_send.at[7], o_relay_recv.at[1], SAME_F),
    ] + [ring.copy(o_src.at[rows_of(slot)], o_pos.at[ring.me], o_send.at[slot], o_recv.at[slot], slot) for slot in (5, 4, 3, 2, 1)]
    o_pass = [
        ring.copy(o_relay.at[0], o_pos.at[ring.at(SAME_T)], o_send.at[8], o_recv.at[SAME_O], SAME_F),
        ring.copy(o_relay.at[1], o_pos.at[ring.at(SAME_F)], o_send.at[9], o_recv.at[OTHER_O], OTHER_T),
    ]
    o_keep = pltpu.make_async_copy(o_src.at[rows_of(0)], o_pos.at[ring.me], o_send.at[0])

    late = slab - to_f.shape[0] % slab
    early = {slot: late if slot in (SAME_F, OTHER_T) else slab for slot in range(1, 6)}
    du_out = [
        ring.copy(acc.at[1, SAME_O], to_f.at[pl.ds(0, slab)], du_send.at[6], du_relay_recv.at[0], SAME_T),
        ring.copy(acc.at[1, OTHER_O], to_other_t.at[pl.ds(0, slab)], du_send.at[7], du_relay_recv.at[1], SAME_F),
    ] + [ring.copy(acc.at[1, slot, pl.ds(0, early[slot])], du_pos.at[ring.me, pl.ds(0, early[slot])], du_send.at[slot], du_recv.at[slot], slot) for slot in (5, 4, 3, 2, 1)]
    du_keep = pltpu.make_async_copy(acc.at[1, 0], du_pos.at[ring.me], du_send.at[0])
    du_late = [
        pltpu.make_async_copy(acc.at[1, slot, pl.ds(late, slab - late)], dst.at[pl.ds(slab, slab - late)], du_send.at[sem])
        for slot, dst, sem in ((SAME_F, to_f, 8), (OTHER_T, to_other_t, 9))
    ]

    att_f_core.wait_recv()
    att_keep.wait()
    att_out[1].wait_recv()
    start(head_loads(2, 0))
    spare[...] = jnp.zeros_like(spare)
    part_keep[...] = jnp.zeros_like(part_keep)
    uc_keep.wait()
    for slot in range(1, 8):
        ring.copy(uc_own.at[slot], uc_seq.at[slot], a2a_send.at[0], a2a_recv.at[slot], PARTNER).wait_recv()
    start(seq_own)
    start(uc_to_t)
    two_out.wait_recv()
    two_keep.wait()
    start(seq_two)
    out_own.wait()
    acc[1] = jnp.zeros(acc.shape[1:], F32)
    for copy in seq_own:
        copy.wait()

    def chip_step(step, carry):
        buf = step % 2
        seq = step // 4
        relation = relation_of(step)

        @pl.when(step == 4)
        def _():
            for copy in uc_to_t:
                copy.wait_recv()
            start(seq_far)
            for copy in seq_two + seq_far:
                copy.wait()

        for copy in head_loads(0, buf):
            copy.wait()

        @pl.when((step == 0) | (step == 3) | (step == 4))
        def _():
            start(head_loads(relation_of(step + 1), 1 - buf))

        heads = [ring.at_traced(relation * 2 + other) for other in (1, 0)]
        wo_copies = [
            pltpu.make_async_copy(up_all.at[pl.ds(pl.multiple_of(12 * dim + (2 * buf + index) * dim, dim), dim)], wo_full.at[head], wo_sem.at[index])
            for index, head in enumerate(heads)
        ]
        start(wo_copies)
        c_all[2, :, pl.ds(0, 6 * dim)] = dot_nt(u_all[2 * seq], up_all[qkv_rows(buf), :]).astype(BF16)
        c_all[2, :, pl.ds(6 * dim, 2 * dim)] = dot_nt(u_all[2 * seq + 1], up_all[wo_rows(buf), :]).astype(BF16)
        for index, head in enumerate(heads):
            columns = pl.ds(pl.multiple_of(head * dim, dim), dim)
            own = pl.ds(index * 3 * dim, 3 * dim)
            query, key, value = (c_all[2, :, pl.ds((index * 3 + part) * dim, dim)] for part in range(3))
            d_out = c_all[2, :, pl.ds((6 + index) * dim, dim)]
            scores = dot_nt(query, key) * (scale * LOG2_E)
            grown = jnp.exp2(scores - jnp.max(scores, axis=-1, keepdims=True))
            prob = grown * (1.0 / jnp.sum(grown, axis=-1, keepdims=True))
            prob_b = prob.astype(BF16)
            c_all[seq, :, columns] = dot_nn(prob_b, value).astype(BF16)
            d_prob = dot_nt(d_out, value)
            d_score = (prob * (d_prob - jnp.sum(d_prob * prob, axis=-1, keepdims=True)) * scale).astype(BF16)
            c_all[3, :, pl.ds(index * 3 * dim, dim)] = dot_nn(d_score, key).astype(BF16)
            c_all[3, :, pl.ds((index * 3 + 1) * dim, dim)] = dot_nn(query.T, d_score).T.astype(BF16)
            c_all[3, :, pl.ds((index * 3 + 2) * dim, dim)] = dot_nn(d_out.T, prob_b).T.astype(BF16)
            @pl.when((step < 2) | (step >= 4))
            def _():
                dst = (spare, part_keep)[index].at[buf]
                dst[pl.ds(0, 3)] += dot_tn(c_all[3, :, own], u_all[2 * seq]).reshape(3, dim, hidden)
                dst[3] += dot_tn(c_all[seq, :, columns], u_all[2 * seq + 1])

            if index == 0:
                @pl.when(step == 1)
                def _():
                    att_t.wait_recv()
                    att_t_core.start()

                @pl.when(step == 4)
                def _():
                    core_copies[0].start()

                @pl.when(step == 5)
                def _():
                    core_copies[1].start()

        @pl.when(step < 4)
        def _():
            def du_tile(part, carry):
                rows = pl.ds(pl.multiple_of(part * half, half), half)
                acc[1, pl.ds(part * fours, fours)] += dot_nn(c_all[3, rows, pl.ds(0, 6 * dim)], up_all[qkv_rows(buf), :]).reshape(fours, slab, hidden)
                return carry

            lax.fori_loop(0, 2, du_tile, 0)

        @pl.when(step == 1)
        def _():
            att_t_core.wait_recv()
            start(head_loads(1, 0))

        @pl.when(step == 2)
        def _():
            att_o.wait_recv()
            att_o_core.start()
            att_o_core.wait_recv()
            start(head_loads(3, 1))

        @pl.when(step == 3)
        def _():
            start(o_out)
            start(du_out)
            start(du_late)
            o_keep.start()
            du_keep.start()

        @pl.when(step == 4)
        def _():
            near.wait_send()
            core_copies[0].wait_recv()
            core_loads[0].start()
            core_loads[0].wait()
            part_keep[0] += acc[0, pl.ds(0, 4)]
            f_copy.start()

        for copy in wo_copies:
            copy.wait()
        return carry

    lax.fori_loop(0, 6, chip_step, 0)
    for copy in o_out[:2]:
        copy.wait_recv()
    start(o_pass)
    core_copies[1].wait_recv()
    core_loads[1].start()
    core_loads[1].wait()
    part_keep[1] += acc[0, pl.ds(0, 4)]
    for copy in du_out[2:]:
        copy.wait_recv()
    for slot in range(1, 8):
        ring.copy(o_pos.at[0], o_pos.at[ring.at(slot)], near_sem.at[0], o_recv.at[slot], PARTNER).wait_recv()
    for copy in du_out[:2]:
        copy.wait_recv()
    near.wait_recv()
    f_copy.wait_recv()
    own_f_load.start()
    own_f_load.wait()
    part_keep[1] += acc[0, pl.ds(4, 4)]
    d_att_copy = pltpu.make_async_copy(part_keep.at[1], d_att, load_sem.at[0])
    d_att_copy.start()

    sends = att_out + [att_t, att_o, att_f_core, att_t_core, att_o_core] + list(a2a_out.values()) + a2a_pass + [two_out]
    for copy in sends + o_out + du_out + o_pass + uc_to_t + core_copies + [f_copy]:
        copy.wait_send()
    for copy in du_late:
        copy.wait()
    o_keep.wait()
    du_keep.wait()
    d_att_copy.wait()


def block_call(y_one, y_two, dy_one, dy_two, w_up, w_down, w_qkv, w_out):
    slabs, slab, hidden = y_one.shape
    tokens = slabs * slab
    ffn = w_down.shape[0]
    dim = w_out.shape[0]
    any_spec = pl.BlockSpec(memory_space=pl.ANY)
    dma, vmem, wide, narrow = pltpu.SemaphoreType.DMA, pltpu.VMEM, F32, BF16
    results = [
        ((slabs, slab, hidden), wide), ((slabs, slab, hidden), wide), ((slabs, slab, hidden), wide), ((slabs, slab, hidden), wide),
        ((4, dim, hidden), wide), ((slabs, slab, hidden), narrow), ((slabs, slab, hidden), wide), ((8, dim, hidden), narrow),
        ((slab + slab // 2, hidden), wide), ((slab + slab // 2, hidden), wide),
    ]
    landing = [
        ((8, 2, slab, hidden), narrow), ((4, 2, slab, hidden), narrow), ((4, 2, slab, hidden), narrow), ((8, 4 * dim, hidden), narrow),
        ((2, 4, dim, hidden), wide), ((4, dim, hidden), wide), ((2, slab, hidden), narrow),
    ]
    scratch = [
        vmem((4, tokens, hidden), BF16), vmem((4, tokens, hidden), BF16), vmem((6 * ffn, hidden), BF16), vmem((6 * ffn, hidden), BF16),
        vmem((2, slabs, slab, hidden), F32), vmem((2, 5, slab, hidden), F32), vmem((2, 4, dim, hidden), F32),
        vmem((8, 2, slab, hidden), BF16), vmem((4 * dim, hidden), BF16),
        dma((8,)), dma((2, 3)), dma((2, 2)), dma((14,)), dma((8, 2)), dma((6,)), dma((4, 2)), dma((7,)), dma((8,)), dma((11,)), dma((8,)), dma((3,)), dma((2,)), dma((2,)),
        dma((4, 8)), dma((2, 2, 2)), dma((2,)), dma((2,)), dma((2,)), dma((2,)), dma((4,)), dma((10,)), dma((8,)), dma((10,)), dma((8,)), dma((2,)), dma((2,)),
        pltpu.SemaphoreType.REGULAR((2,)),
    ]
    return pl.pallas_call(
        functools.partial(block_kernel, dim ** -0.5),
        out_shape=[jax.ShapeDtypeStruct(shape, dtype) for shape, dtype in results + landing],
        in_specs=[any_spec] * 8,
        out_specs=[any_spec] * (len(results) + len(landing)),
        scratch_shapes=scratch,
        compiler_params=pltpu.CompilerParams(collective_id=0, has_side_effects=True, vmem_limit_bytes=VMEM_LIMIT),
        cost_estimate=pl.CostEstimate(flops=120 * 10**9, bytes_accessed=128 * 2**20, transcendentals=0),
        name="block",
    )(y_one, y_two, dy_one, dy_two, w_up.reshape(8, hidden // 8, ffn), w_down, w_qkv.reshape(3, 8, hidden // 8, dim), w_out)[: len(results)]


def finish_kernel(
    y_one, o_pos, wo_full, x_two, dx_one, dy_two, du_pos, part_own, near_recv, d_att,
    x_one_out, x_two_out, dx_one_out, dx_two_out, dw_up, dw_down, dw_qkv, dw_out,
    y_buf, o_buf, wo_buf, x_buf, dx_buf, dy_buf, du_buf, own_buf, near_buf, att_buf, up_out, qkv_out, load_sem, store_sem,
):
    tokens = y_buf.shape[0]
    dim = wo_buf.shape[0] // 8
    chunk = 256
    chunks = [pl.ds(index * chunk, chunk) for index in range(tokens // chunk)]

    def pieces(src, dst, sem, row):
        return [pltpu.make_async_copy(src.at[rows], dst.at[rows], sem.at[row, index]) for index, rows in enumerate(chunks)]

    def whole(src, dst, sem, row):
        return pltpu.make_async_copy(src, dst, sem.at[row, 0])

    ring = Ring()
    slab = tokens // 8
    sizes = (slab, slab, slab, slab // 2, slab // 2, slab)
    slots = [pl.ds(pl.multiple_of(ring.at(slot) * slab, slab), size) for slot, size in enumerate(sizes)]

    def slabs(src, dst, sem, row):
        return [pltpu.make_async_copy(src.at[rows], dst.at[rows], sem.at[row, index]) for index, rows in enumerate(slots)]

    x_in, dy_in, du_in = pieces(x_two, x_buf, load_sem, 0), slabs(dy_two, dy_buf, load_sem, 1), slabs(du_pos, du_buf, load_sem, 2)
    y_in, o_in = pieces(y_one, y_buf, load_sem, 3), pieces(o_pos, o_buf, load_sem, 4)
    wo_in, dx_in = whole(wo_full, wo_buf, load_sem, 5), whole(dx_one, dx_buf, load_sem, 6)
    own_in, near_in, att_in = whole(part_own, own_buf, load_sem, 7), whole(near_recv, near_buf, load_sem, 8), whole(d_att, att_buf, load_sem, 9)
    for group in (x_in, *zip(dy_in, du_in)):
        for copy in group:
            copy.start()
    for copy in (dx_in, wo_in):
        copy.start()
    for group in zip(y_in, o_in):
        for copy in group:
            copy.start()
    for copy in (own_in, near_in, att_in):
        copy.start()

    x_store, dx2_store, x1_store = pieces(x_buf, x_two_out, store_sem, 0), slabs(dy_buf, dx_two_out, store_sem, 1), pieces(y_buf, x_one_out, store_sem, 2)
    for index in range(len(chunks)):
        x_in[index].wait()
        x_store[index].start()
    for index, rows in enumerate(slots):
        dy_in[index].wait()
        du_in[index].wait()
        dy_buf[rows, :] += rms_back(x_buf[rows, :], du_buf[rows, :])
        dx2_store[index].start()
    dx_in.wait()
    dx_store = whole(dx_buf, dx_one_out, store_sem, 3)
    dx_store.start()
    wo_in.wait()
    for index, rows in enumerate(chunks):
        y_in[index].wait()
        o_in[index].wait()
        y_buf[rows, :] -= dot_nn(o_buf[rows, :], wo_buf[...])
        x1_store[index].start()
    own_in.wait()
    near_in.wait()
    ffn = up_out.shape[1]
    own_buf[pl.ds(ffn, ffn), :] += near_buf[pl.ds(ffn, ffn), :]
    down_store = whole(own_buf.at[pl.ds(ffn, ffn)], dw_down, store_sem, 7)
    down_store.start()
    for part in range(up_out.shape[0] // ffn):
        columns = pl.ds(part * ffn, ffn)
        up_out[columns, :] = (own_buf[pl.ds(0, ffn), columns] + near_buf[pl.ds(0, ffn), columns]).T
    up_store = whole(up_out, dw_up, store_sem, 4)
    up_store.start()
    att_in.wait()
    for part in range(3):
        qkv_out[pl.ds(part, tokens, stride=3), 0, :] = att_buf[pl.ds(part * dim, dim), :].T
    qkv_store = whole(qkv_out, dw_qkv, store_sem, 5)
    qkv_store.start()
    out_store = whole(att_buf.at[pl.ds(3 * dim, dim)], dw_out, store_sem, 6)
    out_store.start()
    for copy in x_store + dx2_store + x1_store + [dx_store, up_store, qkv_store, out_store, down_store]:
        copy.wait()


def finish_call(y_one, o_pos, wo_full, x_two, dx_one, dy_two, du_pos, part_own, near_recv, d_att):
    tokens, hidden = y_one.shape
    ffn = part_own.shape[0] // 2
    dim = d_att.shape[0] // 4
    any_spec = pl.BlockSpec(memory_space=pl.ANY)
    dma, vmem = pltpu.SemaphoreType.DMA, pltpu.VMEM
    state = (tokens, hidden)
    out_shape = [jax.ShapeDtypeStruct(shape, F32) for shape in (state, state, state, state, (hidden, ffn), (ffn, hidden), (3 * hidden, 1, dim), (dim, hidden))]
    scratch = [
        vmem(state, F32), vmem(state, BF16), vmem((hidden, hidden), BF16), vmem(state, F32), vmem(state, F32), vmem(state, F32), vmem(state, F32),
        vmem(part_own.shape, F32), vmem(part_own.shape, F32), vmem(d_att.shape, F32), vmem((hidden, ffn), F32), vmem((3 * hidden, 1, dim), F32),
        dma((10, 6)), dma((8, 6)),
    ]
    return pl.pallas_call(
        finish_kernel,
        out_shape=out_shape,
        in_specs=[any_spec] * 10,
        out_specs=[any_spec] * 8,
        scratch_shapes=scratch,
        compiler_params=pltpu.CompilerParams(vmem_limit_bytes=VMEM_LIMIT),
        cost_estimate=pl.CostEstimate(flops=2 * 10**9, bytes_accessed=52 * 2**20, transcendentals=0),
        name="finish",
    )(y_one, o_pos, wo_full, x_two, dx_one, dy_two, du_pos, part_own, near_recv, d_att)


def last_kernel(x_two, dy_two, du_far, du_far_other, dx_two_in, dx_two_out, x_buf, dy_buf, du_buf, load_sem, store_sem):
    ring = Ring()
    slab = x_buf.shape[1]
    half = slab // 2
    loads, stores, sizes = [], [], (slab, slab, half, half)
    for index, (slot, du, skip) in enumerate(((SAME_O, du_far, 0), (OTHER_O, du_far_other, 0), (SAME_F, du_far, half), (OTHER_T, du_far_other, half))):
        size = sizes[index]
        rows = pl.ds(pl.multiple_of(ring.at(slot) * slab + skip, half), size)
        sources = ((x_two.at[rows], x_buf), (dy_two.at[rows], dy_buf), (du.at[pl.ds(2 * skip, size)], du_buf))
        loads.append([pltpu.make_async_copy(src, dst.at[index, pl.ds(0, size)], load_sem.at[index, which]) for which, (src, dst) in enumerate(sources)])
        stores.append(pltpu.make_async_copy(dy_buf.at[index, pl.ds(0, size)], dx_two_out.at[rows], store_sem.at[index]))
    for copies in loads:
        for copy in copies:
            copy.start()
    for index, copies in enumerate(loads):
        for copy in copies:
            copy.wait()
        rows = pl.ds(0, sizes[index])
        dy_buf[index, rows, :] += rms_back(x_buf[index, rows, :], du_buf[index, rows, :])
        stores[index].start()
    for copy in stores:
        copy.wait()


def last_call(x_two, dy_two, du_far, du_far_other, dx_two):
    tokens, hidden = x_two.shape
    any_spec = pl.BlockSpec(memory_space=pl.ANY)
    buf = pltpu.VMEM((4, tokens // 8, hidden), F32)
    return pl.pallas_call(
        last_kernel,
        out_shape=jax.ShapeDtypeStruct(dx_two.shape, F32),
        in_specs=[any_spec] * 5,
        out_specs=any_spec,
        input_output_aliases={4: 0},
        scratch_shapes=[buf, buf, buf, pltpu.SemaphoreType.DMA((4, 3)), pltpu.SemaphoreType.DMA((4,))],
        cost_estimate=pl.CostEstimate(flops=10**6, bytes_accessed=4 * 2**20, transcendentals=0),
        name="last",
    )(x_two, dy_two, du_far, du_far_other, dx_two)


def local_backward(y_one, y_two, dy_one, dy_two, w_qkv, w_out, w_up, w_down):
    hidden = y_one.shape[2]
    _, _, _, parts, dim = w_qkv.shape
    qkv_parts = jnp.swapaxes(w_qkv[0, :, 0], 0, 1)
    results = block_call(y_one, y_two, dy_one, dy_two, w_up[0], w_down[0], qkv_parts, w_out[0, 0])
    x_two, dx_one, part_own, near_recv, d_att, o_pos, du_pos, wo_full = (tensor.reshape(-1, hidden) for tensor in results[:8])
    devices = range(lax.axis_size("tp"))
    to_f = [(device, (3 - device // 2) * 2 + device % 2) for device in devices]
    to_other_t = [(device, 4 * (device // 4) + 3 - device % 4) for device in devices]
    du_far, du_far_other = lax.ppermute(results[8], "tp", to_f), lax.ppermute(results[9], "tp", to_other_t)
    y_flat, dy_flat = y_one.reshape(-1, hidden), dy_two.reshape(-1, hidden)
    *states, dw_up, dw_down, dw_qkv, dw_out = finish_call(y_flat, o_pos, wo_full, x_two, dx_one, dy_flat, du_pos, part_own, near_recv, d_att)
    states[3] = last_call(x_two, dy_flat, du_far, du_far_other, states[3])
    states = [tensor.reshape(y_one.shape) for tensor in states]
    return (*states, dw_qkv.reshape(1, hidden, 1, parts, dim), dw_out[None, None], dw_up[None], dw_down[None])


def solution(mesh):
    state_spec = P("dp", "tp", None)
    in_specs = (state_spec, state_spec, state_spec, state_spec, P(None, None, "tp", None, None), P(None, "tp", None, None), P(None, None, "tp"), P(None, "tp", None))
    out_specs = (state_spec, state_spec, state_spec, state_spec, P("dp", None, "tp", None, None), P("dp", "tp", None, None), P("dp", None, "tp"), P("dp", "tp", None))
    return jax.shard_map(local_backward, mesh=mesh, in_specs=in_specs, out_specs=out_specs, check_vma=False)
```

time: 385 us -> 383 us (level)
    pallas_call x2 -> x1, Pallas kernels: 361 us -> 357 us  [block_call(): pl.pallas_call(functools.partial(block_kernel, dim ** (-0.5)), out_shape=...]
  transfers between devices with their start and end apart: 2 -> 2, of which waited for: 1 -> 0; matrix products, arithmetic and copies ran while one was open for 0% -> 0% of each run, Pallas kernels for 5% -> 5%
where the time goes in v11:
time: 383 us
  Pallas kernels  380 us (99%)
    pallas_call x1, Pallas kernels, block_call(): pl.pallas_call(functools.partial(block_kernel, dim ** (-0.5)), out_shape=...  357 us
    pallas_call x1, Pallas kernels, finish_call(): pl.pallas_call(finish_kernel, out_shape=out_shape, in_specs=[any_spec] *...  19.6 us
  transfers between devices with their start and end apart: 2, of which 0 were waited for; matrix products, arithmetic and copies ran while one was open for 0% of the time, Pallas kernels for 5%

profile of v11, /device:TPU:112, one launch (start us, length us, event | category | flops | bytes accessed | tf_op | source)
XLA Modules:
  0.0 383.0 jit_solution(16986038613654190655)
XLA Ops:
  0.6 357.2 %block.1 = (f32[8,128,1024]{2,1,0:T(8,128)}, f32[8,128,1024]{2,1,0:T(8,128)}, f32[8,128,1024]{2,1,0:T(8,128)}, f32[8,128,1024]{2,1,0:T(8,128)}, f32[4,128,1024]{...) custom-call(f32[8,128,1024]{2,1,0:T(8,128)} %y_one.1, ...), custom_call_target="tpu_custom_call" | custom-call | flops 120000004096 | bytes 134217728 | tf_op jit(solution)/shard_map/block/pallas_call | solution.py:551
  357.9 2.0 collective-permute-start
  359.8 0.0 collective-permute-start.1
  359.8 19.6 %finish.1 = (f32[1024,1024]{1,0:T(8,128)}, f32[1024,1024]{1,0:T(8,128)}, f32[1024,1024]{1,0:T(8,128)}, f32[1024,1024]{1,0:T(8,128)}, f32[1024,512]{1,0:T(8,128)}...) custom-call(f32[1024,1024]{1,0:T(8,128)} %bitcast.32, bf16[1024,1024]{1,0:T(8,128)(2,1)} %bitcast.39, ...), custom_call_target="tpu_custom_call" | custom-call | flops 2000000000 | bytes 54525952 | tf_op jit(solution)/shard_map/finish/pallas_call | solution.py:655
  379.5 0.0 collective-permute-done.du_far
  379.5 0.0 collective-permute-done.1.du_far_other
  379.5 3.3 last.1
Async XLA Ops:
  357.9 21.6 %collective-permute-start = (f32[192,1024]{1,0:T(8,128)}, f32[192,1024]{1,0:T(8,128)}, u32[]{:S(2)}, u32[]{:S(2)}) collective-permute-start(f32[192,1024]{1,0:T(8,128)} %get-tuple-element.37), channel_id=1, source_target_pairs={{0,6},{1,7},{2,4},{3,5},{4,2},{5,3},{6,0},{7,1},{8,14},{9,15},{10,... | collective-permute-start | bytes 2359304 | tf_op jit(solution)/shard_map/ppermute | solution.py:716
  359.8 19.6 %collective-permute-start.1 = (f32[192,1024]{1,0:T(8,128)}, f32[192,1024]{1,0:T(8,128)}, u32[]{:S(2)}, u32[]{:S(2)}) collective-permute-start(f32[192,1024]{1,0:T(8,128)} %get-tuple-element.38), channel_id=1, source_target_pairs={{0,3},{1,2},{2,1},{3,0},{4,7},{5,6},{6,5},{7,4},{8,11},{9,10},{10,... | collective-permute-start | bytes 2359304 | tf_op jit(solution)/shard_map/ppermute | solution.py:716

commit v12 on v11

--- a/solution.py
+++ b/solution.py
@@ -9,6 +9,7 @@
 
 RMS_EPS = 1e-6
 LOG2_E = 1.4426950408889634
+LATE_ROWS = 80
 MESH = pl.DeviceIdType.MESH
 BF16, F32 = jnp.bfloat16, jnp.float32
 VMEM_LIMIT = 64 * 1024 * 1024 - 65536
@@ -82,7 +83,7 @@
     scale,
     y_one, y_two, dy_one, dy_two, w_up, w_down, w_qkv, w_out,
     x_two, dx_one, part_own, near_recv, d_att, o_pos, du_pos, wo_full, to_f, to_other_t,
-    uc_seq, uc_two, uc_far, att_full, part_core, own_f, o_relay,
+    uc_seq, uc_two, att_full, o_relay,
     u_all, c_all, up_all, down_all, acc, spare, part_keep, uc_own, att_own,
     load_sem, y_sem, x_sem, w_send, w_recv, uc_send, uc_recv, att_send, att_recv, a2a_send, a2a_recv, relay_recv, near_sem, two_sem,
     seq_sem, head_sem, wo_sem, core_send, core_recv, f_sem, far_sem, o_send, o_recv, du_send, du_recv, o_relay_recv, du_relay_recv, free_slot,
@@ -97,6 +98,9 @@
     def start(copies):
         for copy in copies:
             copy.start()
+
+    def say_free(index, to):
+        pl.semaphore_signal(free_slot.at[index], inc=1, device_id={"tp": ring.at(to)}, device_id_type=MESH)
 
     rooms = (0, 1, 2, 3, 4, 5, 1, 3)
 
@@ -224,11 +228,11 @@
 
         @pl.when(step == 1)
         def _():
-            pl.semaphore_signal(free_slot.at[0], inc=1, device_id={"tp": ring.at(SAME_F)}, device_id_type=MESH)
+            say_free(0, SAME_F)
 
         @pl.when(step == 4)
         def _():
-            pl.semaphore_signal(free_slot.at[1], inc=1, device_id={"tp": ring.at(PARTNER)}, device_id_type=MESH)
+            say_free(1, PARTNER)
 
         return carry
 
@@ -310,6 +314,7 @@
     out_own.start()
     for copy in w_own + w_near_t + w_near_t_core + w_near_f + w_far + uc_out + uc_pass:
         copy.wait_send()
+    say_free(2, SAME_T)
 
     def relation_of(step):
         base = step % 4
@@ -338,12 +343,13 @@
 
     seq_own = [copy for slot in range(8) for copy in seq_loads(0, uc_seq, slot, slot)]
     seq_two = [copy for slot in range(4) for copy in seq_loads(1, uc_two, slot, slot)]
-    seq_far = [copy for slot in range(4) for copy in seq_loads(1, uc_far, slot, 4 + slot)]
-    uc_to_t = [ring.copy(uc_seq.at[pl.ds(2 * slot, 2)], uc_far.at[pl.ds(slot, 2)], far_sem.at[slot], far_sem.at[slot + 1], SAME_T) for slot in (0, 2)]
-    core_copies = [ring.copy(spare.at[index, pl.ds(0, 4)], part_core.at[index], core_send.at[index], core_recv.at[index], PARTNER) for index in (0, 1)]
-    f_copy = ring.copy(part_keep.at[0], own_f, f_sem.at[0], f_sem.at[1], SAME_F)
-    core_loads = [pltpu.make_async_copy(part_core.at[index], acc.at[0, pl.ds(0, 4)], load_sem.at[2]) for index in (0, 1)]
-    own_f_load = pltpu.make_async_copy(own_f, acc.at[0, pl.ds(4, 4)], load_sem.at[3])
+    uc_to_t = [
+        ring.copy(uc_seq.at[slot, which], u_all.at[2 + which, rows_of(4 + index)], far_sem.at[0, 2 * index + which], far_sem.at[1, 2 * index + which], SAME_T)
+        for index, slot in enumerate((0, 1, 4, 5))
+        for which in (0, 1)
+    ]
+    core_copies = [ring.copy(spare.at[index, pl.ds(0, 4)], acc.at[0, pl.ds(0, 4)], core_send.at[index], core_recv.at[index], PARTNER) for index in (0, 1)]
+    f_copy = ring.copy(part_keep.at[0], acc.at[0, pl.ds(4, 4)], f_sem.at[0], f_sem.at[1], SAME_F)
 
     o_src = c_all.at[0]
     o_out = [
@@ -356,7 +362,7 @@
     ]
     o_keep = pltpu.make_async_copy(o_src.at[rows_of(0)], o_pos.at[ring.me], o_send.at[0])
 
-    late = slab - to_f.shape[0] % slab
+    late = slab - LATE_ROWS
     early = {slot: late if slot in (SAME_F, OTHER_T) else slab for slot in range(1, 6)}
     du_out = [
         ring.copy(acc.at[1, SAME_O], to_f.at[pl.ds(0, slab)], du_send.at[6], du_relay_recv.at[0], SAME_T),
@@ -378,6 +384,7 @@
     for slot in range(1, 8):
         ring.copy(uc_own.at[slot], uc_seq.at[slot], a2a_send.at[0], a2a_recv.at[slot], PARTNER).wait_recv()
     start(seq_own)
+    pl.semaphore_wait(free_slot.at[2], 1)
     start(uc_to_t)
     two_out.wait_recv()
     two_keep.wait()
@@ -394,11 +401,13 @@
 
         @pl.when(step == 4)
         def _():
+            near.wait_send()
+            say_free(3, SAME_F)
+            say_free(4, PARTNER)
+            for copy in seq_two:
+                copy.wait()
             for copy in uc_to_t:
                 copy.wait_recv()
-            start(seq_far)
-            for copy in seq_two + seq_far:
-                copy.wait()
 
         for copy in head_loads(0, buf):
             copy.wait()
@@ -444,10 +453,12 @@
 
                 @pl.when(step == 4)
                 def _():
+                    pl.semaphore_wait(free_slot.at[4], 1)
                     core_copies[0].start()
 
                 @pl.when(step == 5)
                 def _():
+                    pl.semaphore_wait(free_slot.at[4], 1)
                     core_copies[1].start()
 
         @pl.when(step < 4)
@@ -481,11 +492,10 @@
 
         @pl.when(step == 4)
         def _():
-            near.wait_send()
             core_copies[0].wait_recv()
-            core_loads[0].start()
-            core_loads[0].wait()
             part_keep[0] += acc[0, pl.ds(0, 4)]
+            say_free(4, PARTNER)
+            pl.semaphore_wait(free_slot.at[3], 1)
             f_copy.start()
 
         for copy in wo_copies:
@@ -497,8 +507,6 @@
         copy.wait_recv()
     start(o_pass)
     core_copies[1].wait_recv()
-    core_loads[1].start()
-    core_loads[1].wait()
     part_keep[1] += acc[0, pl.ds(0, 4)]
     for copy in du_out[2:]:
         copy.wait_recv()
@@ -508,8 +516,6 @@
         copy.wait_recv()
     near.wait_recv()
     f_copy.wait_recv()
-    own_f_load.start()
-    own_f_load.wait()
     part_keep[1] += acc[0, pl.ds(4, 4)]
     d_att_copy = pltpu.make_async_copy(part_keep.at[1], d_att, load_sem.at[0])
     d_att_copy.start()
@@ -534,19 +540,18 @@
     results = [
         ((slabs, slab, hidden), wide), ((slabs, slab, hidden), wide), ((slabs, slab, hidden), wide), ((slabs, slab, hidden), wide),
         ((4, dim, hidden), wide), ((slabs, slab, hidden), narrow), ((slabs, slab, hidden), wide), ((8, dim, hidden), narrow),
-        ((slab + slab // 2, hidden), wide), ((slab + slab // 2, hidden), wide),
+        ((slab + LATE_ROWS, hidden), wide), ((slab + LATE_ROWS, hidden), wide),
     ]
     landing = [
-        ((8, 2, slab, hidden), narrow), ((4, 2, slab, hidden), narrow), ((4, 2, slab, hidden), narrow), ((8, 4 * dim, hidden), narrow),
-        ((2, 4, dim, hidden), wide), ((4, dim, hidden), wide), ((2, slab, hidden), narrow),
+        ((8, 2, slab, hidden), narrow), ((4, 2, slab, hidden), narrow), ((8, 4 * dim, hidden), narrow), ((2, slab, hidden), narrow),
     ]
     scratch = [
         vmem((4, tokens, hidden), BF16), vmem((4, tokens, hidden), BF16), vmem((6 * ffn, hidden), BF16), vmem((6 * ffn, hidden), BF16),
         vmem((2, slabs, slab, hidden), F32), vmem((2, 5, slab, hidden), F32), vmem((2, 4, dim, hidden), F32),
         vmem((8, 2, slab, hidden), BF16), vmem((4 * dim, hidden), BF16),
         dma((8,)), dma((2, 3)), dma((2, 2)), dma((14,)), dma((8, 2)), dma((6,)), dma((4, 2)), dma((7,)), dma((8,)), dma((11,)), dma((8,)), dma((3,)), dma((2,)), dma((2,)),
-        dma((4, 8)), dma((2, 2, 2)), dma((2,)), dma((2,)), dma((2,)), dma((2,)), dma((4,)), dma((10,)), dma((8,)), dma((10,)), dma((8,)), dma((2,)), dma((2,)),
-        pltpu.SemaphoreType.REGULAR((2,)),
+        dma((4, 8)), dma((2, 2, 2)), dma((2,)), dma((2,)), dma((2,)), dma((2,)), dma((2, 8)), dma((10,)), dma((8,)), dma((10,)), dma((8,)), dma((2,)), dma((2,)),
+        pltpu.SemaphoreType.REGULAR((5,)),
     ]
     return pl.pallas_call(
         functools.partial(block_kernel, dim ** -0.5),
@@ -578,7 +583,7 @@
 
     ring = Ring()
     slab = tokens // 8
-    sizes = (slab, slab, slab, slab // 2, slab // 2, slab)
+    sizes = (slab, slab, slab, slab - LATE_ROWS, slab - LATE_ROWS, slab)
     slots = [pl.ds(pl.multiple_of(ring.at(slot) * slab, slab), size) for slot, size in enumerate(sizes)]
 
     def slabs(src, dst, sem, row):
@@ -667,12 +672,12 @@
 def last_kernel(x_two, dy_two, du_far, du_far_other, dx_two_in, dx_two_out, x_buf, dy_buf, du_buf, load_sem, store_sem):
     ring = Ring()
     slab = x_buf.shape[1]
-    half = slab // 2
-    loads, stores, sizes = [], [], (slab, slab, half, half)
-    for index, (slot, du, skip) in enumerate(((SAME_O, du_far, 0), (OTHER_O, du_far_other, 0), (SAME_F, du_far, half), (OTHER_T, du_far_other, half))):
+    early = slab - LATE_ROWS
+    loads, stores, sizes = [], [], (slab, slab, LATE_ROWS, LATE_ROWS)
+    for index, (slot, du, skip) in enumerate(((SAME_O, du_far, 0), (OTHER_O, du_far_other, 0), (SAME_F, du_far, early), (OTHER_T, du_far_other, early))):
         size = sizes[index]
-        rows = pl.ds(pl.multiple_of(ring.at(slot) * slab + skip, half), size)
-        sources = ((x_two.at[rows], x_buf), (dy_two.at[rows], dy_buf), (du.at[pl.ds(2 * skip, size)], du_buf))
+        rows = pl.ds(pl.multiple_of(ring.at(slot) * slab + skip, 16), size)
+        sources = ((x_two.at[rows], x_buf), (dy_two.at[rows], dy_buf), (du.at[pl.ds(slab if skip else 0, size)], du_buf))
         loads.append([pltpu.make_async_copy(src, dst.at[index, pl.ds(0, size)], load_sem.at[index, which]) for which, (src, dst) in enumerate(sources)])
         stores.append(pltpu.make_async_copy(dy_buf.at[index, pl.ds(0, size)], dx_two_out.at[rows], store_sem.at[index]))
     for copies in loads:

time: 383 us -> 381 us (level)
  transfers between devices with their start and end apart: 2 -> 2, of which waited for: 0 -> 1; matrix products, arithmetic and copies ran while one was open for 0% -> 0% of each run, Pallas kernels for 5% -> 5%
where the time goes in v12:
time: 381 us
  Pallas kernels  377 us (99%)
    pallas_call x1, Pallas kernels, block_call(): pl.pallas_call(functools.partial(block_kernel, dim ** (-0.5)), out_shape=...  354 us
    pallas_call x1, Pallas kernels, finish_call(): pl.pallas_call(finish_kernel, out_shape=out_shape, in_specs=[any_spec] *...  19.5 us
  transfers between devices with their start and end apart: 2, of which 1 were waited for; matrix products, arithmetic and copies ran while one was open for 0% of the time, Pallas kernels for 5%

profile of v12, /device:TPU:112, one launch (start us, length us, event | category | flops | bytes accessed | tf_op | source)
XLA Modules:
  0.0 380.6 jit_solution(9572571666066636563)
XLA Ops:
  0.6 354.4 %block.1 = (f32[8,128,1024]{2,1,0:T(8,128)}, f32[8,128,1024]{2,1,0:T(8,128)}, f32[8,128,1024]{2,1,0:T(8,128)}, f32[8,128,1024]{2,1,0:T(8,128)}, f32[4,128,1024]{...) custom-call(f32[8,128,1024]{2,1,0:T(8,128)} %y_one.1, ...), custom_call_target="tpu_custom_call" | custom-call | flops 120000004096 | bytes 134217728 | tf_op jit(solution)/shard_map/block/pallas_call | solution.py:556
  355.0 2.0 collective-permute-start
  357.0 0.0 collective-permute-start.1
  357.0 19.5 %finish.1 = (f32[1024,1024]{1,0:T(8,128)}, f32[1024,1024]{1,0:T(8,128)}, f32[1024,1024]{1,0:T(8,128)}, f32[1024,1024]{1,0:T(8,128)}, f32[1024,512]{1,0:T(8,128)}...) custom-call(f32[1024,1024]{1,0:T(8,128)} %bitcast.32, bf16[1024,1024]{1,0:T(8,128)(2,1)} %bitcast.39, ...), custom_call_target="tpu_custom_call" | custom-call | flops 2000000000 | bytes 54525952 | tf_op jit(solution)/shard_map/finish/pallas_call | solution.py:660
  376.5 0.0 collective-permute-done.du_far
  376.5 0.4 collective-permute-done.1.du_far_other
  376.9 3.4 last.1
Async XLA Ops:
  355.0 21.5 %collective-permute-start = (f32[208,1024]{1,0:T(8,128)}, f32[208,1024]{1,0:T(8,128)}, u32[]{:S(2)}, u32[]{:S(2)}) collective-permute-start(f32[208,1024]{1,0:T(8,128)} %get-tuple-element.37), channel_id=1, source_target_pairs={{0,6},{1,7},{2,4},{3,5},{4,2},{5,3},{6,0},{7,1},{8,14},{9,15},{10,... | collective-permute-start | bytes 2555912 | tf_op jit(solution)/shard_map/ppermute | solution.py:721
  357.0 20.0 %collective-permute-start.1 = (f32[208,1024]{1,0:T(8,128)}, f32[208,1024]{1,0:T(8,128)}, u32[]{:S(2)}, u32[]{:S(2)}) collective-permute-start(f32[208,1024]{1,0:T(8,128)} %get-tuple-element.38), channel_id=1, source_target_pairs={{0,3},{1,2},{2,1},{3,0},{4,7},{5,6},{6,5},{7,4},{8,11},{9,10},{10,... | collective-permute-start | bytes 2555912 | tf_op jit(solution)/shard_map/ppermute | solution.py:721

commit v13 on v12

--- a/solution.py
+++ b/solution.py
@@ -82,8 +82,8 @@
 def block_kernel(
     scale,
     y_one, y_two, dy_one, dy_two, w_up, w_down, w_qkv, w_out,
-    x_two, dx_one, part_own, near_recv, d_att, o_pos, du_pos, wo_full, to_f, to_other_t,
-    uc_seq, uc_two, att_full, o_relay,
+    x_two, dx_one, part_own, near_recv, d_att, o_pos, du_pos, wo_full, to_f,
+    uc_seq, uc_two, att_full, o_relay, du_relay,
     u_all, c_all, up_all, down_all, acc, spare, part_keep, uc_own, att_own,
     load_sem, y_sem, x_sem, w_send, w_recv, uc_send, uc_recv, att_send, att_recv, a2a_send, a2a_recv, relay_recv, near_sem, two_sem,
     seq_sem, head_sem, wo_sem, core_send, core_recv, f_sem, far_sem, o_send, o_recv, du_send, du_recv, o_relay_recv, du_relay_recv, free_slot,
@@ -363,23 +363,19 @@
     o_keep = pltpu.make_async_copy(o_src.at[rows_of(0)], o_pos.at[ring.me], o_send.at[0])
 
     late = slab - LATE_ROWS
-    early = {slot: late if slot in (SAME_F, OTHER_T) else slab for slot in range(1, 6)}
+    early = {slot: late if slot == SAME_F else slab for slot in range(1, 6)}
     du_out = [
         ring.copy(acc.at[1, SAME_O], to_f.at[pl.ds(0, slab)], du_send.at[6], du_relay_recv.at[0], SAME_T),
-        ring.copy(acc.at[1, OTHER_O], to_other_t.at[pl.ds(0, slab)], du_send.at[7], du_relay_recv.at[1], SAME_F),
+        ring.copy(acc.at[1, OTHER_O], du_relay, du_send.at[7], du_relay_recv.at[1], SAME_F),
     ] + [ring.copy(acc.at[1, slot, pl.ds(0, early[slot])], du_pos.at[ring.me, pl.ds(0, early[slot])], du_send.at[slot], du_recv.at[slot], slot) for slot in (5, 4, 3, 2, 1)]
     du_keep = pltpu.make_async_copy(acc.at[1, 0], du_pos.at[ring.me], du_send.at[0])
-    du_late = [
-        pltpu.make_async_copy(acc.at[1, slot, pl.ds(late, slab - late)], dst.at[pl.ds(slab, slab - late)], du_send.at[sem])
-        for slot, dst, sem in ((SAME_F, to_f, 8), (OTHER_T, to_other_t, 9))
-    ]
+    du_late = pltpu.make_async_copy(acc.at[1, SAME_F, pl.ds(late, slab - late)], to_f.at[pl.ds(slab, slab - late)], du_send.at[8])
+    du_pass = ring.copy(du_relay, du_pos.at[ring.at(SAME_F)], du_send.at[9], du_recv.at[OTHER_O], OTHER_T)
 
     att_f_core.wait_recv()
     att_keep.wait()
     att_out[1].wait_recv()
     start(head_loads(2, 0))
-    spare[...] = jnp.zeros_like(spare)
-    part_keep[...] = jnp.zeros_like(part_keep)
     uc_keep.wait()
     for slot in range(1, 8):
         ring.copy(uc_own.at[slot], uc_seq.at[slot], a2a_send.at[0], a2a_recv.at[slot], PARTNER).wait_recv()
@@ -416,6 +412,7 @@
         def _():
             start(head_loads(relation_of(step + 1), 1 - buf))
 
+        kept = pl.ds(pl.multiple_of(jnp.where(step < 2, step, 2) * seq_len, seq_len), seq_len)
         heads = [ring.at_traced(relation * 2 + other) for other in (1, 0)]
         wo_copies = [
             pltpu.make_async_copy(up_all.at[pl.ds(pl.multiple_of(12 * dim + (2 * buf + index) * dim, dim), dim)], wo_full.at[head], wo_sem.at[index])
@@ -436,14 +433,14 @@
             c_all[seq, :, columns] = dot_nn(prob_b, value).astype(BF16)
             d_prob = dot_nt(d_out, value)
             d_score = (prob * (d_prob - jnp.sum(d_prob * prob, axis=-1, keepdims=True)) * scale).astype(BF16)
-            c_all[3, :, pl.ds(index * 3 * dim, dim)] = dot_nn(d_score, key).astype(BF16)
-            c_all[3, :, pl.ds((index * 3 + 1) * dim, dim)] = dot_nn(query.T, d_score).T.astype(BF16)
-            c_all[3, :, pl.ds((index * 3 + 2) * dim, dim)] = dot_nn(d_out.T, prob_b).T.astype(BF16)
-            @pl.when((step < 2) | (step >= 4))
+            down_all[kept, pl.ds(index * 3 * dim, dim)] = dot_nn(d_score, key).astype(BF16)
+            down_all[kept, pl.ds((index * 3 + 1) * dim, dim)] = dot_nn(query.T, d_score).T.astype(BF16)
+            down_all[kept, pl.ds((index * 3 + 2) * dim, dim)] = dot_nn(d_out.T, prob_b).T.astype(BF16)
+            @pl.when(step >= 4)
             def _():
                 dst = (spare, part_keep)[index].at[buf]
-                dst[pl.ds(0, 3)] += dot_tn(c_all[3, :, own], u_all[2 * seq]).reshape(3, dim, hidden)
-                dst[3] += dot_tn(c_all[seq, :, columns], u_all[2 * seq + 1])
+                dst[pl.ds(0, 3)] += dot_tn(down_all[kept, own], u_all[2]).reshape(3, dim, hidden)
+                dst[3] += dot_tn(c_all[1, :, columns], u_all[3])
 
             if index == 0:
                 @pl.when(step == 1)
@@ -461,15 +458,6 @@
                     pl.semaphore_wait(free_slot.at[4], 1)
                     core_copies[1].start()
 
-        @pl.when(step < 4)
-        def _():
-            def du_tile(part, carry):
-                rows = pl.ds(pl.multiple_of(part * half, half), half)
-                acc[1, pl.ds(part * fours, fours)] += dot_nn(c_all[3, rows, pl.ds(0, 6 * dim)], up_all[qkv_rows(buf), :]).reshape(fours, slab, hidden)
-                return carry
-
-            lax.fori_loop(0, 2, du_tile, 0)
-
         @pl.when(step == 1)
         def _():
             att_t_core.wait_recv()
@@ -479,6 +467,18 @@
         def _():
             att_o.wait_recv()
             att_o_core.start()
+
+        @pl.when(step < 4)
+        def _():
+            def du_tile(part, carry):
+                rows = pl.ds(pl.multiple_of(jnp.where(step < 2, step, 2) * seq_len + part * half, half), half)
+                acc[1, pl.ds(part * fours, fours)] += dot_nn(down_all[rows, pl.ds(0, 6 * dim)], up_all[qkv_rows(buf), :]).reshape(fours, slab, hidden)
+                return carry
+
+            lax.fori_loop(0, 2, du_tile, 0)
+
+        @pl.when(step == 2)
+        def _():
             att_o_core.wait_recv()
             start(head_loads(3, 1))
 
@@ -486,9 +486,20 @@
         def _():
             start(o_out)
             start(du_out)
-            start(du_late)
+            du_late.start()
             o_keep.start()
             du_keep.start()
+
+            def own_gradients(pair, carry):
+                own_rows = pl.ds(pl.multiple_of(pair * seq_len, seq_len), seq_len)
+                for index, other in enumerate((1, 0)):
+                    columns = pl.ds(pl.multiple_of(ring.at_traced(relation_of(pair) * 2 + other) * dim, dim), dim)
+                    dst = (spare, part_keep)[index].at[pair]
+                    dst[pl.ds(0, 3)] = dot_tn(down_all[own_rows, pl.ds(index * 3 * dim, 3 * dim)], u_all[0]).reshape(3, dim, hidden)
+                    dst[3] = dot_tn(c_all[0, :, columns], u_all[1])
+                return carry
+
+            lax.fori_loop(0, 2, own_gradients, 0)
 
         @pl.when(step == 4)
         def _():
@@ -506,14 +517,16 @@
     for copy in o_out[:2]:
         copy.wait_recv()
     start(o_pass)
+    du_out[1].wait_recv()
+    du_pass.start()
     core_copies[1].wait_recv()
     part_keep[1] += acc[0, pl.ds(0, 4)]
     for copy in du_out[2:]:
         copy.wait_recv()
     for slot in range(1, 8):
         ring.copy(o_pos.at[0], o_pos.at[ring.at(slot)], near_sem.at[0], o_recv.at[slot], PARTNER).wait_recv()
-    for copy in du_out[:2]:
-        copy.wait_recv()
+    du_out[0].wait_recv()
+    du_pass.wait_recv()
     near.wait_recv()
     f_copy.wait_recv()
     part_keep[1] += acc[0, pl.ds(4, 4)]
@@ -521,10 +534,9 @@
     d_att_copy.start()
 
     sends = att_out + [att_t, att_o, att_f_core, att_t_core, att_o_core] + list(a2a_out.values()) + a2a_pass + [two_out]
-    for copy in sends + o_out + du_out + o_pass + uc_to_t + core_copies + [f_copy]:
+    for copy in sends + o_out + du_out + o_pass + uc_to_t + core_copies + [du_pass, f_copy]:
         copy.wait_send()
-    for copy in du_late:
-        copy.wait()
+    du_late.wait()
     o_keep.wait()
     du_keep.wait()
     d_att_copy.wait()
@@ -540,10 +552,10 @@
     results = [
         ((slabs, slab, hidden), wide), ((slabs, slab, hidden), wide), ((slabs, slab, hidden), wide), ((slabs, slab, hidden), wide),
         ((4, dim, hidden), wide), ((slabs, slab, hidden), narrow), ((slabs, slab, hidden), wide), ((8, dim, hidden), narrow),
-        ((slab + LATE_ROWS, hidden), wide), ((slab + LATE_ROWS, hidden), wide),
+        ((slab + LATE_ROWS, hidden), wide),
     ]
     landing = [
-        ((8, 2, slab, hidden), narrow), ((4, 2, slab, hidden), narrow), ((8, 4 * dim, hidden), narrow), ((2, slab, hidden), narrow),
+        ((8, 2, slab, hidden), narrow), ((4, 2, slab, hidden), narrow), ((8, 4 * dim, hidden), narrow), ((2, slab, hidden), narrow), ((slab, hidden), wide),
     ]
     scratch = [
         vmem((4, tokens, hidden), BF16), vmem((4, tokens, hidden), BF16), vmem((6 * ffn, hidden), BF16), vmem((6 * ffn, hidden), BF16),
@@ -583,8 +595,8 @@
 
     ring = Ring()
     slab = tokens // 8
-    sizes = (slab, slab, slab, slab - LATE_ROWS, slab - LATE_ROWS, slab)
-    slots = [pl.ds(pl.multiple_of(ring.at(slot) * slab, slab), size) for slot, size in enumerate(sizes)]
+    sizes = {0: slab, PARTNER: slab, SAME_T: slab, OTHER_T: slab, SAME_F: slab - LATE_ROWS, OTHER_F: slab, OTHER_O: slab}
+    slots = [pl.ds(pl.multiple_of(ring.at(slot) * slab, slab), size) for slot, size in sizes.items()]
 
     def slabs(src, dst, sem, row):
         return [pltpu.make_async_copy(src.at[rows], dst.at[rows], sem.at[row, index]) for index, rows in enumerate(slots)]
@@ -655,7 +667,7 @@
     scratch = [
         vmem(state, F32), vmem(state, BF16), vmem((hidden, hidden), BF16), vmem(state, F32), vmem(state, F32), vmem(state, F32), vmem(state, F32),
         vmem(part_own.shape, F32), vmem(part_own.shape, F32), vmem(d_att.shape, F32), vmem((hidden, ffn), F32), vmem((3 * hidden, 1, dim), F32),
-        dma((10, 6)), dma((8, 6)),
+        dma((10, 7)), dma((8, 7)),
     ]
     return pl.pallas_call(
         finish_kernel,
@@ -669,15 +681,14 @@
     )(y_one, o_pos, wo_full, x_two, dx_one, dy_two, du_pos, part_own, near_recv, d_att)
 
 
-def last_kernel(x_two, dy_two, du_far, du_far_other, dx_two_in, dx_two_out, x_buf, dy_buf, du_buf, load_sem, store_sem):
+def last_kernel(x_two, dy_two, du_far, dx_two_in, dx_two_out, x_buf, dy_buf, du_buf, load_sem, store_sem):
     ring = Ring()
     slab = x_buf.shape[1]
-    early = slab - LATE_ROWS
-    loads, stores, sizes = [], [], (slab, slab, LATE_ROWS, LATE_ROWS)
-    for index, (slot, du, skip) in enumerate(((SAME_O, du_far, 0), (OTHER_O, du_far_other, 0), (SAME_F, du_far, early), (OTHER_T, du_far_other, early))):
+    loads, stores, sizes = [], [], (slab, LATE_ROWS)
+    for index, (slot, skip) in enumerate(((SAME_O, 0), (SAME_F, slab - LATE_ROWS))):
         size = sizes[index]
         rows = pl.ds(pl.multiple_of(ring.at(slot) * slab + skip, 16), size)
-        sources = ((x_two.at[rows], x_buf), (dy_two.at[rows], dy_buf), (du.at[pl.ds(slab if skip else 0, size)], du_buf))
+        sources = ((x_two.at[rows], x_buf), (dy_two.at[rows], dy_buf), (du_far.at[pl.ds(index * slab, size)], du_buf))
         loads.append([pltpu.make_async_copy(src, dst.at[index, pl.ds(0, size)], load_sem.at[index, which]) for which, (src, dst) in enumerate(sources)])
         stores.append(pltpu.make_async_copy(dy_buf.at[index, pl.ds(0, size)], dx_two_out.at[rows], store_sem.at[index]))
     for copies in loads:
@@ -693,20 +704,20 @@
         copy.wait()
 
 
-def last_call(x_two, dy_two, du_far, du_far_other, dx_two):
+def last_call(x_two, dy_two, du_far, dx_two):
     tokens, hidden = x_two.shape
     any_spec = pl.BlockSpec(memory_space=pl.ANY)
-    buf = pltpu.VMEM((4, tokens // 8, hidden), F32)
+    buf = pltpu.VMEM((2, tokens // 8, hidden), F32)
     return pl.pallas_call(
         last_kernel,
         out_shape=jax.ShapeDtypeStruct(dx_two.shape, F32),
-        in_specs=[any_spec] * 5,
+        in_specs=[any_spec] * 4,
         out_specs=any_spec,
-        input_output_aliases={4: 0},
-        scratch_shapes=[buf, buf, buf, pltpu.SemaphoreType.DMA((4, 3)), pltpu.SemaphoreType.DMA((4,))],
+        input_output_aliases={3: 0},
+        scratch_shapes=[buf, buf, buf, pltpu.SemaphoreType.DMA((2, 3)), pltpu.SemaphoreType.DMA((2,))],
         cost_estimate=pl.CostEstimate(flops=10**6, bytes_accessed=4 * 2**20, transcendentals=0),
         name="last",
-    )(x_two, dy_two, du_far, du_far_other, dx_two)
+    )(x_two, dy_two, du_far, dx_two)
 
 
 def local_backward(y_one, y_two, dy_one, dy_two, w_qkv, w_out, w_up, w_down):
@@ -717,11 +728,10 @@
     x_two, dx_one, part_own, near_recv, d_att, o_pos, du_pos, wo_full = (tensor.reshape(-1, hidden) for tensor in results[:8])
     devices = range(lax.axis_size("tp"))
     to_f = [(device, (3 - device // 2) * 2 + device % 2) for device in devices]
-    to_other_t = [(device, 4 * (device // 4) + 3 - device % 4) for device in devices]
-    du_far, du_far_other = lax.ppermute(results[8], "tp", to_f), lax.ppermute(results[9], "tp", to_other_t)
+    du_far = lax.ppermute(results[8], "tp", to_f)
     y_flat, dy_flat = y_one.reshape(-1, hidden), dy_two.reshape(-1, hidden)
     *states, dw_up, dw_down, dw_qkv, dw_out = finish_call(y_flat, o_pos, wo_full, x_two, dx_one, dy_flat, du_pos, part_own, near_recv, d_att)
-    states[3] = last_call(x_two, dy_flat, du_far, du_far_other, states[3])
+    states[3] = last_call(x_two, dy_flat, du_far, states[3])
     states = [tensor.reshape(y_one.shape) for tensor in states]
     return (*states, dw_qkv.reshape(1, hidden, 1, parts, dim), dw_out[None, None], dw_up[None], dw_down[None])
 

time: 381 us -> 381 us (level)
  transfers between devices with their start and end apart: 2 -> 1, of which waited for: 1 -> 0; matrix products, arithmetic and copies ran while one was open for 0% -> 0% of each run, Pallas kernels for 5% -> 5%
where the time goes in v13:
time: 381 us; the launch traced here: 380 us
  Pallas kernels  377 us (99%)
    pallas_call x1, Pallas kernels, block_call(): pl.pallas_call(functools.partial(block_kernel, dim ** (-0.5)), out_shape=...  354 us
    pallas_call x1, Pallas kernels, finish_call(): pl.pallas_call(finish_kernel, out_shape=out_shape, in_specs=[any_spec] *...  20.5 us
  transfers between devices with their start and end apart: 1, of which 0 were waited for; matrix products, arithmetic and copies ran while one was open for 0% of the time, Pallas kernels for 5%

profile of v13, /device:TPU:112, one launch (start us, length us, event | category | flops | bytes accessed | tf_op | source)
XLA Modules:
  0.0 380.2 jit_solution(11342167187122499770)
XLA Ops:
  0.6 354.4 %block.1 = (f32[8,128,1024]{2,1,0:T(8,128)}, f32[8,128,1024]{2,1,0:T(8,128)}, f32[8,128,1024]{2,1,0:T(8,128)}, f32[8,128,1024]{2,1,0:T(8,128)}, f32[4,128,1024]{...) custom-call(f32[8,128,1024]{2,1,0:T(8,128)} %y_one.1, ...), custom_call_target="tpu_custom_call" | custom-call | flops 120000004096 | bytes 134217728 | tf_op jit(solution)/shard_map/block/pallas_call | solution.py:568
  355.0 2.0 collective-permute-start
  357.0 20.5 %finish.1 = (f32[1024,1024]{1,0:T(8,128)}, f32[1024,1024]{1,0:T(8,128)}, f32[1024,1024]{1,0:T(8,128)}, f32[1024,1024]{1,0:T(8,128)}, f32[1024,512]{1,0:T(8,128)}...) custom-call(f32[1024,1024]{1,0:T(8,128)} %bitcast.32, bf16[1024,1024]{1,0:T(8,128)(2,1)} %bitcast.39, ...), custom_call_target="tpu_custom_call" | custom-call | flops 2000000000 | bytes 54525952 | tf_op jit(solution)/shard_map/finish/pallas_call | solution.py:672
  377.4 0.0 collective-permute-done.du_far
  377.4 2.6 last.1
Async XLA Ops:
  355.0 22.4 %collective-permute-start = (f32[208,1024]{1,0:T(8,128)}, f32[208,1024]{1,0:T(8,128)}, u32[]{:S(2)}, u32[]{:S(2)}) collective-permute-start(f32[208,1024]{1,0:T(8,128)} %get-tuple-element.36), channel_id=1, source_target_pairs={{0,6},{1,7},{2,4},{3,5},{4,2},{5,3},{6,0},{7,1},{8,14},{9,15},{10,... | collective-permute-start | bytes 2555912 | tf_op jit(solution)/shard_map/ppermute | solution.py:731

commit v14 on v13

--- a/solution.py
+++ b/solution.py
@@ -9,7 +9,8 @@
 
 RMS_EPS = 1e-6
 LOG2_E = 1.4426950408889634
-LATE_ROWS = 80
+LATE_ROWS = 96
+FAR_ROWS = 16
 MESH = pl.DeviceIdType.MESH
 BF16, F32 = jnp.bfloat16, jnp.float32
 VMEM_LIMIT = 64 * 1024 * 1024 - 65536
@@ -86,7 +87,7 @@
     uc_seq, uc_two, att_full, o_relay, du_relay,
     u_all, c_all, up_all, down_all, acc, spare, part_keep, uc_own, att_own,
     load_sem, y_sem, x_sem, w_send, w_recv, uc_send, uc_recv, att_send, att_recv, a2a_send, a2a_recv, relay_recv, near_sem, two_sem,
-    seq_sem, head_sem, wo_sem, core_send, core_recv, f_sem, far_sem, o_send, o_recv, du_send, du_recv, o_relay_recv, du_relay_recv, free_slot,
+    seq_sem, head_sem, wo_sem, core_send, core_recv, f_sem, far_sem, o_send, o_recv, du_send, du_recv, o_relay_recv, du_relay_recv, far_recv, free_slot,
 ):
     ring = Ring()
     slabs, slab, hidden = acc.shape[1:]
@@ -114,7 +115,12 @@
         ]
 
     w_own = weight_pair(0, 1, PARTNER, 0) + weight_pair(0, 2, SAME_T, 2) + weight_pair(0, 4, SAME_F, 4)
-    w_near_t = weight_pair(2, 6, SAME_F, 6)
+    def far_part(src_slot, first, count, to, index, recv_sem):
+        src, dst = (pl.ds(rooms[slot] * half + first, count) for slot in (src_slot, 6))
+        return [ring.copy(buf.at[src], buf.at[dst], w_send.at[index + which], recv_sem.at[which], to) for which, buf in enumerate((up_all, down_all))]
+
+    w_near_t = far_part(2, FAR_ROWS, half - FAR_ROWS, SAME_F, 6, w_recv.at[6])
+    w_over_t = far_part(4, 0, FAR_ROWS, SAME_T, 14, far_recv)
     w_near_t_core = weight_pair(2, 3, PARTNER, 8)
     w_near_f = weight_pair(4, 5, PARTNER, 10)
     w_far = weight_pair(6, 7, PARTNER, 12)
@@ -122,7 +128,8 @@
     def uc_pair(src_slot, dst_slot, to, index):
         return [ring.copy(buf.at[src_slot], buf.at[dst_slot], uc_send.at[index + which], uc_recv.at[dst_slot, which], to) for which, buf in enumerate((u_all, c_all))]
 
-    uc_out = uc_pair(0, 2, SAME_T, 0) + uc_pair(0, 1, PARTNER, 2)
+    u_to_t, c_to_t = uc_pair(0, 2, SAME_T, 0)
+    uc_core = uc_pair(0, 1, PARTNER, 2)
     uc_pass = uc_pair(2, 3, PARTNER, 4)
 
     def att(src, dst_slot, to, index):
@@ -171,7 +178,8 @@
         return carry
 
     lax.fori_loop(0, slabs, normalize, 0)
-    start(uc_out)
+    u_to_t.start()
+    start(uc_core)
     for part in range(3):
         qkv_loads[part].wait()
         att_own[pl.ds(part * dim, dim), :] = uc_own[:, 1, :, pl.ds(part * dim, dim)].reshape(hidden, dim).T
@@ -190,10 +198,15 @@
         slot = jnp.where(step == 3, 4, jnp.where(step == 4, 3, step))
         place = pl.ds(pl.multiple_of(jnp.where(step == 6, 1, jnp.where(step == 7, 3, slot)) * half, half), half)
 
-        @pl.when(step >= 1)
+        @pl.when((step >= 1) & (step != 6))
         def _():
             for which, buf in enumerate((up_all, down_all)):
                 ring.copy(buf.at[place], buf.at[place], w_send.at[0], w_recv.at[slot, which], PARTNER).wait_recv()
+
+        @pl.when(step == 6)
+        def _():
+            for copy in w_near_t + w_over_t:
+                copy.wait_recv()
 
         @pl.when(step == 2)
         def _():
@@ -204,6 +217,9 @@
 
         @pl.when(step == 3)
         def _():
+            pl.semaphore_wait(free_slot.at[5], 1)
+            start(w_over_t)
+            c_to_t.start()
             start(w_near_f)
 
         @pl.when(step == 6)
@@ -229,6 +245,7 @@
         @pl.when(step == 1)
         def _():
             say_free(0, SAME_F)
+            say_free(5, SAME_T)
 
         @pl.when(step == 4)
         def _():
@@ -312,7 +329,7 @@
     lax.fori_loop(0, 16, gradients, 0)
     out_own = pltpu.make_async_copy(acc.at[1], part_own, load_sem.at[1])
     out_own.start()
-    for copy in w_own + w_near_t + w_near_t_core + w_near_f + w_far + uc_out + uc_pass:
+    for copy in w_own + w_near_t + w_over_t + w_near_t_core + w_near_f + w_far + [u_to_t, c_to_t] + uc_core + uc_pass:
         copy.wait_send()
     say_free(2, SAME_T)
 
@@ -345,8 +362,8 @@
     seq_two = [copy for slot in range(4) for copy in seq_loads(1, uc_two, slot, slot)]
     uc_to_t = [
         ring.copy(uc_seq.at[slot, which], u_all.at[2 + which, rows_of(4 + index)], far_sem.at[0, 2 * index + which], far_sem.at[1, 2 * index + which], SAME_T)
+        for which in (0, 1)
         for index, slot in enumerate((0, 1, 4, 5))
-        for which in (0, 1)
     ]
     core_copies = [ring.copy(spare.at[index, pl.ds(0, 4)], acc.at[0, pl.ds(0, 4)], core_send.at[index], core_recv.at[index], PARTNER) for index in (0, 1)]
     f_copy = ring.copy(part_keep.at[0], acc.at[0, pl.ds(4, 4)], f_sem.at[0], f_sem.at[1], SAME_F)
@@ -402,7 +419,7 @@
             say_free(4, PARTNER)
             for copy in seq_two:
                 copy.wait()
-            for copy in uc_to_t:
+            for copy in uc_to_t[:4]:
                 copy.wait_recv()
 
         for copy in head_loads(0, buf):
@@ -420,17 +437,23 @@
         ]
         start(wo_copies)
         c_all[2, :, pl.ds(0, 6 * dim)] = dot_nt(u_all[2 * seq], up_all[qkv_rows(buf), :]).astype(BF16)
-        c_all[2, :, pl.ds(6 * dim, 2 * dim)] = dot_nt(u_all[2 * seq + 1], up_all[wo_rows(buf), :]).astype(BF16)
         for index, head in enumerate(heads):
             columns = pl.ds(pl.multiple_of(head * dim, dim), dim)
             own = pl.ds(index * 3 * dim, 3 * dim)
             query, key, value = (c_all[2, :, pl.ds((index * 3 + part) * dim, dim)] for part in range(3))
-            d_out = c_all[2, :, pl.ds((6 + index) * dim, dim)]
             scores = dot_nt(query, key) * (scale * LOG2_E)
             grown = jnp.exp2(scores - jnp.max(scores, axis=-1, keepdims=True))
             prob = grown * (1.0 / jnp.sum(grown, axis=-1, keepdims=True))
             prob_b = prob.astype(BF16)
             c_all[seq, :, columns] = dot_nn(prob_b, value).astype(BF16)
+            if index == 0:
+                @pl.when(step == 4)
+                def _():
+                    for copy in uc_to_t[4:]:
+                        copy.wait_recv()
+
+                c_all[2, :, pl.ds(6 * dim, 2 * dim)] = dot_nt(u_all[2 * seq + 1], up_all[wo_rows(buf), :]).astype(BF16)
+            d_out = c_all[2, :, pl.ds((6 + index) * dim, dim)]
             d_prob = dot_nt(d_out, value)
             d_score = (prob * (d_prob - jnp.sum(d_prob * prob, axis=-1, keepdims=True)) * scale).astype(BF16)
             down_all[kept, pl.ds(index * 3 * dim, dim)] = dot_nn(d_score, key).astype(BF16)
@@ -561,9 +584,9 @@
         vmem((4, tokens, hidden), BF16), vmem((4, tokens, hidden), BF16), vmem((6 * ffn, hidden), BF16), vmem((6 * ffn, hidden), BF16),
         vmem((2, slabs, slab, hidden), F32), vmem((2, 5, slab, hidden), F32), vmem((2, 4, dim, hidden), F32),
         vmem((8, 2, slab, hidden), BF16), vmem((4 * dim, hidden), BF16),
-        dma((8,)), dma((2, 3)), dma((2, 2)), dma((14,)), dma((8, 2)), dma((6,)), dma((4, 2)), dma((7,)), dma((8,)), dma((11,)), dma((8,)), dma((3,)), dma((2,)), dma((2,)),
-        dma((4, 8)), dma((2, 2, 2)), dma((2,)), dma((2,)), dma((2,)), dma((2,)), dma((2, 8)), dma((10,)), dma((8,)), dma((10,)), dma((8,)), dma((2,)), dma((2,)),
-        pltpu.SemaphoreType.REGULAR((5,)),
+        dma((8,)), dma((2, 3)), dma((2, 2)), dma((16,)), dma((8, 2)), dma((6,)), dma((4, 2)), dma((7,)), dma((8,)), dma((11,)), dma((8,)), dma((3,)), dma((2,)), dma((2,)),
+        dma((4, 8)), dma((2, 2, 2)), dma((2,)), dma((2,)), dma((2,)), dma((2,)), dma((2, 8)), dma((10,)), dma((8,)), dma((10,)), dma((8,)), dma((2,)), dma((2,)), dma((2,)),
+        pltpu.SemaphoreType.REGULAR((6,)),
     ]
     return pl.pallas_call(
         functools.partial(block_kernel, dim ** -0.5),
@@ -603,37 +626,14 @@
 
     x_in, dy_in, du_in = pieces(x_two, x_buf, load_sem, 0), slabs(dy_two, dy_buf, load_sem, 1), slabs(du_pos, du_buf, load_sem, 2)
     y_in, o_in = pieces(y_one, y_buf, load_sem, 3), pieces(o_pos, o_buf, load_sem, 4)
-    wo_in, dx_in = whole(wo_full, wo_buf, load_sem, 5), whole(dx_one, dx_buf, load_sem, 6)
+    wo_in, dx_in = whole(wo_full, wo_buf, load_sem, 5), pieces(dx_one, dx_buf, load_sem, 6)
     own_in, near_in, att_in = whole(part_own, own_buf, load_sem, 7), whole(near_recv, near_buf, load_sem, 8), whole(d_att, att_buf, load_sem, 9)
-    for group in (x_in, *zip(dy_in, du_in)):
-        for copy in group:
-            copy.start()
-    for copy in (dx_in, wo_in):
+    order = [own_in, near_in, att_in, wo_in, *(copy for group in zip(y_in, o_in) for copy in group), *x_in, *(copy for group in zip(dy_in, du_in) for copy in group), *dx_in]
+    for copy in order:
         copy.start()
-    for group in zip(y_in, o_in):
-        for copy in group:
-            copy.start()
-    for copy in (own_in, near_in, att_in):
-        copy.start()
 
     x_store, dx2_store, x1_store = pieces(x_buf, x_two_out, store_sem, 0), slabs(dy_buf, dx_two_out, store_sem, 1), pieces(y_buf, x_one_out, store_sem, 2)
-    for index in range(len(chunks)):
-        x_in[index].wait()
-        x_store[index].start()
-    for index, rows in enumerate(slots):
-        dy_in[index].wait()
-        du_in[index].wait()
-        dy_buf[rows, :] += rms_back(x_buf[rows, :], du_buf[rows, :])
-        dx2_store[index].start()
-    dx_in.wait()
-    dx_store = whole(dx_buf, dx_one_out, store_sem, 3)
-    dx_store.start()
-    wo_in.wait()
-    for index, rows in enumerate(chunks):
-        y_in[index].wait()
-        o_in[index].wait()
-        y_buf[rows, :] -= dot_nn(o_buf[rows, :], wo_buf[...])
-        x1_store[index].start()
+    dx_store = pieces(dx_buf, dx_one_out, store_sem, 3)
     own_in.wait()
     near_in.wait()
     ffn = up_out.shape[1]
@@ -652,7 +652,24 @@
     qkv_store.start()
     out_store = whole(att_buf.at[pl.ds(3 * dim, dim)], dw_out, store_sem, 6)
     out_store.start()
-    for copy in x_store + dx2_store + x1_store + [dx_store, up_store, qkv_store, out_store, down_store]:
+    wo_in.wait()
+    for index, rows in enumerate(chunks):
+        y_in[index].wait()
+        o_in[index].wait()
+        y_buf[rows, :] -= dot_nn(o_buf[rows, :], wo_buf[...])
+        x1_store[index].start()
+    for index in range(len(chunks)):
+        x_in[index].wait()
+        x_store[index].start()
+    for index, rows in enumerate(slots):
+        dy_in[index].wait()
+        du_in[index].wait()
+        dy_buf[rows, :] += rms_back(x_buf[rows, :], du_buf[rows, :])
+        dx2_store[index].start()
+    for index in range(len(chunks)):
+        dx_in[index].wait()
+        dx_store[index].start()
+    for copy in x_store + dx2_store + x1_store + dx_store + [up_store, qkv_store, out_store, down_store]:
         copy.wait()
 
 

time: 381 us -> 378 us (level)
  transfers between devices with their start and end apart: 1 -> 1, of which waited for: 0 -> 1; matrix products, arithmetic and copies ran while one was open for 0% -> 0% of each run, Pallas kernels for 5% -> 5%
where the time goes in v14:
time: 378 us; the launch traced here: 377 us
  Pallas kernels  374 us (99%)
    pallas_call x1, Pallas kernels, block_call(): pl.pallas_call(functools.partial(block_kernel, dim ** (-0.5)), out_shape=...  352 us
    pallas_call x1, Pallas kernels, finish_call(): pl.pallas_call(finish_kernel, out_shape=out_shape, in_specs=[any_spec] *...  19.8 us
  transfers between devices with their start and end apart: 1, of which 1 were waited for; matrix products, arithmetic and copies ran while one was open for 0% of the time, Pallas kernels for 5%

profile of v14, /device:TPU:112, one launch (start us, length us, event | category | flops | bytes accessed | tf_op | source)
XLA Modules:
  0.0 377.5 jit_solution(7226598783921284455)
XLA Ops:
  0.6 351.6 %block.1 = (f32[8,128,1024]{2,1,0:T(8,128)}, f32[8,128,1024]{2,1,0:T(8,128)}, f32[8,128,1024]{2,1,0:T(8,128)}, f32[8,128,1024]{2,1,0:T(8,128)}, f32[4,128,1024]{...) custom-call(f32[8,128,1024]{2,1,0:T(8,128)} %y_one.1, ...), custom_call_target="tpu_custom_call" | custom-call | flops 120000004096 | bytes 134217728 | tf_op jit(solution)/shard_map/block/pallas_call | solution.py:591
  352.2 2.0 collective-permute-start
  354.2 19.8 %finish.1 = (f32[1024,1024]{1,0:T(8,128)}, f32[1024,1024]{1,0:T(8,128)}, f32[1024,1024]{1,0:T(8,128)}, f32[1024,1024]{1,0:T(8,128)}, f32[1024,512]{1,0:T(8,128)}...) custom-call(f32[1024,1024]{1,0:T(8,128)} %bitcast.32, bf16[1024,1024]{1,0:T(8,128)(2,1)} %bitcast.39, ...), custom_call_target="tpu_custom_call" | custom-call | flops 2000000000 | bytes 54525952 | tf_op jit(solution)/shard_map/finish/pallas_call | solution.py:689
  374.0 0.6 collective-permute-done.du_far
  374.6 2.7 last.1
Async XLA Ops:
  352.2 22.4 %collective-permute-start = (f32[224,1024]{1,0:T(8,128)}, f32[224,1024]{1,0:T(8,128)}, u32[]{:S(2)}, u32[]{:S(2)}) collective-permute-start(f32[224,1024]{1,0:T(8,128)} %get-tuple-element.36), channel_id=1, source_target_pairs={{0,6},{1,7},{2,4},{3,5},{4,2},{5,3},{6,0},{7,1},{8,14},{9,15},{10,... | collective-permute-start | bytes 2752520 | tf_op jit(solution)/shard_map/ppermute | solution.py:748

commit v15 on v14

--- a/solution.py
+++ b/solution.py
@@ -10,7 +10,7 @@
 RMS_EPS = 1e-6
 LOG2_E = 1.4426950408889634
 LATE_ROWS = 96
-FAR_ROWS = 16
+FAR_ROWS = 32
 MESH = pl.DeviceIdType.MESH
 BF16, F32 = jnp.bfloat16, jnp.float32
 VMEM_LIMIT = 64 * 1024 * 1024 - 65536
@@ -85,7 +85,7 @@
     y_one, y_two, dy_one, dy_two, w_up, w_down, w_qkv, w_out,
     x_two, dx_one, part_own, near_recv, d_att, o_pos, du_pos, wo_full, to_f,
     uc_seq, uc_two, att_full, o_relay, du_relay,
-    u_all, c_all, up_all, down_all, acc, spare, part_keep, uc_own, att_own,
+    u_all, c_all, up_all, down_all, acc, spare, part_keep, uc_own,
     load_sem, y_sem, x_sem, w_send, w_recv, uc_send, uc_recv, att_send, att_recv, a2a_send, a2a_recv, relay_recv, near_sem, two_sem,
     seq_sem, head_sem, wo_sem, core_send, core_recv, f_sem, far_sem, o_send, o_recv, du_send, du_recv, o_relay_recv, du_relay_recv, far_recv, free_slot,
 ):
@@ -135,9 +135,9 @@
     def att(src, dst_slot, to, index):
         return ring.copy(src, att_full.at[dst_slot], att_send.at[index], att_recv.at[dst_slot], to)
 
-    att_keep = pltpu.make_async_copy(att_own, att_full.at[0], load_sem.at[6])
-    att_out = [att(att_own, 4, SAME_F, 0), att(att_own, 1, PARTNER, 1)]
-    att_t, att_o = att(att_own, 2, SAME_T, 2), att(att_full.at[4], 6, SAME_T, 3)
+    att_keep = [pltpu.make_async_copy(uc_own.at[part, 0], att_full.at[0, pl.ds(part * dim, dim)], x_sem.at[part // 2, part % 2]) for part in range(4)]
+    att_out = [att(att_full.at[0], 4, SAME_F, 0), att(att_full.at[0], 1, PARTNER, 1)]
+    att_t, att_o = att(att_full.at[0], 2, SAME_T, 2), att(att_full.at[4], 6, SAME_T, 3)
     att_f_core, att_t_core, att_o_core = att(att_full.at[4], 5, PARTNER, 4), att(att_full.at[2], 3, PARTNER, 5), att(att_full.at[6], 7, PARTNER, 6)
 
     a2a_out = {slot: ring.copy(uc_own.at[slot], uc_seq.at[slot], a2a_send.at[slot], a2a_recv.at[slot], slot) for slot in (1, 2, 3, 4, 5)}
@@ -154,7 +154,6 @@
         pltpu.make_async_copy(w_up, uc_own.at[:, 0, :, pl.ds(0, half)], load_sem.at[1]),
         pltpu.make_async_copy(y_one, acc.at[0], load_sem.at[2]),
         pltpu.make_async_copy(dy_two, acc.at[1], load_sem.at[3]),
-        pltpu.make_async_copy(w_out, att_own.at[pl.ds(3 * dim, dim)], load_sem.at[7]),
     ]
     qkv_loads = [pltpu.make_async_copy(w_qkv.at[part], uc_own.at[:, 1, :, pl.ds(part * dim, dim)], y_sem.at[0, part]) for part in range(3)]
     start(loads)
@@ -166,6 +165,8 @@
     for part in range(half // dim):
         up_all[pl.ds(part * dim, dim), :] = uc_own[:, 0, :, pl.ds(part * dim, dim)].reshape(hidden, dim).T
     start(w_own[0::2])
+    out_load = pltpu.make_async_copy(w_out, uc_own.at[3, 0], load_sem.at[7])
+    out_load.start()
     loads[2].wait()
     loads[3].wait()
 
@@ -182,9 +183,9 @@
     start(uc_core)
     for part in range(3):
         qkv_loads[part].wait()
-        att_own[pl.ds(part * dim, dim), :] = uc_own[:, 1, :, pl.ds(part * dim, dim)].reshape(hidden, dim).T
-    loads[4].wait()
-    att_keep.start()
+        uc_own[part, 0] = uc_own[:, 1, :, pl.ds(part * dim, dim)].reshape(hidden, dim).T
+    out_load.wait()
+    start(att_keep)
 
     def y_loads(step, buf):
         seq = ring.at_traced(7 - step)
@@ -198,7 +199,7 @@
         slot = jnp.where(step == 3, 4, jnp.where(step == 4, 3, step))
         place = pl.ds(pl.multiple_of(jnp.where(step == 6, 1, jnp.where(step == 7, 3, slot)) * half, half), half)
 
-        @pl.when((step >= 1) & (step != 6))
+        @pl.when((step == 1) | ((step >= 3) & (step != 6)))
         def _():
             for which, buf in enumerate((up_all, down_all)):
                 ring.copy(buf.at[place], buf.at[place], w_send.at[0], w_recv.at[slot, which], PARTNER).wait_recv()
@@ -211,8 +212,12 @@
         @pl.when(step == 2)
         def _():
             pl.semaphore_wait(free_slot.at[0], 1)
-            start(w_near_t)
-            start(w_near_t_core)
+            for which, buf in ((1, down_all), (0, up_all)):
+                ring.copy(buf.at[room(2)], buf.at[room(2)], w_send.at[0], w_recv.at[2, which], PARTNER).wait_recv()
+                w_near_t[which].start()
+                w_near_t_core[which].start()
+            for copy in att_keep:
+                copy.wait()
             start(att_out)
 
         @pl.when(step == 3)
@@ -390,13 +395,24 @@
     du_pass = ring.copy(du_relay, du_pos.at[ring.at(SAME_F)], du_send.at[9], du_recv.at[OTHER_O], OTHER_T)
 
     att_f_core.wait_recv()
-    att_keep.wait()
     att_out[1].wait_recv()
     start(head_loads(2, 0))
+    start(head_loads(0, 1))
+
+    def arrive(slots):
+        for slot in slots:
+            if slot:
+                ring.copy(uc_own.at[slot], uc_seq.at[slot], a2a_send.at[0], a2a_recv.at[slot], PARTNER).wait_recv()
+            start(seq_own[2 * slot : 2 * slot + 2])
+
+    def project(first, count):
+        rows = pl.ds(first, count)
+        for buf in (0, 1):
+            c_all[2 + buf, rows, pl.ds(0, 6 * dim)] = dot_nt(u_all[0, rows, :], up_all[qkv_rows(buf), :]).astype(BF16)
+            c_all[2 + buf, rows, pl.ds(6 * dim, 2 * dim)] = dot_nt(u_all[1, rows, :], up_all[wo_rows(buf), :]).astype(BF16)
+
     uc_keep.wait()
-    for slot in range(1, 8):
-        ring.copy(uc_own.at[slot], uc_seq.at[slot], a2a_send.at[0], a2a_recv.at[slot], PARTNER).wait_recv()
-    start(seq_own)
+    arrive((0, 1, 4, 5, 2, 3))
     pl.semaphore_wait(free_slot.at[2], 1)
     start(uc_to_t)
     two_out.wait_recv()
@@ -404,8 +420,13 @@
     start(seq_two)
     out_own.wait()
     acc[1] = jnp.zeros(acc.shape[1:], F32)
-    for copy in seq_own:
+    for copy in seq_own[:12] + head_loads(2, 0) + head_loads(0, 1):
         copy.wait()
+    project(0, 6 * slab)
+    arrive((6, 7))
+    for copy in seq_own[12:]:
+        copy.wait()
+    project(6 * slab, 2 * slab)
 
     def chip_step(step, carry):
         buf = step % 2
@@ -422,10 +443,12 @@
             for copy in uc_to_t[:4]:
                 copy.wait_recv()
 
-        for copy in head_loads(0, buf):
-            copy.wait()
-
-        @pl.when((step == 0) | (step == 3) | (step == 4))
+        @pl.when(step >= 2)
+        def _():
+            for copy in head_loads(0, buf):
+                copy.wait()
+
+        @pl.when((step == 3) | (step == 4))
         def _():
             start(head_loads(relation_of(step + 1), 1 - buf))
 
@@ -436,11 +459,15 @@
             for index, head in enumerate(heads)
         ]
         start(wo_copies)
-        c_all[2, :, pl.ds(0, 6 * dim)] = dot_nt(u_all[2 * seq], up_all[qkv_rows(buf), :]).astype(BF16)
+
+        @pl.when(step >= 2)
+        def _():
+            c_all[2 + buf, :, pl.ds(0, 6 * dim)] = dot_nt(u_all[2 * seq], up_all[qkv_rows(buf), :]).astype(BF16)
+
         for index, head in enumerate(heads):
             columns = pl.ds(pl.multiple_of(head * dim, dim), dim)
             own = pl.ds(index * 3 * dim, 3 * dim)
-            query, key, value = (c_all[2, :, pl.ds((index * 3 + part) * dim, dim)] for part in range(3))
+            query, key, value = (c_all[2 + buf, :, pl.ds((index * 3 + part) * dim, dim)] for part in range(3))
             scores = dot_nt(query, key) * (scale * LOG2_E)
             grown = jnp.exp2(scores - jnp.max(scores, axis=-1, keepdims=True))
             prob = grown * (1.0 / jnp.sum(grown, axis=-1, keepdims=True))
@@ -452,8 +479,11 @@
                     for copy in uc_to_t[4:]:
                         copy.wait_recv()
 
-                c_all[2, :, pl.ds(6 * dim, 2 * dim)] = dot_nt(u_all[2 * seq + 1], up_all[wo_rows(buf), :]).astype(BF16)
-            d_out = c_all[2, :, pl.ds((6 + index) * dim, dim)]
+                @pl.when(step >= 2)
+                def _():
+                    c_all[2 + buf, :, pl.ds(6 * dim, 2 * dim)] = dot_nt(u_all[2 * seq + 1], up_all[wo_rows(buf), :]).astype(BF16)
+
+            d_out = c_all[2 + buf, :, pl.ds((6 + index) * dim, dim)]
             d_prob = dot_nt(d_out, value)
             d_score = (prob * (d_prob - jnp.sum(d_prob * prob, axis=-1, keepdims=True)) * scale).astype(BF16)
             down_all[kept, pl.ds(index * 3 * dim, dim)] = dot_nn(d_score, key).astype(BF16)
@@ -583,7 +613,7 @@
     scratch = [
         vmem((4, tokens, hidden), BF16), vmem((4, tokens, hidden), BF16), vmem((6 * ffn, hidden), BF16), vmem((6 * ffn, hidden), BF16),
         vmem((2, slabs, slab, hidden), F32), vmem((2, 5, slab, hidden), F32), vmem((2, 4, dim, hidden), F32),
-        vmem((8, 2, slab, hidden), BF16), vmem((4 * dim, hidden), BF16),
+        vmem((8, 2, slab, hidden), BF16),
         dma((8,)), dma((2, 3)), dma((2, 2)), dma((16,)), dma((8, 2)), dma((6,)), dma((4, 2)), dma((7,)), dma((8,)), dma((11,)), dma((8,)), dma((3,)), dma((2,)), dma((2,)),
         dma((4, 8)), dma((2, 2, 2)), dma((2,)), dma((2,)), dma((2,)), dma((2,)), dma((2, 8)), dma((10,)), dma((8,)), dma((10,)), dma((8,)), dma((2,)), dma((2,)), dma((2,)),
         pltpu.SemaphoreType.REGULAR((6,)),

time: 378 us -> 379 us (level)
  no operation moved by 1% of the time
where the time goes in v15:
time: 379 us
  Pallas kernels  375 us (99%)
    pallas_call x1, Pallas kernels, block_call(): pl.pallas_call(functools.partial(block_kernel, dim ** (-0.5)), out_shape=...  353 us
    pallas_call x1, Pallas kernels, finish_call(): pl.pallas_call(finish_kernel, out_shape=out_shape, in_specs=[any_spec] *...  19.8 us
  transfers between devices with their start and end apart: 1, of which 1 were waited for; matrix products, arithmetic and copies ran while one was open for 0% of the time, Pallas kernels for 5%

profile of v15, /device:TPU:112, one launch (start us, length us, event | category | flops | bytes accessed | tf_op | source)
XLA Modules:
  0.0 378.8 jit_solution(8615717679968775929)
XLA Ops:
  0.6 352.9 %block.1 = (f32[8,128,1024]{2,1,0:T(8,128)}, f32[8,128,1024]{2,1,0:T(8,128)}, f32[8,128,1024]{2,1,0:T(8,128)}, f32[8,128,1024]{2,1,0:T(8,128)}, f32[4,128,1024]{...) custom-call(f32[8,128,1024]{2,1,0:T(8,128)} %y_one.1, ...), custom_call_target="tpu_custom_call" | custom-call | flops 120000004096 | bytes 134217728 | tf_op jit(solution)/shard_map/block/pallas_call | solution.py:621
  353.6 1.4 collective-permute-start
  355.0 19.8 %finish.1 = (f32[1024,1024]{1,0:T(8,128)}, f32[1024,1024]{1,0:T(8,128)}, f32[1024,1024]{1,0:T(8,128)}, f32[1024,1024]{1,0:T(8,128)}, f32[1024,512]{1,0:T(8,128)}...) custom-call(f32[1024,1024]{1,0:T(8,128)} %bitcast.32, bf16[1024,1024]{1,0:T(8,128)(2,1)} %bitcast.39, ...), custom_call_target="tpu_custom_call" | custom-call | flops 2000000000 | bytes 54525952 | tf_op jit(solution)/shard_map/finish/pallas_call | solution.py:719
  374.8 1.2 collective-permute-done.du_far
  375.9 2.7 last.1
Async XLA Ops:
  353.6 22.4 %collective-permute-start = (f32[224,1024]{1,0:T(8,128)}, f32[224,1024]{1,0:T(8,128)}, u32[]{:S(2)}, u32[]{:S(2)}) collective-permute-start(f32[224,1024]{1,0:T(8,128)} %get-tuple-element.36), channel_id=1, source_target_pairs={{0,6},{1,7},{2,4},{3,5},{4,2},{5,3},{6,0},{7,1},{8,14},{9,15},{10,... | collective-permute-start | bytes 2752520 | tf_op jit(solution)/shard_map/ppermute | solution.py:778

commit v16 on v15

--- a/solution.py
+++ b/solution.py
@@ -10,7 +10,7 @@
 RMS_EPS = 1e-6
 LOG2_E = 1.4426950408889634
 LATE_ROWS = 96
-FAR_ROWS = 32
+FAR_ROWS = 16
 MESH = pl.DeviceIdType.MESH
 BF16, F32 = jnp.bfloat16, jnp.float32
 VMEM_LIMIT = 64 * 1024 * 1024 - 65536
@@ -67,11 +67,12 @@
         chip = jnp.where(relation == 0, own, jnp.where(relation == 1, near_t, jnp.where(relation == 2, near_f, opposite)))
         return chip * 2 + (self.core + other) % 2
 
-    def barrier(self):
-        barrier = pltpu.get_barrier_semaphore()
+    def arrive(self):
         for slot in (1, 2, 3, 4, 5):
-            pl.semaphore_signal(barrier, inc=1, device_id={"tp": self.at(slot)}, device_id_type=MESH)
-        pl.semaphore_wait(barrier, 5)
+            pl.semaphore_signal(pltpu.get_barrier_semaphore(), inc=1, device_id={"tp": self.at(slot)}, device_id_type=MESH)
+
+    def meet(self):
+        pl.semaphore_wait(pltpu.get_barrier_semaphore(), 5)
 
     def copy(self, src, dst, send_sem, recv_sem, slot):
         return pltpu.make_async_remote_copy(src_ref=src, dst_ref=dst, send_sem=send_sem, recv_sem=recv_sem, device_id={"tp": self.at(slot)}, device_id_type=MESH)
@@ -156,9 +157,10 @@
         pltpu.make_async_copy(dy_two, acc.at[1], load_sem.at[3]),
     ]
     qkv_loads = [pltpu.make_async_copy(w_qkv.at[part], uc_own.at[:, 1, :, pl.ds(part * dim, dim)], y_sem.at[0, part]) for part in range(3)]
+    ring.arrive()
     start(loads)
     start(qkv_loads)
-    ring.barrier()
+    ring.meet()
     loads[0].wait()
     start(w_own[1::2])
     loads[1].wait()

time: 379 us -> 378 us (level)
  no operation moved by 1% of the time
where the time goes in v16:
time: 378 us; the launch traced here: 377 us
  Pallas kernels  374 us (99%)
    pallas_call x1, Pallas kernels, block_call(): pl.pallas_call(functools.partial(block_kernel, dim ** (-0.5)), out_shape=...  352 us
    pallas_call x1, Pallas kernels, finish_call(): pl.pallas_call(finish_kernel, out_shape=out_shape, in_specs=[any_spec] *...  19.8 us
  transfers between devices with their start and end apart: 1, of which 1 were waited for; matrix products, arithmetic and copies ran while one was open for 0% of the time, Pallas kernels for 5%

profile of v16, /device:TPU:112, one launch (start us, length us, event | category | flops | bytes accessed | tf_op | source)
XLA Modules:
  0.0 377.4 jit_solution(3099164126388561861)
XLA Ops:
  0.6 351.5 %block.1 = (f32[8,128,1024]{2,1,0:T(8,128)}, f32[8,128,1024]{2,1,0:T(8,128)}, f32[8,128,1024]{2,1,0:T(8,128)}, f32[8,128,1024]{2,1,0:T(8,128)}, f32[4,128,1024]{...) custom-call(f32[8,128,1024]{2,1,0:T(8,128)} %y_one.1, ...), custom_call_target="tpu_custom_call" | custom-call | flops 120000004096 | bytes 134217728 | tf_op jit(solution)/shard_map/block/pallas_call | solution.py:623
  352.1 1.4 collective-permute-start
  353.6 19.8 %finish.1 = (f32[1024,1024]{1,0:T(8,128)}, f32[1024,1024]{1,0:T(8,128)}, f32[1024,1024]{1,0:T(8,128)}, f32[1024,1024]{1,0:T(8,128)}, f32[1024,512]{1,0:T(8,128)}...) custom-call(f32[1024,1024]{1,0:T(8,128)} %bitcast.32, bf16[1024,1024]{1,0:T(8,128)(2,1)} %bitcast.39, ...), custom_call_target="tpu_custom_call" | custom-call | flops 2000000000 | bytes 54525952 | tf_op jit(solution)/shard_map/finish/pallas_call | solution.py:721
  373.3 1.2 collective-permute-done.du_far
  374.5 2.7 last.1
Async XLA Ops:
  352.1 22.4 %collective-permute-start = (f32[224,1024]{1,0:T(8,128)}, f32[224,1024]{1,0:T(8,128)}, u32[]{:S(2)}, u32[]{:S(2)}) collective-permute-start(f32[224,1024]{1,0:T(8,128)} %get-tuple-element.36), channel_id=1, source_target_pairs={{0,6},{1,7},{2,4},{3,5},{4,2},{5,3},{6,0},{7,1},{8,14},{9,15},{10,... | collective-permute-start | bytes 2752520 | tf_op jit(solution)/shard_map/ppermute | solution.py:780

commit v17 on v16

--- a/solution.py
+++ b/solution.py
@@ -368,7 +368,7 @@
     seq_own = [copy for slot in range(8) for copy in seq_loads(0, uc_seq, slot, slot)]
     seq_two = [copy for slot in range(4) for copy in seq_loads(1, uc_two, slot, slot)]
     uc_to_t = [
-        ring.copy(uc_seq.at[slot, which], u_all.at[2 + which, rows_of(4 + index)], far_sem.at[0, 2 * index + which], far_sem.at[1, 2 * index + which], SAME_T)
+        ring.copy(u_all.at[which, rows_of(slot)], u_all.at[2 + which, rows_of(4 + index)], far_sem.at[0, 2 * index + which], far_sem.at[1, 2 * index + which], SAME_T)
         for which in (0, 1)
         for index, slot in enumerate((0, 1, 4, 5))
     ]
@@ -415,8 +415,6 @@
 
     uc_keep.wait()
     arrive((0, 1, 4, 5, 2, 3))
-    pl.semaphore_wait(free_slot.at[2], 1)
-    start(uc_to_t)
     two_out.wait_recv()
     two_keep.wait()
     start(seq_two)
@@ -424,6 +422,8 @@
     acc[1] = jnp.zeros(acc.shape[1:], F32)
     for copy in seq_own[:12] + head_loads(2, 0) + head_loads(0, 1):
         copy.wait()
+    pl.semaphore_wait(free_slot.at[2], 1)
+    start(uc_to_t)
     project(0, 6 * slab)
     arrive((6, 7))
     for copy in seq_own[12:]:

time: 378 us -> 378 us (level)
  no operation moved by 1% of the time
where the time goes in v17:
time: 378 us; the launch traced here: 377 us
  Pallas kernels  374 us (99%)
    pallas_call x1, Pallas kernels, block_call(): pl.pallas_call(functools.partial(block_kernel, dim ** (-0.5)), out_shape=...  352 us
    pallas_call x1, Pallas kernels, finish_call(): pl.pallas_call(finish_kernel, out_shape=out_shape, in_specs=[any_spec] *...  19.8 us
  transfers between devices with their start and end apart: 1, of which 1 were waited for; matrix products, arithmetic and copies ran while one was open for 0% of the time, Pallas kernels for 5%

profile of v17, /device:TPU:112, one launch (start us, length us, event | category | flops | bytes accessed | tf_op | source)
XLA Modules:
  0.0 377.4 jit_solution(7932671231002491257)
XLA Ops:
  0.6 351.5 %block.1 = (f32[8,128,1024]{2,1,0:T(8,128)}, f32[8,128,1024]{2,1,0:T(8,128)}, f32[8,128,1024]{2,1,0:T(8,128)}, f32[8,128,1024]{2,1,0:T(8,128)}, f32[4,128,1024]{...) custom-call(f32[8,128,1024]{2,1,0:T(8,128)} %y_one.1, ...), custom_call_target="tpu_custom_call" | custom-call | flops 120000004096 | bytes 134217728 | tf_op jit(solution)/shard_map/block/pallas_call | solution.py:623
  352.1 1.4 collective-permute-start
  353.6 19.8 %finish.1 = (f32[1024,1024]{1,0:T(8,128)}, f32[1024,1024]{1,0:T(8,128)}, f32[1024,1024]{1,0:T(8,128)}, f32[1024,1024]{1,0:T(8,128)}, f32[1024,512]{1,0:T(8,128)}...) custom-call(f32[1024,1024]{1,0:T(8,128)} %bitcast.32, bf16[1024,1024]{1,0:T(8,128)(2,1)} %bitcast.39, ...), custom_call_target="tpu_custom_call" | custom-call | flops 2000000000 | bytes 54525952 | tf_op jit(solution)/shard_map/finish/pallas_call | solution.py:721
  373.3 1.2 collective-permute-done.du_far
  374.5 2.7 last.1
Async XLA Ops:
  352.1 22.4 %collective-permute-start = (f32[224,1024]{1,0:T(8,128)}, f32[224,1024]{1,0:T(8,128)}, u32[]{:S(2)}, u32[]{:S(2)}) collective-permute-start(f32[224,1024]{1,0:T(8,128)} %get-tuple-element.36), channel_id=1, source_target_pairs={{0,6},{1,7},{2,4},{3,5},{4,2},{5,3},{6,0},{7,1},{8,14},{9,15},{10,... | collective-permute-start | bytes 2752520 | tf_op jit(solution)/shard_map/ppermute | solution.py:780

commit v18 on v17

--- a/solution.py
+++ b/solution.py
@@ -305,14 +305,20 @@
         tokens = (step % 8) // 2
         place = pl.ds(pl.multiple_of((4 - 4 * first) * half, half), half)
 
-        @pl.when((step == 2) | (step == 4) | (step == 6))
+        @pl.when(step == 0)
+        def _():
+            u_to_t.wait_recv()
+            uc_pass[0].start()
+
+        @pl.when((step == 2) | (step == 6))
         def _():
             for which, buf in enumerate((u_all, c_all)):
                 ring.copy(buf.at[tokens], buf.at[tokens], uc_send.at[0], uc_recv.at[tokens, which], PARTNER).wait_recv()
 
         @pl.when(step == 4)
         def _():
-            start(uc_pass)
+            c_to_t.wait_recv()
+            uc_pass[1].start()
             for index in (0, 1):
                 a2a_out[SAME_O + index].wait_recv()
             start(a2a_pass)

time: 378 us -> 378 us (level)
  no operation moved by 1% of the time
where the time goes in v18:
time: 378 us; the launch traced here: 377 us
  Pallas kernels  374 us (99%)
    pallas_call x1, Pallas kernels, block_call(): pl.pallas_call(functools.partial(block_kernel, dim ** (-0.5)), out_shape=...  352 us
    pallas_call x1, Pallas kernels, finish_call(): pl.pallas_call(finish_kernel, out_shape=out_shape, in_specs=[any_spec] *...  19.8 us
  transfers between devices with their start and end apart: 1, of which 1 were waited for; matrix products, arithmetic and copies ran while one was open for 0% of the time, Pallas kernels for 5%

profile of v18, /device:TPU:112, one launch (start us, length us, event | category | flops | bytes accessed | tf_op | source)
XLA Modules:
  0.0 377.4 jit_solution(10191016115012502048)
XLA Ops:
  0.6 351.5 %block.1 = (f32[8,128,1024]{2,1,0:T(8,128)}, f32[8,128,1024]{2,1,0:T(8,128)}, f32[8,128,1024]{2,1,0:T(8,128)}, f32[8,128,1024]{2,1,0:T(8,128)}, f32[4,128,1024]{...) custom-call(f32[8,128,1024]{2,1,0:T(8,128)} %y_one.1, ...), custom_call_target="tpu_custom_call" | custom-call | flops 120000004096 | bytes 134217728 | tf_op jit(solution)/shard_map/block/pallas_call | solution.py:629
  352.1 1.4 collective-permute-start
  353.6 19.8 %finish.1 = (f32[1024,1024]{1,0:T(8,128)}, f32[1024,1024]{1,0:T(8,128)}, f32[1024,1024]{1,0:T(8,128)}, f32[1024,1024]{1,0:T(8,128)}, f32[1024,512]{1,0:T(8,128)}...) custom-call(f32[1024,1024]{1,0:T(8,128)} %bitcast.32, bf16[1024,1024]{1,0:T(8,128)(2,1)} %bitcast.39, ...), custom_call_target="tpu_custom_call" | custom-call | flops 2000000000 | bytes 54525952 | tf_op jit(solution)/shard_map/finish/pallas_call | solution.py:727
  373.3 1.2 collective-permute-done.du_far
  374.5 2.7 last.1
Async XLA Ops:
  352.1 22.4 %collective-permute-start = (f32[224,1024]{1,0:T(8,128)}, f32[224,1024]{1,0:T(8,128)}, u32[]{:S(2)}, u32[]{:S(2)}) collective-permute-start(f32[224,1024]{1,0:T(8,128)} %get-tuple-element.36), channel_id=1, source_target_pairs={{0,6},{1,7},{2,4},{3,5},{4,2},{5,3},{6,0},{7,1},{8,14},{9,15},{10,... | collective-permute-start | bytes 2752520 | tf_op jit(solution)/shard_map/ppermute | solution.py:786

commit v19 on v18

--- a/solution.py
+++ b/solution.py
@@ -9,7 +9,7 @@
 
 RMS_EPS = 1e-6
 LOG2_E = 1.4426950408889634
-LATE_ROWS = 96
+LATE_ROWS = 80
 FAR_ROWS = 16
 MESH = pl.DeviceIdType.MESH
 BF16, F32 = jnp.bfloat16, jnp.float32

time: 378 us -> 378 us (level)
  transfers between devices with their start and end apart: 1 -> 1, of which waited for: 1 -> 0; matrix products, arithmetic and copies ran while one was open for 0% -> 0% of each run, Pallas kernels for 5% -> 5%
where the time goes in v19:
time: 378 us
  Pallas kernels  375 us (99%)
    pallas_call x1, Pallas kernels, block_call(): pl.pallas_call(functools.partial(block_kernel, dim ** (-0.5)), out_shape=...  353 us
    pallas_call x1, Pallas kernels, finish_call(): pl.pallas_call(finish_kernel, out_shape=out_shape, in_specs=[any_spec] *...  19.8 us
  transfers between devices with their start and end apart: 1, of which 0 were waited for; matrix products, arithmetic and copies ran while one was open for 0% of the time, Pallas kernels for 5%

profile of v19, /device:TPU:112, one launch (start us, length us, event | category | flops | bytes accessed | tf_op | source)
XLA Modules:
  0.0 377.6 jit_solution(13998048748201871656)
XLA Ops:
  0.6 352.9 %block.1 = (f32[8,128,1024]{2,1,0:T(8,128)}, f32[8,128,1024]{2,1,0:T(8,128)}, f32[8,128,1024]{2,1,0:T(8,128)}, f32[8,128,1024]{2,1,0:T(8,128)}, f32[4,128,1024]{...) custom-call(f32[8,128,1024]{2,1,0:T(8,128)} %y_one.1, ...), custom_call_target="tpu_custom_call" | custom-call | flops 120000004096 | bytes 134217728 | tf_op jit(solution)/shard_map/block/pallas_call | solution.py:629
  353.6 1.4 collective-permute-start
  355.0 19.8 %finish.1 = (f32[1024,1024]{1,0:T(8,128)}, f32[1024,1024]{1,0:T(8,128)}, f32[1024,1024]{1,0:T(8,128)}, f32[1024,1024]{1,0:T(8,128)}, f32[1024,512]{1,0:T(8,128)}...) custom-call(f32[1024,1024]{1,0:T(8,128)} %bitcast.32, bf16[1024,1024]{1,0:T(8,128)(2,1)} %bitcast.39, ...), custom_call_target="tpu_custom_call" | custom-call | flops 2000000000 | bytes 54525952 | tf_op jit(solution)/shard_map/finish/pallas_call | solution.py:727
  374.8 0.0 collective-permute-done.du_far
  374.8 2.6 last.1
Async XLA Ops:
  353.6 21.3 %collective-permute-start = (f32[208,1024]{1,0:T(8,128)}, f32[208,1024]{1,0:T(8,128)}, u32[]{:S(2)}, u32[]{:S(2)}) collective-permute-start(f32[208,1024]{1,0:T(8,128)} %get-tuple-element.36), channel_id=1, source_target_pairs={{0,6},{1,7},{2,4},{3,5},{4,2},{5,3},{6,0},{7,1},{8,14},{9,15},{10,... | collective-permute-start | bytes 2555912 | tf_op jit(solution)/shard_map/ppermute | solution.py:786

commit v20 on v18

--- a/solution.py
+++ b/solution.py
@@ -10,7 +10,6 @@
 RMS_EPS = 1e-6
 LOG2_E = 1.4426950408889634
 LATE_ROWS = 96
-FAR_ROWS = 16
 MESH = pl.DeviceIdType.MESH
 BF16, F32 = jnp.bfloat16, jnp.float32
 VMEM_LIMIT = 64 * 1024 * 1024 - 65536
@@ -88,7 +87,7 @@
     uc_seq, uc_two, att_full, o_relay, du_relay,
     u_all, c_all, up_all, down_all, acc, spare, part_keep, uc_own,
     load_sem, y_sem, x_sem, w_send, w_recv, uc_send, uc_recv, att_send, att_recv, a2a_send, a2a_recv, relay_recv, near_sem, two_sem,
-    seq_sem, head_sem, wo_sem, core_send, core_recv, f_sem, far_sem, o_send, o_recv, du_send, du_recv, o_relay_recv, du_relay_recv, far_recv, free_slot,
+    seq_sem, head_sem, wo_sem, core_send, core_recv, f_sem, far_sem, o_send, o_recv, du_send, du_recv, o_relay_recv, du_relay_recv, free_slot,
 ):
     ring = Ring()
     slabs, slab, hidden = acc.shape[1:]
@@ -116,12 +115,7 @@
         ]
 
     w_own = weight_pair(0, 1, PARTNER, 0) + weight_pair(0, 2, SAME_T, 2) + weight_pair(0, 4, SAME_F, 4)
-    def far_part(src_slot, first, count, to, index, recv_sem):
-        src, dst = (pl.ds(rooms[slot] * half + first, count) for slot in (src_slot, 6))
-        return [ring.copy(buf.at[src], buf.at[dst], w_send.at[index + which], recv_sem.at[which], to) for which, buf in enumerate((up_all, down_all))]
-
-    w_near_t = far_part(2, FAR_ROWS, half - FAR_ROWS, SAME_F, 6, w_recv.at[6])
-    w_over_t = far_part(4, 0, FAR_ROWS, SAME_T, 14, far_recv)
+    w_near_t = weight_pair(2, 6, SAME_F, 6)
     w_near_t_core = weight_pair(2, 3, PARTNER, 8)
     w_near_f = weight_pair(4, 5, PARTNER, 10)
     w_far = weight_pair(6, 7, PARTNER, 12)
@@ -208,7 +202,7 @@
 
         @pl.when(step == 6)
         def _():
-            for copy in w_near_t + w_over_t:
+            for copy in w_near_t:
                 copy.wait_recv()
 
         @pl.when(step == 2)
@@ -224,8 +218,6 @@
 
         @pl.when(step == 3)
         def _():
-            pl.semaphore_wait(free_slot.at[5], 1)
-            start(w_over_t)
             c_to_t.start()
             start(w_near_f)
 
@@ -252,7 +244,6 @@
         @pl.when(step == 1)
         def _():
             say_free(0, SAME_F)
-            say_free(5, SAME_T)
 
         @pl.when(step == 4)
         def _():
@@ -342,7 +333,7 @@
     lax.fori_loop(0, 16, gradients, 0)
     out_own = pltpu.make_async_copy(acc.at[1], part_own, load_sem.at[1])
     out_own.start()
-    for copy in w_own + w_near_t + w_over_t + w_near_t_core + w_near_f + w_far + [u_to_t, c_to_t] + uc_core + uc_pass:
+    for copy in w_own + w_near_t + w_near_t_core + w_near_f + w_far + [u_to_t, c_to_t] + uc_core + uc_pass:
         copy.wait_send()
     say_free(2, SAME_T)
 
@@ -622,9 +613,9 @@
         vmem((4, tokens, hidden), BF16), vmem((4, tokens, hidden), BF16), vmem((6 * ffn, hidden), BF16), vmem((6 * ffn, hidden), BF16),
         vmem((2, slabs, slab, hidden), F32), vmem((2, 5, slab, hidden), F32), vmem((2, 4, dim, hidden), F32),
         vmem((8, 2, slab, hidden), BF16),
-        dma((8,)), dma((2, 3)), dma((2, 2)), dma((16,)), dma((8, 2)), dma((6,)), dma((4, 2)), dma((7,)), dma((8,)), dma((11,)), dma((8,)), dma((3,)), dma((2,)), dma((2,)),
-        dma((4, 8)), dma((2, 2, 2)), dma((2,)), dma((2,)), dma((2,)), dma((2,)), dma((2, 8)), dma((10,)), dma((8,)), dma((10,)), dma((8,)), dma((2,)), dma((2,)), dma((2,)),
-        pltpu.SemaphoreType.REGULAR((6,)),
+        dma((8,)), dma((2, 3)), dma((2, 2)), dma((14,)), dma((8, 2)), dma((6,)), dma((4, 2)), dma((7,)), dma((8,)), dma((11,)), dma((8,)), dma((3,)), dma((2,)), dma((2,)),
+        dma((4, 8)), dma((2, 2, 2)), dma((2,)), dma((2,)), dma((2,)), dma((2,)), dma((2, 8)), dma((10,)), dma((8,)), dma((10,)), dma((8,)), dma((2,)), dma((2,)),
+        pltpu.SemaphoreType.REGULAR((5,)),
     ]
     return pl.pallas_call(
         functools.partial(block_kernel, dim ** -0.5),

time: 378 us -> 378 us (level)
  no operation moved by 1% of the time
where the time goes in v20:
time: 378 us; the launch traced here: 377 us
  Pallas kernels  374 us (99%)
    pallas_call x1, Pallas kernels, block_call(): pl.pallas_call(functools.partial(block_kernel, dim ** (-0.5)), out_shape=...  351 us
    pallas_call x1, Pallas kernels, finish_call(): pl.pallas_call(finish_kernel, out_shape=out_shape, in_specs=[any_spec] *...  19.8 us
  transfers between devices with their start and end apart: 1, of which 1 were waited for; matrix products, arithmetic and copies ran while one was open for 0% of the time, Pallas kernels for 5%

profile of v20, /device:TPU:112, one launch (start us, length us, event | category | flops | bytes accessed | tf_op | source)
XLA Modules:
  0.0 377.2 jit_solution(717728819461092050)
XLA Ops:
  0.6 351.3 %block.1 = (f32[8,128,1024]{2,1,0:T(8,128)}, f32[8,128,1024]{2,1,0:T(8,128)}, f32[8,128,1024]{2,1,0:T(8,128)}, f32[8,128,1024]{2,1,0:T(8,128)}, f32[4,128,1024]{...) custom-call(f32[8,128,1024]{2,1,0:T(8,128)} %y_one.1, ...), custom_call_target="tpu_custom_call" | custom-call | flops 120000004096 | bytes 134217728 | tf_op jit(solution)/shard_map/block/pallas_call | solution.py:620
  351.9 1.3 collective-permute-start
  353.3 19.8 %finish.1 = (f32[1024,1024]{1,0:T(8,128)}, f32[1024,1024]{1,0:T(8,128)}, f32[1024,1024]{1,0:T(8,128)}, f32[1024,1024]{1,0:T(8,128)}, f32[1024,512]{1,0:T(8,128)}...) custom-call(f32[1024,1024]{1,0:T(8,128)} %bitcast.32, bf16[1024,1024]{1,0:T(8,128)(2,1)} %bitcast.39, ...), custom_call_target="tpu_custom_call" | custom-call | flops 2000000000 | bytes 54525952 | tf_op jit(solution)/shard_map/finish/pallas_call | solution.py:718
  373.1 1.2 collective-permute-done.du_far
  374.3 2.7 last.1
Async XLA Ops:
  351.9 22.4 %collective-permute-start = (f32[224,1024]{1,0:T(8,128)}, f32[224,1024]{1,0:T(8,128)}, u32[]{:S(2)}, u32[]{:S(2)}) collective-permute-start(f32[224,1024]{1,0:T(8,128)} %get-tuple-element.36), channel_id=1, source_target_pairs={{0,6},{1,7},{2,4},{3,5},{4,2},{5,3},{6,0},{7,1},{8,14},{9,15},{10,... | collective-permute-start | bytes 2752520 | tf_op jit(solution)/shard_map/ppermute | solution.py:777

commit v21 on v20

--- a/solution.py
+++ b/solution.py
@@ -519,6 +519,7 @@
         def _():
             att_o.wait_recv()
             att_o_core.start()
+            start(head_loads(3, 1)[2:])
 
         @pl.when(step < 4)
         def _():
@@ -532,7 +533,7 @@
         @pl.when(step == 2)
         def _():
             att_o_core.wait_recv()
-            start(head_loads(3, 1))
+            start(head_loads(3, 1)[:2])
 
         @pl.when(step == 3)
         def _():

time: 378 us -> 378 us (level)
  no operation moved by 1% of the time
where the time goes in v21:
time: 378 us; the launch traced here: 377 us
  Pallas kernels  374 us (99%)
    pallas_call x1, Pallas kernels, block_call(): pl.pallas_call(functools.partial(block_kernel, dim ** (-0.5)), out_shape=...  351 us
    pallas_call x1, Pallas kernels, finish_call(): pl.pallas_call(finish_kernel, out_shape=out_shape, in_specs=[any_spec] *...  19.8 us
  transfers between devices with their start and end apart: 1, of which 1 were waited for; matrix products, arithmetic and copies ran while one was open for 0% of the time, Pallas kernels for 5%

profile of v21, /device:TPU:112, one launch (start us, length us, event | category | flops | bytes accessed | tf_op | source)
XLA Modules:
  0.0 377.2 jit_solution(18405480880847211357)
XLA Ops:
  0.6 351.3 %block.1 = (f32[8,128,1024]{2,1,0:T(8,128)}, f32[8,128,1024]{2,1,0:T(8,128)}, f32[8,128,1024]{2,1,0:T(8,128)}, f32[8,128,1024]{2,1,0:T(8,128)}, f32[4,128,1024]{...) custom-call(f32[8,128,1024]{2,1,0:T(8,128)} %y_one.1, ...), custom_call_target="tpu_custom_call" | custom-call | flops 120000004096 | bytes 134217728 | tf_op jit(solution)/shard_map/block/pallas_call | solution.py:621
  351.9 1.3 collective-permute-start
  353.3 19.8 %finish.1 = (f32[1024,1024]{1,0:T(8,128)}, f32[1024,1024]{1,0:T(8,128)}, f32[1024,1024]{1,0:T(8,128)}, f32[1024,1024]{1,0:T(8,128)}, f32[1024,512]{1,0:T(8,128)}...) custom-call(f32[1024,1024]{1,0:T(8,128)} %bitcast.32, bf16[1024,1024]{1,0:T(8,128)(2,1)} %bitcast.39, ...), custom_call_target="tpu_custom_call" | custom-call | flops 2000000000 | bytes 54525952 | tf_op jit(solution)/shard_map/finish/pallas_call | solution.py:719
  373.1 1.2 collective-permute-done.du_far
  374.3 2.7 last.1
Async XLA Ops:
  351.9 22.4 %collective-permute-start = (f32[224,1024]{1,0:T(8,128)}, f32[224,1024]{1,0:T(8,128)}, u32[]{:S(2)}, u32[]{:S(2)}) collective-permute-start(f32[224,1024]{1,0:T(8,128)} %get-tuple-element.36), channel_id=1, source_target_pairs={{0,6},{1,7},{2,4},{3,5},{4,2},{5,3},{6,0},{7,1},{8,14},{9,15},{10,... | collective-permute-start | bytes 2752520 | tf_op jit(solution)/shard_map/ppermute | solution.py:778
